TPU v7x, 32 devices: a whole 2x2x4 slice. The times are simulated.
32 devices in a mesh: fsdp: 16 (over z, x, core), tp: 2 (over y).
Axes of the slice: x: 2, y: 2, z: 4, core: 2. Of those that a mesh axis runs over, the one named last changes fastest.
Arguments:
- inputs: bfloat16 [32768, 1024], P(('fsdp', 'tp')), may hold values from -6 to 6
- cotangent: bfloat16 [32768, 1024], P(('fsdp', 'tp')), may hold values from -18 to 18
- first_gain: float32 [1024], replicated, may hold values from 0.5 to 1.5
- first_shift: float32 [1024], replicated, may hold values from -1.5 to 1.5
- second_gain: float32 [1024], replicated, may hold values from 0.5 to 1.5
- second_shift: float32 [1024], replicated, may hold values from -1.5 to 1.5
- project_weight: bfloat16 [1024, 3, 1024], P('fsdp', None, 'tp'), may hold values from -0.1875 to 0.1875
- project_bias: float32 [3, 1024], P(None, 'tp'), may hold values from -1.5 to 1.5
- dense_weight: bfloat16 [1024, 1024], P('tp', 'fsdp'), may hold values from -4 to 4
- dense_bias: float32 [1024], replicated, may hold values from -1.5 to 1.5
- expand_weight: bfloat16 [1024, 4096], P('fsdp', 'tp'), may hold values from -0.1875 to 0.1875
- expand_bias: float32 [4096], P('tp'), may hold values from -2.5 to 2.5
- shrink_weight: bfloat16 [4096, 1024], P('tp', 'fsdp'), may hold values from -0.09375 to 0.09375
- shrink_bias: float32 [1024], replicated, may hold values from -1.5 to 1.5
Outputs:
- output: bfloat16 [32768, 1024], P(('fsdp', 'tp'))
- input_grad: float32 [32768, 1024], P(('fsdp', 'tp'))
- first_gain_grad: float32 [1024], replicated
- first_shift_grad: float32 [1024], replicated
- second_gain_grad: float32 [1024], replicated
- second_shift_grad: float32 [1024], replicated
- project_weight_grad: float32 [1024, 3, 1024], P('fsdp', None, 'tp')
- project_bias_grad: float32 [3, 1024], P(None, 'tp')
- dense_weight_grad: float32 [1024, 1024], P('tp', 'fsdp')
- dense_bias_grad: float32 [1024], replicated
- expand_weight_grad: float32 [1024, 4096], P('fsdp', 'tp')
- expand_bias_grad: float32 [4096], P('tp')
- shrink_weight_grad: float32 [4096, 1024], P('tp', 'fsdp')
- shrink_bias_grad: float32 [1024], replicated
All inputs are finite; a program needn't handle non-finite values.
Results may differ from a plain program's by a relative error of at most 0.0094.
Values may be sent and summed in bfloat16 or wider, within the bound.
A program may use at most 320 MiB of HBM per device.

v0:
```python
import jax
import jax.numpy as jnp
from jax import lax
from jax.sharding import PartitionSpec as P

HS = 64
ROT = 16
LEN = 2048


EPS = 1e-05


def normalize(values, gain_vector, shift_vector):
    mean_row = jnp.mean(values, axis=-1, keepdims=True)
    centred = values - mean_row
    spread = lax.rsqrt(jnp.mean(centred * centred, axis=-1, keepdims=True) + EPS)
    normal = centred * spread
    return (normal * gain_vector + shift_vector, normal, spread)


def norm_back(grad_in, normal, spread, gain_vector):
    scaled = grad_in * gain_vector
    mean_first = jnp.mean(scaled, axis=-1, keepdims=True)
    mean_second = jnp.mean(scaled * normal, axis=-1, keepdims=True)
    return spread * (scaled - mean_first - normal * mean_second)


def rotary_tables(row_count):
    half_rot = ROT // 2
    position = (jnp.arange(row_count) % LEN).astype(jnp.float32)
    inverse = 10000.0 ** (-(jnp.arange(half_rot).astype(jnp.float32) * 2.0) / ROT)
    angle = position[:, None] * inverse[None, :]
    return (jnp.cos(angle), jnp.sin(angle))


def rotate(heads_in, cosine_table, sine_table):
    half_rot = ROT // 2
    first_half = heads_in[..., :half_rot]
    second_half = heads_in[..., half_rot:ROT]
    cos_wide = cosine_table[:, None, :]
    sin_wide = sine_table[:, None, :]
    return jnp.concatenate(
        [
            first_half * cos_wide - second_half * sin_wide,
            second_half * cos_wide + first_half * sin_wide,
            heads_in[..., ROT:],
        ],
        axis=-1,
    )


def causal_scores(query_rows, key_rows, first_row, score_scale):
    block_rows = query_rows.shape[0]
    raw_scores = (
        jnp.einsum("qhd,khd->hqk", query_rows, key_rows, preferred_element_type=jnp.float32)
        * score_scale
    )
    row_pos = first_row + jnp.arange(block_rows)[:, None]
    col_pos = jnp.arange(key_rows.shape[0])[None, :]
    return jnp.where((col_pos <= row_pos)[None], raw_scores, -1e30)


def gelu_exact(pre_act):
    return jax.nn.gelu(pre_act, approximate=False)


def body(
    inputs,
    cotangent,
    first_gain,
    first_shift,
    second_gain,
    second_shift,
    project_weight,
    project_bias,
    dense_weight,
    dense_bias,
    expand_weight,
    expand_bias,
    shrink_weight,
    shrink_bias,
):
    project_full, expand_full = (
        lax.all_gather(project_weight, "fsdp", axis=0, tiled=True),
        lax.all_gather(expand_weight, "fsdp", axis=0, tiled=True),
    )
    dense_full, shrink_full = (
        lax.all_gather(dense_weight, "fsdp", axis=1, tiled=True),
        lax.all_gather(shrink_weight, "fsdp", axis=1, tiled=True),
    )
    model_width = project_full.shape[0]
    local_width = project_full.shape[2]
    heads_here = local_width // HS
    own_rows = inputs.astype(jnp.float32)
    own_grads = cotangent.astype(jnp.float32)
    first_out, first_normal, first_spread = normalize(own_rows, first_gain, first_shift)
    second_out, second_normal, second_spread = normalize(own_rows, second_gain, second_shift)
    first_normed, second_normed = (
        lax.all_gather(first_out.astype(jnp.bfloat16), "tp", axis=0, tiled=True),
        lax.all_gather(second_out.astype(jnp.bfloat16), "tp", axis=0, tiled=True),
    )
    row_count = first_normed.shape[0]
    seq_count = row_count // LEN
    block_rows = min(512, LEN)
    block_count = LEN // block_rows
    score_scale = HS ** (-0.5)
    project_flat = project_full.reshape(model_width, 3 * local_width)
    joined_rows = (
        jnp.dot(first_normed, project_flat, preferred_element_type=jnp.float32).reshape(
            row_count, 3, local_width
        )
        + project_bias[None]
    )
    cosine_table, sine_table = rotary_tables(row_count)
    queries = rotate(
        joined_rows[:, 0].reshape(row_count, heads_here, HS), cosine_table, sine_table
    ).astype(jnp.bfloat16)
    keys_all = rotate(
        joined_rows[:, 1].reshape(row_count, heads_here, HS), cosine_table, sine_table
    ).astype(jnp.bfloat16)
    values_all = joined_rows[:, 2].reshape(row_count, heads_here, HS).astype(jnp.bfloat16)

    def attend_sequence(seq_index):
        seq_start = seq_index * LEN
        seq_keys = lax.dynamic_slice_in_dim(keys_all, seq_start, LEN, 0)
        seq_values = lax.dynamic_slice_in_dim(values_all, seq_start, LEN, 0)

        def attend_block(block_index):
            first_row = block_index * block_rows
            block_queries = lax.dynamic_slice_in_dim(queries, seq_start + first_row, block_rows, 0)
            scores = causal_scores(block_queries, seq_keys, first_row, score_scale)
            row_top = jnp.max(scores, axis=-1, keepdims=True)
            shifted = jnp.exp(scores - row_top)
            row_total = jnp.sum(shifted, axis=-1, keepdims=True)
            weights_low = (shifted / row_total).astype(jnp.bfloat16)
            mixture = jnp.einsum(
                "hqk,khd->qhd", weights_low, seq_values, preferred_element_type=jnp.float32
            )
            return (mixture.astype(jnp.bfloat16), (row_top + jnp.log(row_total))[..., 0])

        return lax.map(attend_block, jnp.arange(block_count))

    context_blocks, log_totals = lax.map(attend_sequence, jnp.arange(seq_count))
    context = context_blocks.reshape(row_count, local_width)
    pre_act = jnp.dot(second_normed, expand_full, preferred_element_type=jnp.float32) + expand_bias
    activation = gelu_exact(pre_act).astype(jnp.bfloat16)
    branch = lax.psum_scatter(
        jnp.dot(context, dense_full, preferred_element_type=jnp.float32)
        + jnp.dot(activation, shrink_full, preferred_element_type=jnp.float32),
        "tp",
        scatter_dimension=0,
        tiled=True,
    )
    output = (own_rows + branch + dense_bias + shrink_bias).astype(jnp.bfloat16)
    grad_rows = lax.all_gather(cotangent, "tp", axis=0, tiled=True)
    dense_grad = jnp.dot(context.T, grad_rows, preferred_element_type=jnp.float32)
    shrink_grad = jnp.dot(activation.T, grad_rows, preferred_element_type=jnp.float32)
    context_grad = jnp.dot(grad_rows, dense_full.T, preferred_element_type=jnp.float32).astype(
        jnp.bfloat16
    )
    activation_grad = jnp.dot(grad_rows, shrink_full.T, preferred_element_type=jnp.float32)
    unused_value, gelu_pull = jax.vjp(gelu_exact, pre_act)
    pre_grad = gelu_pull(activation_grad)[0].astype(jnp.bfloat16)
    expand_grad = jnp.dot(second_normed.T, pre_grad, preferred_element_type=jnp.float32)
    expand_bias_part = jnp.sum(pre_grad.astype(jnp.float32), axis=0)
    second_grad = jnp.dot(pre_grad, expand_full.T, preferred_element_type=jnp.float32)
    context_heads = context_grad.reshape(row_count, heads_here, HS)

    def back_sequence(pack):
        seq_index, seq_totals = pack
        seq_start = seq_index * LEN
        seq_keys = lax.dynamic_slice_in_dim(keys_all, seq_start, LEN, 0)
        seq_values = lax.dynamic_slice_in_dim(values_all, seq_start, LEN, 0)

        def back_block(carry, item):
            key_sum, value_sum = carry
            block_index, block_totals = item
            first_row = block_index * block_rows
            block_queries = lax.dynamic_slice_in_dim(queries, seq_start + first_row, block_rows, 0)
            block_grads = lax.dynamic_slice_in_dim(
                context_heads, seq_start + first_row, block_rows, 0
            )
            scores = causal_scores(block_queries, seq_keys, first_row, score_scale)
            attention = jnp.exp(scores - block_totals[..., None])
            prob_grad = jnp.einsum(
                "qhd,khd->hqk", block_grads, seq_values, preferred_element_type=jnp.float32
            )
            score_grad = (
                attention * (prob_grad - jnp.sum(attention * prob_grad, axis=-1, keepdims=True))
            ).astype(jnp.bfloat16)
            query_part = (
                jnp.einsum("hqk,khd->qhd", score_grad, seq_keys, preferred_element_type=jnp.float32)
                * score_scale
            )
            key_sum = (
                key_sum
                + jnp.einsum(
                    "hqk,qhd->khd", score_grad, block_queries, preferred_element_type=jnp.float32
                )
                * score_scale
            )
            value_sum = value_sum + jnp.einsum(
                "hqk,qhd->khd",
                attention.astype(jnp.bfloat16),
                block_grads,
                preferred_element_type=jnp.float32,
            )
            return ((key_sum, value_sum), query_part)

        zero_heads = jnp.zeros((LEN, heads_here, HS), jnp.float32)
        (key_sum, value_sum), query_parts = lax.scan(
            back_block, (zero_heads, zero_heads), (jnp.arange(block_count), seq_totals)
        )
        return (query_parts.reshape(LEN, heads_here, HS), key_sum, value_sum)

    query_grad, key_grad, value_grad = lax.map(back_sequence, (jnp.arange(seq_count), log_totals))
    query_grad = rotate(query_grad.reshape(row_count, heads_here, HS), cosine_table, -sine_table)
    key_grad = rotate(key_grad.reshape(row_count, heads_here, HS), cosine_table, -sine_table)
    joined_grad = jnp.stack(
        [
            query_grad.reshape(row_count, local_width),
            key_grad.reshape(row_count, local_width),
            value_grad.reshape(row_count, local_width),
        ],
        axis=1,
    ).astype(jnp.bfloat16)
    project_bias_part = jnp.sum(joined_grad.astype(jnp.float32), axis=0)
    joined_flat = joined_grad.reshape(row_count, 3 * local_width)
    project_grad = jnp.dot(first_normed.T, joined_flat, preferred_element_type=jnp.float32).reshape(
        model_width, 3, local_width
    )
    first_grad = jnp.dot(joined_flat, project_flat.T, preferred_element_type=jnp.float32)
    first_rows, second_rows = (
        lax.psum_scatter(first_grad, "tp", scatter_dimension=0, tiled=True),
        lax.psum_scatter(second_grad, "tp", scatter_dimension=0, tiled=True),
    )
    input_grad = (
        own_grads
        + norm_back(first_rows, first_normal, first_spread, first_gain)
        + norm_back(second_rows, second_normal, second_spread, second_gain)
    )
    first_gain_part = jnp.sum(first_rows * first_normal, axis=0)
    first_shift_part = jnp.sum(first_rows, axis=0)
    second_gain_part = jnp.sum(second_rows * second_normal, axis=0)
    second_shift_part = jnp.sum(second_rows, axis=0)
    out_bias_part = jnp.sum(own_grads, axis=0)
    first_gain_grad, first_shift_grad, second_gain_grad, second_shift_grad, out_bias_grad = (
        lax.psum(
            (first_gain_part, first_shift_part, second_gain_part, second_shift_part, out_bias_part),
            ("fsdp", "tp"),
        )
    )
    project_bias_grad, expand_bias_grad = lax.psum((project_bias_part, expand_bias_part), "fsdp")
    project_weight_grad, expand_weight_grad = (
        lax.psum_scatter(project_grad, "fsdp", scatter_dimension=0, tiled=True),
        lax.psum_scatter(expand_grad, "fsdp", scatter_dimension=0, tiled=True),
    )
    dense_weight_grad, shrink_weight_grad = (
        lax.psum_scatter(dense_grad, "fsdp", scatter_dimension=1, tiled=True),
        lax.psum_scatter(shrink_grad, "fsdp", scatter_dimension=1, tiled=True),
    )
    return (
        output,
        input_grad,
        first_gain_grad,
        first_shift_grad,
        second_gain_grad,
        second_shift_grad,
        project_weight_grad,
        project_bias_grad,
        dense_weight_grad,
        out_bias_grad,
        expand_weight_grad,
        expand_bias_grad,
        shrink_weight_grad,
        out_bias_grad,
    )


def solution(mesh):
    return jax.shard_map(
        body,
        mesh=mesh,
        in_specs=(
            P(("fsdp", "tp"), None),
            P(("fsdp", "tp"), None),
            P(),
            P(),
            P(),
            P(),
            P("fsdp", None, "tp"),
            P(None, "tp"),
            P("tp", "fsdp"),
            P(),
            P("fsdp", "tp"),
            P("tp"),
            P("tp", "fsdp"),
            P(),
        ),
        out_specs=(
            P(("fsdp", "tp"), None),
            P(("fsdp", "tp"), None),
            P(),
            P(),
            P(),
            P(),
            P("fsdp", None, "tp"),
            P(None, "tp"),
            P("tp", "fsdp"),
            P(),
            P("fsdp", "tp"),
            P("tp"),
            P("tp", "fsdp"),
            P(),
        ),
        check_vma=False,
    )
```

profile of v0, /device:TPU:0, one launch (start us, length us, event | category | flops | bytes accessed | tf_op | source)
XLA Modules:
  0.0 1660.6 jit_solution(12958320723334942280)
XLA Ops:
  18.0 32.8 %all-gather.12.cloned.1.call-done = bf16[512,1024]{0,1:T(8,128)(2,1)} async-done(((bf16[512,64]{0,1:T(8,128)(2,1)}), bf16[512,1024]{0,1:T(8,128)(2,1)}) %all-gather.12.cloned.1.call-update) | async-done | bytes 1048592 | tf_op jit(solution)/shard_map/all_gather | solution.py:89
  50.8 57.3 %all-gather.20.cloned.1.call-done = bf16[2048,1024]{1,0:T(8,128)(2,1)} async-done(((bf16[1024,1024]{1,0:T(8,128)(2,1)}), bf16[2048,1024]{1,0:T(8,128)(2,1)}) %all-gather.20.cloned.1.call-update) | async-done | bytes 4194320 | tf_op jit(solution)/shard_map/all_gather | solution.py:156
  114.3 41.5 %all-gather.10.cloned.1.call-done = bf16[1024,3,512]{2,0,1:T(8,128)(2,1)} async-done(((bf16[64,3,512]{2,0,1:T(8,128)(2,1)}), bf16[1024,3,512]{2,0,1:T(8,128)(2,1)}) %all-gather.10.cloned.1.call-update) | async-done | bytes 3145744 | tf_op jit(solution)/shard_map/all_gather | solution.py:85
  160.5 51.8 %all-gather.8.cloned.1.call-done = bf16[2048,1024]{1,0:T(8,128)(2,1)} async-done(((bf16[1024,1024]{1,0:T(8,128)(2,1)}), bf16[2048,1024]{1,0:T(8,128)(2,1)}) %all-gather.8.cloned.1.call-update) | async-done | bytes 4194320 | tf_op jit(solution)/shard_map/all_gather | solution.py:100
  212.3 9.6 broadcast_add_fusion
  227.0 190.9 %while.49 = (s32[]{:T(128)}, bf16[4,512,8,64]{1,3,2,0:T(8,128)(2,1)}, f32[4,8,512]{2,1,0:T(8,128)S(1)}, s32[4]{0:T(128)S(1)}, bf16[2048,8,64]{0,2,1:T(8,128)(2,1...) while((s32[]{:T(128)}, ...), condition=%wide.region_5.6_spmd, body=%wide.region_2.5_spmd.sunk | while | flops 2249454080 | bytes 110236336 | solution.py:142
  229.4 14.8 fusion.120
  244.2 15.0 fusion.121
  259.2 15.6 fusion.122
  276.7 14.9 fusion.120
  291.6 15.3 fusion.121
  307.0 15.7 fusion.122
  324.6 15.0 fusion.120
  339.5 15.2 fusion.121
  354.8 15.8 fusion.122
  372.5 14.9 fusion.120
  387.4 15.0 fusion.121
  402.4 15.6 fusion.122
  417.9 523.5 %while.50 = (s32[]{:T(128)}, f32[2048,8,64]{0,2,1:T(8,128)}, f32[2048,8,64]{0,2,1:T(8,128)}, f32[4,512,8,64]{1,0,3,2:T(4,128)}, s32[4]{0:T(128)S(1)}, /*index=5*...) while((s32[]{:T(128)}, f32[2048,8,64]{0,2,1:T(8,128)}, ...), condition=%wide.region_9.10_spmd.clone, body=%wide.region_7.9_spmd.clone.sunk | while | flops 5450756608 | bytes 284250304 | solution.py:212
  419.3 17.4 %fusion.132 = f32[8,512,2048]{2,1,0:T(8,128)} fusion(bf16[2048,8,64]{0,2,1:T(8,128)(2,1)} %get-tuple-element.520, bf16[2048,8,64]{0,2,1:T(8,128)(2,1)} %get-tuple-element.519, s32[]{:T(128)S(6)} %select_n.101), kind=kOutput, calls=%fused_computation.28.clone.1 | convolution fusion | flops 1073741824 | bytes 36175876 | tf_op jit(solution)/shard_map/while/body/eval_jaxpr/while/body/eval_jaxpr/qhd,khd->hqk/dot_general | solution.py:186
  437.4 24.6 %multiply_reduce_fusion.4 = (f32[8,512]{1,0:T(8,128)S(1)}, f32[8,512,2048]{2,1,0:T(8,128)}) fusion(f32[8,512,2048]{2,1,0:T(8,128)} %fusion.132, f32[8,512]{1,0:T(8,128)S(1)} %dynamic-slice_bitcast_fusion.2, bf16[2048,8,64]{0,2,1:T(8,128)(2,1)S(1)} %get-tuple-element.517, bf16[2048,8,64]{0,2,1:T(8,128)(2,1)} %get-tuple-element.516, ...), kind=kOutput, calls=%fused_computation.18.clone.1 | convolution fusion | flops 1115680768 | bytes 70811648 | tf_op jit(solution)/shard_map/while/body/eval_jaxpr/while/body/eval_jaxpr/qhd,khd->hqk/dot_general | solution.py:56
  462.0 27.4 %multiply_convert_fusion.3 = bf16[8,512,2048]{2,1,0:T(8,128)(2,1)} fusion(f32[8,512,2048]{2,1,0:T(8,128)} %get-tuple-element.448, f32[8,512,2048]{2,1,0:T(8,128)} %fusion.132, f32[8,512]{1,0:T(8,128)S(1)} %get-tuple-element.449), kind=kLoop, calls=%fused_computation.17.clone.1 | loop fusion | flops 25165824 | bytes 83902464 | tf_op jit(solution)/shard_map/while/body/eval_jaxpr/while/body/eval_jaxpr/convert_element_type | solution.py:191
  489.4 8.7 fusion.133
  499.2 21.0 %dynamic_update_slice.39 = f32[4,512,8,64]{1,0,3,2:T(4,128)} dynamic-update-slice(f32[4,512,8,64]{1,0,3,2:T(4,128)} %get-tuple-element.500, f32[1,512,8,64]{1,0,3,2:T(1,128)S(1)} %copy.59, s32[]{:T(128)} %get-tuple-element.497, s32[]{:T(128)} %constant.176.clone.1..sunk.1, s32[]{:T(128)} %constant.176.clone.1..sunk.1, s32[]{:T(128)} %constant.176.clone.1..sunk.1) | dynamic-update-slice | bytes 2097156 | tf_op jit(solution)/shard_map/while/body/eval_jaxpr/while/body/jit(dynamic_update_index_in_dim)/dynamic_update_slice | solution.py:212
  520.2 11.0 bitcast_add_fusion.4
  531.2 15.8 bitcast_add_fusion.5
  548.3 17.4 %fusion.132 = f32[8,512,2048]{2,1,0:T(8,128)} fusion(bf16[2048,8,64]{0,2,1:T(8,128)(2,1)} %get-tuple-element.520, bf16[2048,8,64]{0,2,1:T(8,128)(2,1)} %get-tuple-element.519, s32[]{:T(128)S(6)} %select_n.101), kind=kOutput, calls=%fused_computation.28.clone.1 | convolution fusion | flops 1073741824 | bytes 36175876 | tf_op jit(solution)/shard_map/while/body/eval_jaxpr/while/body/eval_jaxpr/qhd,khd->hqk/dot_general | solution.py:186
  566.3 24.6 %multiply_reduce_fusion.4 = (f32[8,512]{1,0:T(8,128)S(1)}, f32[8,512,2048]{2,1,0:T(8,128)}) fusion(f32[8,512,2048]{2,1,0:T(8,128)} %fusion.132, f32[8,512]{1,0:T(8,128)S(1)} %dynamic-slice_bitcast_fusion.2, bf16[2048,8,64]{0,2,1:T(8,128)(2,1)S(1)} %get-tuple-element.517, bf16[2048,8,64]{0,2,1:T(8,128)(2,1)} %get-tuple-element.516, ...), kind=kOutput, calls=%fused_computation.18.clone.1 | convolution fusion | flops 1115680768 | bytes 70811648 | tf_op jit(solution)/shard_map/while/body/eval_jaxpr/while/body/eval_jaxpr/qhd,khd->hqk/dot_general | solution.py:56
  591.0 27.4 %multiply_convert_fusion.3 = bf16[8,512,2048]{2,1,0:T(8,128)(2,1)} fusion(f32[8,512,2048]{2,1,0:T(8,128)} %get-tuple-element.448, f32[8,512,2048]{2,1,0:T(8,128)} %fusion.132, f32[8,512]{1,0:T(8,128)S(1)} %get-tuple-element.449), kind=kLoop, calls=%fused_computation.17.clone.1 | loop fusion | flops 25165824 | bytes 83902464 | tf_op jit(solution)/shard_map/while/body/eval_jaxpr/while/body/eval_jaxpr/convert_element_type | solution.py:191
  618.4 8.7 fusion.133
  628.2 21.0 %dynamic_update_slice.39 = f32[4,512,8,64]{1,0,3,2:T(4,128)} dynamic-update-slice(f32[4,512,8,64]{1,0,3,2:T(4,128)} %get-tuple-element.500, f32[1,512,8,64]{1,0,3,2:T(1,128)S(1)} %copy.59, s32[]{:T(128)} %get-tuple-element.497, s32[]{:T(128)} %constant.176.clone.1..sunk.1, s32[]{:T(128)} %constant.176.clone.1..sunk.1, s32[]{:T(128)} %constant.176.clone.1..sunk.1) | dynamic-update-slice | bytes 2097156 | tf_op jit(solution)/shard_map/while/body/eval_jaxpr/while/body/jit(dynamic_update_index_in_dim)/dynamic_update_slice | solution.py:212
  649.2 12.2 bitcast_add_fusion.4
  661.4 17.0 %bitcast_add_fusion.5 = f32[2048,8,64]{0,2,1:T(8,128)} fusion(f32[2048,8,64]{0,2,1:T(8,128)} %get-tuple-element.499, f32[8,512,2048]{2,1,0:T(8,128)} %get-tuple-element.448, pred[]{:T(512)S(6)} %compare.4, bf16[2048,8,64]{0,2,1:T(8,128)(2,1)} %get-tuple-element.519, s32[]{:T(128)S(6)} %select_n.101), kind=kOutput, calls=%fused_computation.22.clone.1 | convolution fusion | flops 1084227584 | bytes 42467332 | tf_op jit(solution)/shard_map/while/body/eval_jaxpr/while/body/eval_jaxpr/hqk,qhd->khd/dot_general | solution.py:203
  679.6 17.4 %fusion.132 = f32[8,512,2048]{2,1,0:T(8,128)} fusion(bf16[2048,8,64]{0,2,1:T(8,128)(2,1)} %get-tuple-element.520, bf16[2048,8,64]{0,2,1:T(8,128)(2,1)} %get-tuple-element.519, s32[]{:T(128)S(6)} %select_n.101), kind=kOutput, calls=%fused_computation.28.clone.1 | convolution fusion | flops 1073741824 | bytes 36175876 | tf_op jit(solution)/shard_map/while/body/eval_jaxpr/while/body/eval_jaxpr/qhd,khd->hqk/dot_general | solution.py:186
  697.7 24.6 %multiply_reduce_fusion.4 = (f32[8,512]{1,0:T(8,128)S(1)}, f32[8,512,2048]{2,1,0:T(8,128)}) fusion(f32[8,512,2048]{2,1,0:T(8,128)} %fusion.132, f32[8,512]{1,0:T(8,128)S(1)} %dynamic-slice_bitcast_fusion.2, bf16[2048,8,64]{0,2,1:T(8,128)(2,1)S(1)} %get-tuple-element.517, bf16[2048,8,64]{0,2,1:T(8,128)(2,1)} %get-tuple-element.516, ...), kind=kOutput, calls=%fused_computation.18.clone.1 | convolution fusion | flops 1115680768 | bytes 70811648 | tf_op jit(solution)/shard_map/while/body/eval_jaxpr/while/body/eval_jaxpr/qhd,khd->hqk/dot_general | solution.py:56
  722.3 27.4 %multiply_convert_fusion.3 = bf16[8,512,2048]{2,1,0:T(8,128)(2,1)} fusion(f32[8,512,2048]{2,1,0:T(8,128)} %get-tuple-element.448, f32[8,512,2048]{2,1,0:T(8,128)} %fusion.132, f32[8,512]{1,0:T(8,128)S(1)} %get-tuple-element.449), kind=kLoop, calls=%fused_computation.17.clone.1 | loop fusion | flops 25165824 | bytes 83902464 | tf_op jit(solution)/shard_map/while/body/eval_jaxpr/while/body/eval_jaxpr/convert_element_type | solution.py:191
  749.7 8.7 fusion.133
  759.5 21.0 %dynamic_update_slice.39 = f32[4,512,8,64]{1,0,3,2:T(4,128)} dynamic-update-slice(f32[4,512,8,64]{1,0,3,2:T(4,128)} %get-tuple-element.500, f32[1,512,8,64]{1,0,3,2:T(1,128)S(1)} %copy.59, s32[]{:T(128)} %get-tuple-element.497, s32[]{:T(128)} %constant.176.clone.1..sunk.1, s32[]{:T(128)} %constant.176.clone.1..sunk.1, s32[]{:T(128)} %constant.176.clone.1..sunk.1) | dynamic-update-slice | bytes 2097156 | tf_op jit(solution)/shard_map/while/body/eval_jaxpr/while/body/jit(dynamic_update_index_in_dim)/dynamic_update_slice | solution.py:212
  780.5 12.2 bitcast_add_fusion.4
  792.7 17.0 %bitcast_add_fusion.5 = f32[2048,8,64]{0,2,1:T(8,128)} fusion(f32[2048,8,64]{0,2,1:T(8,128)} %get-tuple-element.499, f32[8,512,2048]{2,1,0:T(8,128)} %get-tuple-element.448, pred[]{:T(512)S(6)} %compare.4, bf16[2048,8,64]{0,2,1:T(8,128)(2,1)} %get-tuple-element.519, s32[]{:T(128)S(6)} %select_n.101), kind=kOutput, calls=%fused_computation.22.clone.1 | convolution fusion | flops 1084227584 | bytes 42467332 | tf_op jit(solution)/shard_map/while/body/eval_jaxpr/while/body/eval_jaxpr/hqk,qhd->khd/dot_general | solution.py:203
  810.9 17.4 %fusion.132 = f32[8,512,2048]{2,1,0:T(8,128)} fusion(bf16[2048,8,64]{0,2,1:T(8,128)(2,1)} %get-tuple-element.520, bf16[2048,8,64]{0,2,1:T(8,128)(2,1)} %get-tuple-element.519, s32[]{:T(128)S(6)} %select_n.101), kind=kOutput, calls=%fused_computation.28.clone.1 | convolution fusion | flops 1073741824 | bytes 36175876 | tf_op jit(solution)/shard_map/while/body/eval_jaxpr/while/body/eval_jaxpr/qhd,khd->hqk/dot_general | solution.py:186
  829.0 24.6 %multiply_reduce_fusion.4 = (f32[8,512]{1,0:T(8,128)S(1)}, f32[8,512,2048]{2,1,0:T(8,128)}) fusion(f32[8,512,2048]{2,1,0:T(8,128)} %fusion.132, f32[8,512]{1,0:T(8,128)S(1)} %dynamic-slice_bitcast_fusion.2, bf16[2048,8,64]{0,2,1:T(8,128)(2,1)S(1)} %get-tuple-element.517, bf16[2048,8,64]{0,2,1:T(8,128)(2,1)} %get-tuple-element.516, ...), kind=kOutput, calls=%fused_computation.18.clone.1 | convolution fusion | flops 1115680768 | bytes 70811648 | tf_op jit(solution)/shard_map/while/body/eval_jaxpr/while/body/eval_jaxpr/qhd,khd->hqk/dot_general | solution.py:56
  853.6 27.4 %multiply_convert_fusion.3 = bf16[8,512,2048]{2,1,0:T(8,128)(2,1)} fusion(f32[8,512,2048]{2,1,0:T(8,128)} %get-tuple-element.448, f32[8,512,2048]{2,1,0:T(8,128)} %fusion.132, f32[8,512]{1,0:T(8,128)S(1)} %get-tuple-element.449), kind=kLoop, calls=%fused_computation.17.clone.1 | loop fusion | flops 25165824 | bytes 83902464 | tf_op jit(solution)/shard_map/while/body/eval_jaxpr/while/body/eval_jaxpr/convert_element_type | solution.py:191
  881.0 8.7 fusion.133
  890.8 21.0 %dynamic_update_slice.39 = f32[4,512,8,64]{1,0,3,2:T(4,128)} dynamic-update-slice(f32[4,512,8,64]{1,0,3,2:T(4,128)} %get-tuple-element.500, f32[1,512,8,64]{1,0,3,2:T(1,128)S(1)} %copy.59, s32[]{:T(128)} %get-tuple-element.497, s32[]{:T(128)} %constant.176.clone.1..sunk.1, s32[]{:T(128)} %constant.176.clone.1..sunk.1, s32[]{:T(128)} %constant.176.clone.1..sunk.1) | dynamic-update-slice | bytes 2097156 | tf_op jit(solution)/shard_map/while/body/eval_jaxpr/while/body/jit(dynamic_update_index_in_dim)/dynamic_update_slice | solution.py:212
  911.8 12.2 bitcast_add_fusion.4
  924.0 17.0 %bitcast_add_fusion.5 = f32[2048,8,64]{0,2,1:T(8,128)} fusion(f32[2048,8,64]{0,2,1:T(8,128)} %get-tuple-element.499, f32[8,512,2048]{2,1,0:T(8,128)} %get-tuple-element.448, pred[]{:T(512)S(6)} %compare.4, bf16[2048,8,64]{0,2,1:T(8,128)(2,1)} %get-tuple-element.519, s32[]{:T(128)S(6)} %select_n.101), kind=kOutput, calls=%fused_computation.22.clone.1 | convolution fusion | flops 1084227584 | bytes 42467332 | tf_op jit(solution)/shard_map/while/body/eval_jaxpr/while/body/eval_jaxpr/hqk,qhd->khd/dot_general | solution.py:203
  972.0 9.0 convolution_bitcast_fusion
  981.6 49.4 %multiply_convert_fusion.1 = (bf16[2048,2048]{1,0:T(8,128)(2,1)}, f32[2048,2048]{1,0:T(8,128)}, f32[2048,2048]{1,0:T(8,128)}) fusion(f32[2048]{0:T(1024)S(1)} %copy-done.25, bf16[2048,1024]{1,0:T(8,128)(2,1)} %all-gather.14.cloned.1.call-done, bf16[1024,2048]{1,0:T(8,128)(2,1)} %all-gather.16.cloned.1.call-done), kind=kOutput, calls=%fused_computation.42 | convolution fusion | flops 8866758656 | bytes 50339840 | tf_op jit(solution)/shard_map/dot_general | solution.py:146
  1031.0 27.8 %convert_reduce_fusion = (f32[2048]{0:T(1024)S(1)}, bf16[2048,2048]{1,0:T(8,128)(2,1)}) fusion(f32[2048,2048]{1,0:T(8,128)} %get-tuple-element.306, bf16[2048,1024]{1,0:T(8,128)(2,1)} %all-gather.20.cloned.1.call-done, bf16[2048,1024]{0,1:T(8,128)(2,1)} %all-gather.18.cloned.1.call-done, f32[2048,2048]{1,0:T(8,128)} %get-tuple-element.333, ...), kind=kOutput, calls=%fused_computation.40 | convolution fusion | flops 8661235712 | bytes 50348032 | tf_op jit(solution)/shard_map/dot_general | solution.py:162
  1058.8 14.5 fusion.71
  1077.2 11.4 fusion.70
  1100.7 8.8 copy.38
  1109.5 11.9 fusion.31
  1121.5 14.7 fusion.73
  1136.5 14.9 fusion.74
  1152.2 61.4 %all-reduce.1 = (f32[3,512]{1,0:T(4,128)}, f32[2048]{0:T(1024)}) all-reduce(f32[3,512]{1,0:T(4,128)S(1)} %copy-done.17, f32[2048]{0:T(1024)S(1)} %get-tuple-element.334), channel_id=1, replica_groups=mesh['fsdp'=16,'tp'=2] {'fsdp'}, use_global_device_ids=true, to_apply=%region_26.27 | all-reduce | flops 3584 | bytes 28672 | tf_op jit(solution)/shard_map/psum | solution.py:254
  1219.2 64.6 %reduce-scatter.8.cloned.1.call-done = f32[1024,1024]{1,0:T(8,128)} async-done(((f32[2048,1024]{1,0:T(8,128)}), f32[1024,1024]{1,0:T(8,128)}) %reduce-scatter.8.cloned.1.call-update) | async-done | bytes 4194320 | tf_op jit(solution)/shard_map/reduce_scatter | solution.py:148
  1283.8 8.5 convert_reduce_fusion.3
  1292.4 40.1 %all-reduce = (f32[1024]{0:T(1024)}, f32[1024]{0:T(1024)}, f32[1024]{0:T(1024)}, f32[1024]{0:T(1024)}, f32[1024]{0:T(1024)S(1)}) all-reduce(f32[1024]{0:T(1024)S(1)} %get-tuple-element.252, f32[1024]{0:T(1024)S(1)} %get-tuple-element.257, f32[1024]{0:T(1024)S(1)} %get-tuple-element.261, ...), channel_id=1, replica_groups=mesh['fsdp'=16,'tp'=2] {'fsdp','tp'}, use_global_device_ids=true, to_apply=%region_17.18 | all-reduce | flops 5120 | bytes 40960 | tf_op jit(solution)/shard_map/psum | solution.py:249
  1332.4 17.6 %reduce-scatter.16.cloned.1.call-done = f32[512,64]{0,1:T(8,128)} async-done(((f32[512,1024]{0,1:T(8,128)}), f32[512,64]{0,1:T(8,128)}) %reduce-scatter.16.cloned.1.call-update) | async-done | bytes 131088 | tf_op jit(solution)/shard_map/reduce_scatter | solution.py:260
  1350.1 88.4 %reduce-scatter.14.cloned.1.call-done = f32[64,3,512]{2,0,1:T(8,128)} async-done(((f32[1024,3,512]{2,0,1:T(8,128)}), f32[64,3,512]{2,0,1:T(8,128)}) %reduce-scatter.14.cloned.1.call-update) | async-done | bytes 393232 | tf_op jit(solution)/shard_map/reduce_scatter | solution.py:256
  1438.5 107.2 %reduce-scatter.18.cloned.1.call-done = f32[64,2048]{1,0:T(8,128)} async-done(((f32[1024,2048]{1,0:T(8,128)}), f32[64,2048]{1,0:T(8,128)}) %reduce-scatter.18.cloned.1.call-update) | async-done | bytes 524304 | tf_op jit(solution)/shard_map/reduce_scatter | solution.py:257
  1545.7 107.6 %reduce-scatter.20.cloned.1.call-done = f32[2048,64]{0,1:T(8,128)} async-done(((f32[2048,1024]{0,1:T(8,128)}), f32[2048,64]{0,1:T(8,128)}) %reduce-scatter.20.cloned.1.call-update) | async-done | bytes 524304 | tf_op jit(solution)/shard_map/reduce_scatter | solution.py:261
  (164 shorter events, 95.0 us)
Async XLA Ops:
  7.2 4.3 copy-start
  7.2 5.0 copy-start.13
  7.2 5.0 copy-start.18
  7.2 5.0 copy-start.15
  7.2 5.0 copy-start.19
  7.2 43.6 %all-gather.12.cloned.1.call-start = ((), (), s32[]{:S(2)}) async-start(), calls=%async_computation.9 | async-start | bytes 1114112 | tf_op jit(solution)/shard_map/all_gather | solution.py:89
  8.0 100.1 %all-gather.20.cloned.1.call-start = ((), (), s32[]{:S(2)}) async-start(), calls=%async_computation.14 | async-start | bytes 6291456 | tf_op jit(solution)/shard_map/all_gather | solution.py:156
  8.7 147.1 %all-gather.10.cloned.1.call-start = ((), (), s32[]{:S(2)}) async-start(), calls=%async_computation.8 | async-start | bytes 3342336 | tf_op jit(solution)/shard_map/all_gather | solution.py:85
  9.5 202.9 %all-gather.8.cloned.1.call-start = ((), (), s32[]{:S(2)}) async-start(), calls=%async_computation.7 | async-start | bytes 6291456 | tf_op jit(solution)/shard_map/all_gather | solution.py:100
  11.5 3.6 copy-start.9
  12.2 2.8 copy-start.11
  15.0 966.0 %all-gather.14.cloned.1.call-start = ((), (), s32[]{:S(2)}) async-start(), calls=%async_computation.10 | async-start | bytes 6291456 | tf_op jit(solution)/shard_map/all_gather | solution.py:101
  15.6 965.4 %all-gather.16.cloned.1.call-start = ((), (), s32[]{:S(2)}) async-start(), calls=%async_computation.11 | async-start | bytes 4456448 | tf_op jit(solution)/shard_map/all_gather | solution.py:86
  16.2 1014.8 %all-gather.18.cloned.1.call-start = ((), (), s32[]{:S(2)}) async-start(), calls=%async_computation.12 | async-start | bytes 4456448 | tf_op jit(solution)/shard_map/all_gather | solution.py:90
  17.0 1196.6 %reduce-scatter.10.cloned.1.call-start = ((), (), s32[]{:S(2)}) async-start(), calls=%async_computation.15 | async-start | bytes 12582912 | tf_op jit(solution)/shard_map/reduce_scatter | solution.py:235
  18.0 207.1 %copy-start.6 = (f32[2048,8]{0,1:T(8,128)}, f32[2048,8]{0,1:T(8,128)S(1)}, u32[]{:S(2)}) copy-start(f32[2048,8]{0,1:T(8,128)S(1)} %get-tuple-element.332) | copy-start | bytes 196612
  114.3 98.0 %copy-start.24 = (f32[3,512]{1,0:T(4,128)S(1)}, f32[3,512]{1,0:T(4,128)}, u32[]{:S(2)}) copy-start(f32[3,512]{1,0:T(4,128)} %param.25) | copy-start | bytes 18436
  947.5 5.4 copy-start.7
  947.5 5.4 copy-start.8
  964.9 7.1 copy-start.3
  969.2 2.7 copy-start.2
  980.9 0.7 copy-start.25
  980.9 232.6 %reduce-scatter.12.cloned.1.call-start = ((), (), s32[]{:S(2)}) async-start(), calls=%async_computation.16 | async-start | bytes 12582912 | tf_op jit(solution)/shard_map/reduce_scatter | solution.py:236
  1073.3 1.6 copy-start.4
  1073.4 210.5 %reduce-scatter.8.cloned.1.call-start = ((), (), s32[]{:S(2)}) async-start(), calls=%async_computation.13 | async-start | bytes 12582912 | tf_op jit(solution)/shard_map/reduce_scatter | solution.py:148
  1074.9 2.3 copy-start.23
  1077.2 11.4 copy-start.5
  1094.2 255.8 %reduce-scatter.16.cloned.1.call-start = ((), (), s32[]{:S(2)}) async-start(), calls=%async_computation.18 | async-start | bytes 2228224 | tf_op jit(solution)/shard_map/reduce_scatter | solution.py:260
  1100.3 338.2 %reduce-scatter.14.cloned.1.call-start = ((), (), s32[]{:S(2)}) async-start(), calls=%async_computation.17 | async-start | bytes 6684672 | tf_op jit(solution)/shard_map/reduce_scatter | solution.py:256
  1121.5 424.2 %reduce-scatter.18.cloned.1.call-start = ((), (), s32[]{:S(2)}) async-start(), calls=%async_computation.19 | async-start | bytes 8912896 | tf_op jit(solution)/shard_map/reduce_scatter | solution.py:257
  1136.3 517.0 %reduce-scatter.20.cloned.1.call-start = ((), (), s32[]{:S(2)}) async-start(), calls=%async_computation.20 | async-start | bytes 8912896 | tf_op jit(solution)/shard_map/reduce_scatter | solution.py:261
  1151.5 0.7 copy-start.17
  1151.5 62.1 %copy-start.1 = (bf16[1024,1024]{1,0:T(8,128)(2,1)S(1)}, bf16[1024,1024]{1,0:T(8,128)(2,1)}, u32[]{:S(2)}) copy-start(bf16[1024,1024]{1,0:T(8,128)(2,1)} %param.18) | copy-start | bytes 6291460
  1151.5 62.1 %copy-start.10 = (f32[1024]{0:T(1024)S(1)}, f32[1024]{0:T(1024)}, u32[]{:S(2)}) copy-start(f32[1024]{0:T(1024)} %copy-done.9) | copy-start | bytes 12292
  1151.5 62.1 %copy-start.12 = (f32[1024]{0:T(1024)S(1)}, f32[1024]{0:T(1024)}, u32[]{:S(2)}) copy-start(f32[1024]{0:T(1024)} %copy-done.11) | copy-start | bytes 12292
  1151.5 62.1 %copy-start.14 = (f32[1024]{0:T(1024)S(1)}, f32[1024]{0:T(1024)}, u32[]{:S(2)}) copy-start(f32[1024]{0:T(1024)} %param.20) | copy-start | bytes 12292
  1151.5 62.1 %copy-start.16 = (f32[1024]{0:T(1024)S(1)}, f32[1024]{0:T(1024)}, u32[]{:S(2)}) copy-start(f32[1024]{0:T(1024)} %param.22) | copy-start | bytes 12292
  1213.5 70.3 %copy-start.20 = (f32[1024]{0:T(1024)S(1)}, f32[1024]{0:T(1024)}, u32[]{:S(2)}) copy-start(f32[1024]{0:T(1024)} %param.31) | copy-start | bytes 12292
  1213.5 70.3 %copy-start.21 = (f32[1024]{0:T(1024)S(1)}, f32[1024]{0:T(1024)}, u32[]{:S(2)}) copy-start(f32[1024]{0:T(1024)} %param.27) | copy-start | bytes 12292
  1332.4 321.5 %copy-start.22 = (f32[1024]{0:T(1024)}, f32[1024]{0:T(1024)S(1)}, u32[]{:S(2)}) copy-start(f32[1024]{0:T(1024)S(1)} %get-tuple-element.552) | copy-start | bytes 12292
Sparse Core Ops, SparseCore 0:
  10.2 40.5 all-gather.11
  52.3 55.6 all-gather.19
  110.3 45.4 all-gather.9
  157.2 55.0 all-gather.7
  213.7 56.7 all-gather.13
  272.5 50.3 all-gather.15
  325.0 48.8 all-gather.17
  981.1 99.5 reduce-scatter.9
  1083.0 99.3 reduce-scatter.11
  1184.5 99.3 reduce-scatter.7
  1288.1 61.8 reduce-scatter.15
  1354.4 83.9 reduce-scatter.13
  1443.1 102.5 reduce-scatter.17
  1550.1 103.0 reduce-scatter.19
where the time goes:
time: 1670 us; the launch traced here: 1660 us
  matrix products  621 us (37%)
  waiting for transfers between devices  573 us (34%)
  other arithmetic  206 us (12%)
  local copies, waits for them, and re-layouts  138 us (8%)
  blocking collectives  101 us (6%)
    dot_general x8, matrix products, causal_scores(): jnp.einsum('qhd,khd->hqk', query_rows, key_rows, preferred_element_type=j...  158 us
    convert_element_type x4, other arithmetic, back_block(): score_grad = (attention * (prob_grad - jnp.sum(attention * prob_grad, axi...  110 us
    reduce_scatter x1, waiting for transfers between devices, body(): lax.psum_scatter(shrink_grad, 'fsdp', scatter_dimension=1, tiled=True)  108 us
    reduce_scatter x1, waiting for transfers between devices, body(): lax.psum_scatter(expand_grad, 'fsdp', scatter_dimension=0, tiled=True)  107 us
    reduce_scatter x1, waiting for transfers between devices, body(): lax.psum_scatter(project_grad, 'fsdp', scatter_dimension=0, tiled=True)  88.4 us
    dynamic_update_slice x8, local copies, waits for them, and re-layouts, back_sequence(): lax.scan(back_block, (zero_heads, zero_heads), (jnp.arange(block_count),...  88.3 us
    dot_general x4, matrix products, back_block(): jnp.einsum('qhd,khd->hqk', block_grads, seq_values, preferred_element_typ...  69.5 us
    dot_general x4, matrix products, back_block(): jnp.einsum('hqk,qhd->khd', attention.astype(jnp.bfloat16), block_grads, p...  66.8 us
  transfers between devices with their start and end apart: 14, of which 9 were waited for; matrix products, arithmetic and copies ran while one was open for 58% of the time, Pallas kernels for 0%

commit v1 on v0

v1 whole, which is shorter than its diff:
```python
import functools

import jax
import jax.numpy as jnp
from jax import lax
from jax.experimental import pallas as pl
from jax.experimental.pallas import tpu as pltpu
from jax.sharding import PartitionSpec as P

f32, bf16 = jnp.float32, jnp.bfloat16
HS = 64
ROT = 16
LEN = 2048
EPS = 1e-05
NEG = -1e30
VMEM_LIMIT = 60 << 20
ERFC = (
    0.22567586308569043,
    0.22566953354787173,
    0.20784372127485384,
    0.1685348386069925,
    0.14145750936579315,
    -0.005660950942278366,
    0.16914715407444447,
    -0.18293900460081808,
    0.050271460956987875,
)


def dot(a, b, ca=1, cb=0):
    return lax.dot_general(a, b, (((ca,), (cb,)), ((), ())), preferred_element_type=f32)


def gelu_parts(x):
    t = pl.reciprocal(1.0 + (0.4 * 0.5**0.5) * jnp.abs(x))
    poly = jnp.full_like(t, ERFC[-1])
    for c in ERFC[-2::-1]:
        poly = poly * t + c
    e = jnp.exp(-0.5 * (x * x))
    tail = (0.5 * t) * poly * e
    cdf = jnp.where(x < 0, tail, 1.0 - tail)
    return x * cdf, cdf + x * (e * 0.3989422804014327)


def params():
    return pltpu.CompilerParams(vmem_limit_bytes=VMEM_LIMIT)


def held(rows, cols, col_block=0):
    return pl.BlockSpec((rows, cols), lambda *i: (0, col_block), pipeline_mode=pl.Buffered(1))


def shape(rows, cols, dtype):
    return jax.ShapeDtypeStruct((rows, cols), dtype)


def qkv_kernel(shift, x_ref, vec_ref, w_ref, b_ref, c_ref, sa_ref, sb_ref, n1_ref, n2_ref, st_ref, q_ref, k_ref, v_ref):
    x = x_ref[...].astype(f32)
    mean = jnp.mean(x, axis=1, keepdims=True)
    centred = x - mean
    rstd = lax.rsqrt(jnp.mean(centred * centred, axis=1, keepdims=True) + EPS)
    normal = centred * rstd
    st_ref[:, 0:1] = mean
    st_ref[:, 1:2] = rstd
    n1 = (normal * vec_ref[0:1, :] + vec_ref[1:2, :]).astype(bf16)
    n1_ref[...] = n1
    n2_ref[...] = (normal * vec_ref[2:3, :] + vec_ref[3:4, :]).astype(bf16)
    width = q_ref.shape[1]
    tables = [jnp.concatenate([r[...]] * (width // 128), axis=1) for r in (c_ref, sa_ref, sb_ref)]
    for part, ref in enumerate((q_ref, k_ref, v_ref)):
        y = dot(n1, w_ref[:, part * width : (part + 1) * width]) + b_ref[part : part + 1, :]
        if part < 2:
            y = turn(y, *tables)
        if part == 0:
            y = y * HS**-0.5
        ref[...] = y.astype(bf16)


def turn(y, cos, sin_up, sin_down):
    width = y.shape[1]
    half = ROT // 2
    return y * cos + pltpu.roll(y, width - half, 1) * sin_up + pltpu.roll(y, half, 1) * sin_down


def qkv_call(shift, x, vec, w1, bias, tables, width, rows=256):
    g, d = x.shape
    n = g // rows
    own = lambda c: pl.BlockSpec((rows, c), lambda i, s: (i, 0))
    seq = lambda c: pl.BlockSpec((rows, c), lambda i, s: ((i + s[0] // rows) % n, 0))
    table = pl.BlockSpec((rows, 128), lambda i, s: (((i + s[0] // rows) % n) % (LEN // rows), 0))
    return pl.pallas_call(
        qkv_kernel,
        grid_spec=pltpu.PrefetchScalarGridSpec(
            num_scalar_prefetch=1,
            grid=(n,),
            in_specs=[own(d), held(4, d), held(d, 3 * width), held(3, width), table, table, table],
            out_specs=[own(d), own(d), own(2), seq(width), seq(width), seq(width)],
        ),
        out_shape=[shape(g, d, bf16), shape(g, d, bf16), shape(g, 2, f32)] + [shape(g, width, bf16)] * 3,
        compiler_params=params(),
    )(shift, x, vec, w1, bias, *tables)


def context_grad_kernel(shift, g_ref, w_ref, do_ref):
    do_ref[...] = dot(g_ref[...], w_ref[...]).astype(bf16)


def context_grad_call(shift, grads, w1, width, rows=512):
    g, d = grads.shape
    n = g // rows
    return pl.pallas_call(
        context_grad_kernel,
        grid_spec=pltpu.PrefetchScalarGridSpec(
            num_scalar_prefetch=1,
            grid=(n,),
            in_specs=[pl.BlockSpec((rows, d), lambda i, s: (i, 0)), held(d, width, 3)],
            out_specs=pl.BlockSpec((rows, width), lambda i, s: ((i + s[0] // rows) % n, 0)),
        ),
        out_shape=shape(g, width, bf16),
        compiler_params=params(),
    )(shift, grads, w1)


def attention_kernel(q_ref, k_ref, v_ref, do_ref, c_ref, sa_ref, sb_ref, o_ref, dq_ref, dk_ref, dv_ref, dk_sum, dv_sum, *, block):
    step = pl.program_id(2)
    count = LEN // block
    heads = q_ref.shape[1] // HS

    @pl.when(step == 0)
    def _():
        dk_sum[...] = jnp.zeros_like(dk_sum)
        dv_sum[...] = jnp.zeros_like(dv_sum)

    def turn_back(y, rows):
        return turn(y, c_ref[rows, :], -sa_ref[rows, :], -sb_ref[rows, :])

    def run(i):
        outs, dqs = [], []
        for h in range(heads):
            lanes = slice(h * HS, (h + 1) * HS)
            q, do = q_ref[:, lanes], do_ref[:, lanes]
            parts = [slice(j * block, (j + 1) * block) for j in range(i + 1)]
            scores = [dot(k_ref[rows, lanes], q, 1, 1) for rows in parts]
            key_pos = lax.broadcasted_iota(jnp.int32, (block, block), 0)
            query_pos = lax.broadcasted_iota(jnp.int32, (block, block), 1)
            scores[i] = jnp.where(key_pos <= query_pos, scores[i], NEG)
            top = functools.reduce(jnp.maximum, [jnp.max(s, axis=0, keepdims=True) for s in scores])
            weights = [jnp.exp(s - top) for s in scores]
            total = functools.reduce(jnp.add, [jnp.sum(w, axis=0, keepdims=True) for w in weights])
            scale = 1.0 / total
            weights = [w * scale for w in weights]
            low = [w.astype(bf16) for w in weights]
            mixed = functools.reduce(jnp.add, [dot(v_ref[rows, lanes], low[j], 0, 0) for j, rows in enumerate(parts)])
            do_t = do.astype(f32).T
            delta = jnp.sum(mixed * do_t, axis=0, keepdims=True)
            do_t = do_t.astype(bf16)
            q_t = q.astype(f32).T.astype(bf16)
            dq = 0.0
            for j, rows in enumerate(parts):
                prob_grad = dot(v_ref[rows, lanes], do, 1, 1)
                score_grad = (weights[j] * (prob_grad - delta)).astype(bf16)
                dv_sum[lanes, rows] += dot(do_t, low[j], 1, 1)
                dk_sum[lanes, rows] += dot(q_t, score_grad, 1, 1)
                dq = dq + dot(k_ref[rows, lanes], score_grad, 0, 0)
            outs.append(mixed.T)
            dqs.append(dq.T)
        o_ref[...] = jnp.concatenate(outs, axis=1).astype(bf16)
        here = slice(i * block, (i + 1) * block)
        dq_ref[...] = turn_back(jnp.concatenate(dqs, axis=1) * HS**-0.5, here).astype(bf16)

    for i in range(count):
        pl.when(step == i)(functools.partial(run, i))

    @pl.when(step == count - 1)
    def _():
        for i in range(count):
            rows = slice(i * block, (i + 1) * block)
            dk_ref[rows, :] = turn_back(dk_sum[:, rows].T, rows).astype(bf16)
            dv_ref[rows, :] = dv_sum[:, rows].T.astype(bf16)


def attention_call(q, k, v, do, tables, block=512):
    g, width = q.shape
    seqs, count, pairs = g // LEN, LEN // block, width // 128
    one = pl.BlockSpec((block, 128), lambda s, h, i: (s * count + i, h))
    whole = pl.BlockSpec((LEN, 128), lambda s, h, i: (s, h))
    table = pl.BlockSpec((LEN, 128), lambda s, h, i: (0, 0))
    return pl.pallas_call(
        functools.partial(attention_kernel, block=block),
        grid=(seqs, pairs, count),
        in_specs=[one, whole, whole, one, table, table, table],
        out_specs=[one, one, whole, whole],
        out_shape=[shape(g, width, bf16)] * 4,
        scratch_shapes=[pltpu.VMEM((128, LEN), f32), pltpu.VMEM((128, LEN), f32)],
        compiler_params=params(),
    )(q, k, v, do, *tables)


def first(i):
    return pl.program_id(0) == 0 if i == 0 else pl.program_id(0) == pl.num_programs(0) - 1


def normal_of(x_ref, st_ref):
    return (x_ref[...].astype(f32) - st_ref[:, 0:1]) * st_ref[:, 1:2]


def project_back_kernel(shift, dq_ref, dk_ref, dv_ref, ctx_ref, n1_ref, x_ref, st_ref, g_ref, vec_ref, w_ref, s_ref, dw_ref, cols_ref, bias_ref, acc):
    @pl.when(first(0))
    def _():
        acc[...] = jnp.zeros_like(acc)
        cols_ref[...] = jnp.zeros_like(cols_ref)
        bias_ref[...] = jnp.zeros_like(bias_ref)

    n1 = n1_ref[...]
    width = dq_ref.shape[1]
    s = 0.0
    for part, ref in enumerate((dq_ref, dk_ref, dv_ref)):
        lanes = slice(part * width, (part + 1) * width)
        joined = ref[...]
        bias_ref[part : part + 1, :] += jnp.sum(joined.astype(f32), axis=0, keepdims=True)
        s = s + dot(joined, w_ref[:, lanes], 1, 1)
        acc[:, lanes] += dot(n1, joined, 0, 0)
    acc[:, 3 * width :] += dot(g_ref[...], ctx_ref[...], 0, 0)
    normal = normal_of(x_ref, st_ref)
    cols_ref[0:1, :] += jnp.sum(s * normal, axis=0, keepdims=True)
    cols_ref[1:2, :] += jnp.sum(s, axis=0, keepdims=True)
    s_ref[...] = s * vec_ref[0:1, :]

    @pl.when(first(1))
    def _():
        dw_ref[...] = acc[...].astype(bf16)


def project_back_call(shift, dq, dk, dv, ctx, n1, x, st, grads, vec, w1, rows=256):
    g, d = x.shape
    width = dq.shape[1]
    n = g // rows
    own = lambda c: pl.BlockSpec((rows, c), lambda i, s: (i, 0))
    seq = lambda c: pl.BlockSpec((rows, c), lambda i, s: ((i + s[0] // rows) % n, 0))
    return pl.pallas_call(
        project_back_kernel,
        grid_spec=pltpu.PrefetchScalarGridSpec(
            num_scalar_prefetch=1,
            grid=(n,),
            in_specs=[seq(width)] * 4 + [own(d), own(d), own(2), own(d), held(4, d), held(d, 3 * width)],
            out_specs=[own(d), held(d, 4 * width), held(2, d), held(3, width)],
            scratch_shapes=[pltpu.VMEM((d, 4 * width), f32)],
        ),
        out_shape=[shape(g, d, f32), shape(d, 4 * width, bf16), shape(2, d, f32), shape(3, width, f32)],
        compiler_params=params(),
    )(shift, dq, dk, dv, ctx, n1, x, st, grads, vec, w1)


def feed_forward_kernel(shift, n2_ref, g_ref, ctx_ref, we_ref, ws_ref, wd_ref, be_ref, gp_ref, br_ref, dw_ref, acc, *, chunk):
    @pl.when(first(0))
    def _():
        acc[...] = jnp.zeros_like(acc)

    n2, g = n2_ref[...], g_ref[...]
    branch = dot(ctx_ref[...], wd_ref[...], 1, 1)
    for c in range(we_ref.shape[1] // chunk):
        lanes = slice(c * chunk, (c + 1) * chunk)
        act, slope = gelu_parts(dot(n2, we_ref[:, lanes]) + be_ref[:, lanes])
        act = act.astype(bf16)
        gp_ref[:, lanes] = slope.astype(bf16)
        branch = branch + dot(act, ws_ref[:, lanes], 1, 1)
        acc[:, lanes] += dot(g, act, 0, 0)
    br_ref[...] = branch.astype(bf16)

    @pl.when(first(1))
    def _():
        dw_ref[...] = acc[...].astype(bf16)


def feed_forward_call(shift, n2, grads, ctx, w2, w1, be, rows=512):
    g, d = n2.shape
    hidden, width = w2.shape[1] // 2, ctx.shape[1]
    n = g // rows
    own = lambda c: pl.BlockSpec((rows, c), lambda i, s: (i, 0))
    seq = lambda c: pl.BlockSpec((rows, c), lambda i, s: ((i + s[0] // rows) % n, 0))
    return pl.pallas_call(
        functools.partial(feed_forward_kernel, chunk=min(hidden, 2048)),
        grid_spec=pltpu.PrefetchScalarGridSpec(
            num_scalar_prefetch=1,
            grid=(n,),
            in_specs=[own(d), own(d), seq(width), held(d, hidden, 0), held(d, hidden, 1), held(d, width, 3), held(1, hidden)],
            out_specs=[own(hidden), own(d), held(d, hidden)],
            scratch_shapes=[pltpu.VMEM((d, hidden), f32)],
        ),
        out_shape=[shape(g, hidden, bf16), shape(g, d, bf16), shape(d, hidden, bf16)],
        compiler_params=params(),
    )(shift, n2, grads, ctx, w2, w2, w1, be)


def feed_back_kernel(n2_ref, g_ref, gp_ref, s1_ref, x_ref, st_ref, vec_ref, we_ref, ws_ref, s_ref, dw_ref, cols_ref, bias_ref, acc, *, chunk):
    @pl.when(first(0))
    def _():
        acc[...] = jnp.zeros_like(acc)
        cols_ref[...] = jnp.zeros_like(cols_ref)
        bias_ref[...] = jnp.zeros_like(bias_ref)

    n2, g = n2_ref[...], g_ref[...]
    s = 0.0
    for c in range(we_ref.shape[1] // chunk):
        lanes = slice(c * chunk, (c + 1) * chunk)
        pre_grad = (dot(g, ws_ref[:, lanes]) * gp_ref[:, lanes].astype(f32)).astype(bf16)
        bias_ref[:, lanes] += jnp.sum(pre_grad.astype(f32), axis=0, keepdims=True)
        s = s + dot(pre_grad, we_ref[:, lanes], 1, 1)
        acc[:, lanes] += dot(n2, pre_grad, 0, 0)
    normal = normal_of(x_ref, st_ref)
    cols_ref[0:1, :] += jnp.sum(s * normal, axis=0, keepdims=True)
    cols_ref[1:2, :] += jnp.sum(s, axis=0, keepdims=True)
    s_ref[...] = (s1_ref[...] + s * vec_ref[2:3, :]).astype(bf16)

    @pl.when(first(1))
    def _():
        dw_ref[...] = acc[...].astype(bf16)


def feed_back_call(n2, grads, gp, s1, x, st, vec, w2, rows=256):
    g, d = n2.shape
    hidden = gp.shape[1]
    own = lambda c: pl.BlockSpec((rows, c), lambda i: (i, 0))
    return pl.pallas_call(
        functools.partial(feed_back_kernel, chunk=min(hidden, 1024)),
        grid=(g // rows,),
        in_specs=[own(d), own(d), own(hidden), own(d), own(d), own(2), held(4, d), held(d, hidden, 0), held(d, hidden, 1)],
        out_specs=[own(d), held(d, hidden), held(2, d), held(1, hidden)],
        out_shape=[shape(g, d, bf16), shape(d, hidden, bf16), shape(2, d, f32), shape(1, hidden, f32)],
        scratch_shapes=[pltpu.VMEM((d, hidden), f32)],
        compiler_params=params(),
    )(n2, grads, gp, s1, x, st, vec, w2, w2)


def rotary_tables():
    half = ROT // 2
    position = jnp.arange(LEN).astype(f32)
    inverse = 10000.0 ** (-(jnp.arange(half).astype(f32) * 2.0) / ROT)
    angle = position[:, None] * inverse[None, :]
    cos, sin = jnp.cos(angle), jnp.sin(angle)
    rest = jnp.zeros((LEN, HS - ROT), f32)
    none = jnp.zeros((LEN, half), f32)
    pair = lambda *a: jnp.tile(jnp.concatenate(a, axis=1), (1, 128 // HS))
    return pair(cos, cos, rest + 1.0), pair(-sin, none, rest), pair(none, sin, rest)


def make_body(tp):
    def swap(a):
        return lax.ppermute(a, "tp", [(0, 1), (1, 0)])

    def body(inputs, cotangent, first_gain, first_shift, second_gain, second_shift, project_weight, project_bias, dense_weight, dense_bias, expand_weight, expand_bias, shrink_weight, shrink_bias):
        rows, d = inputs.shape
        width = dense_weight.shape[0]
        hidden = shrink_weight.shape[0]
        part = project_weight.shape[0]
        me = lax.axis_index("tp")
        if tp == 2:
            shift = (me * rows).astype(jnp.int32)[None]
            gather_rows = lambda a: jnp.concatenate([a, swap(a)], axis=0)
            scatter_rows = lambda a: a[:rows].astype(f32) + swap(a[rows:]).astype(f32)
        else:
            shift = jnp.zeros((1,), jnp.int32)
            gather_rows = lambda a: lax.all_gather(a, "tp", axis=0, tiled=True)
            scatter_rows = lambda a: lax.psum_scatter(a, "tp", scatter_dimension=0, tiled=True).astype(f32)
        shard1 = jnp.concatenate([project_weight.reshape(part, 3 * width), dense_weight.T], axis=1)
        shard2 = jnp.concatenate([expand_weight, shrink_weight.T], axis=1)
        w1 = lax.all_gather(shard1, "fsdp", axis=0, tiled=True)
        x = gather_rows(inputs)
        w2 = lax.all_gather(shard2, "fsdp", axis=0, tiled=True)
        grads = gather_rows(cotangent)
        vec = jnp.stack([first_gain, first_shift, second_gain, second_shift])
        tables = rotary_tables()
        n1, n2, st, q, k, v = qkv_call(shift, x, vec, w1, project_bias, tables, width)
        do = context_grad_call(shift, grads, w1, width)
        ctx, dq, dk, dv = attention_call(q, k, v, do, tables)
        s1, dw1, cols1, bias1 = project_back_call(shift, dq, dk, dv, ctx, n1, x, st, grads, vec, w1)
        dw1 = lax.psum_scatter(dw1, "fsdp", scatter_dimension=0, tiled=True).astype(f32)
        gp, branch, dws = feed_forward_call(shift, n2, grads, ctx, w2, w1, expand_bias[None])
        branch = scatter_rows(branch)
        s, dwe, cols2, bias2 = feed_back_call(n2, grads, gp, s1, x, st, vec, w2)
        s = scatter_rows(s)
        dw2 = lax.psum_scatter(jnp.concatenate([dwe, dws], axis=1), "fsdp", scatter_dimension=0, tiled=True).astype(f32)
        own_rows, own_grads = inputs.astype(f32), cotangent.astype(f32)
        output = (own_rows + branch + dense_bias + shrink_bias).astype(bf16)
        own_st = st[:rows] if tp == 2 else lax.dynamic_slice_in_dim(st, me * rows, rows, 0)
        normal = (own_rows - own_st[:, 0:1]) * own_st[:, 1:2]
        term = own_st[:, 1:2] * (s - jnp.mean(s, axis=1, keepdims=True) - normal * jnp.mean(s * normal, axis=1, keepdims=True))
        input_grad = own_grads + term
        local = jnp.concatenate([bias1.reshape(-1), bias2.reshape(-1)])
        slots = lax.dynamic_update_slice_in_dim(jnp.zeros((tp, local.shape[0]), f32), local[None], me, 0)
        small = jnp.concatenate([cols1.reshape(-1), cols2.reshape(-1), jnp.sum(own_grads, axis=0), slots.reshape(-1)])
        small = lax.psum(small, ("fsdp", "tp"))
        cols = small[: 5 * d].reshape(5, d)
        local = lax.dynamic_slice_in_dim(small[5 * d :].reshape(tp, -1), me, 1, 0)[0]
        return (
            output,
            input_grad,
            cols[0],
            cols[1],
            cols[2],
            cols[3],
            dw1[:, : 3 * width].reshape(part, 3, width),
            local[: 3 * width].reshape(3, width),
            dw1[:, 3 * width :].T,
            cols[4],
            dw2[:, :hidden],
            local[3 * width :],
            dw2[:, hidden:].T,
            cols[4],
        )

    return body


def solution(mesh):
    rows, rep = P(("fsdp", "tp"), None), P()
    return jax.shard_map(
        make_body(mesh.shape["tp"]),
        mesh=mesh,
        in_specs=(rows, rows, rep, rep, rep, rep, P("fsdp", None, "tp"), P(None, "tp"), P("tp", "fsdp"), rep, P("fsdp", "tp"), P("tp"), P("tp", "fsdp"), rep),
        out_specs=(rows, rows, rep, rep, rep, rep, P("fsdp", None, "tp"), P(None, "tp"), P("tp", "fsdp"), rep, P("fsdp", "tp"), P("tp"), P("tp", "fsdp"), rep),
        check_vma=False,
    )
```

time: 1670 us -> 497 us (0.30)
  matrix products: 621 us -> 0 us
  waiting for transfers between devices: 573 us -> 157 us
  Pallas kernels: 0 us -> 220 us
  other arithmetic: 206 us -> 25.1 us
  local copies, waits for them, and re-layouts: 138 us -> 30.4 us
  blocking collectives: 101 us -> 40.7 us
    dot_general x40 -> x0, matrix products: 621 us -> none  [the longest x8 158 us: causal_scores(): jnp.einsum('qhd,khd->hqk', query_rows, key_rows, preferred_element_type=j...]
    reduce_scatter x7 -> x2, waiting for transfers between devices: 385 us -> 0.02 us  [the longest x1 0.02 us: body(): lax.psum_scatter(dw1, 'fsdp', scatter_dimension=0, tiled=True).astype(f32)]
    pallas_call x0 -> x6, Pallas kernels: none -> 220 us  [the longest x1 87.6 us: attention_call(): pl.pallas_call(functools.partial(attention_kernel, block=block), grid=(se...]
    all_gather x7 -> x2, waiting for transfers between devices: 183 us -> 0.02 us  [the longest x1 0.02 us: body(): w2 = lax.all_gather(shard2, 'fsdp', axis=0, tiled=True)]
    ppermute x0 -> x4, waiting for transfers between devices: none -> 156 us  [swap(): return lax.ppermute(a, 'tp', [(0, 1), (1, 0)])]
    convert_element_type x6 -> x3, other arithmetic: 112 us -> 2.13 us  [the longest x1 1.11 us: body(): lax.psum_scatter(jnp.concatenate([dwe, dws], axis=1), 'fsdp', scatter_dim...]
    dynamic_update_slice x8 -> x1, local copies, waits for them, and re-layouts: 88.3 us -> 0.14 us  [body(): lax.dynamic_update_slice_in_dim(jnp.zeros((tp, local.shape[0]), f32), loc...]
    reduce_sum x9 -> x2, other arithmetic: 81.6 us -> 9.84 us  [the longest x1 6.54 us: body(): jnp.sum(own_grads, axis=0)]
  transfers between devices with their start and end apart: 14 -> 8, of which waited for: 9 -> 4; matrix products, arithmetic and copies ran while one was open for 58% -> 10% of each run, Pallas kernels for 0% -> 45%
where the time goes in v1:
time: 497 us; the launch traced here: 492 us
  Pallas kernels  220 us (44%)
  waiting for transfers between devices  157 us (32%)
  blocking collectives  40.7 us (8%)
  local copies, waits for them, and re-layouts  30.4 us (6%)
  other arithmetic  25.1 us (5%)
  between operations  14.3 us (3%)
  starting transfers between devices  5.33 us (1%)
    ppermute x4, waiting for transfers between devices, swap(): return lax.ppermute(a, 'tp', [(0, 1), (1, 0)])  156 us
    pallas_call x1, Pallas kernels, attention_call(): pl.pallas_call(functools.partial(attention_kernel, block=block), grid=(se...  87.6 us
    pallas_call x1, Pallas kernels, feed_forward_call(): pl.pallas_call(functools.partial(feed_forward_kernel, chunk=min(hidden, 2...  49.3 us
    psum x1, blocking collectives, body(): small = lax.psum(small, ('fsdp', 'tp'))  40.7 us
    pallas_call x1, Pallas kernels, feed_back_call(): pl.pallas_call(functools.partial(feed_back_kernel, chunk=min(hidden, 1024...  37.5 us
    pallas_call x1, Pallas kernels, project_back_call(): pl.pallas_call(project_back_kernel, grid_spec=pltpu.PrefetchScalarGridSpe...  24.1 us
    pallas_call x1, Pallas kernels, qkv_call(): pl.pallas_call(qkv_kernel, grid_spec=pltpu.PrefetchScalarGridSpec(num_sca...  15.5 us
  transfers between devices with their start and end apart: 8, of which 4 were waited for; matrix products, arithmetic and copies ran while one was open for 10% of the time, Pallas kernels for 45%

profile of v1, /device:TPU:0, one launch (start us, length us, event | category | flops | bytes accessed | tf_op | source)
XLA Modules:
  0.0 492.5 jit_solution(11113949017229973154)
XLA Ops:
  7.2 0.0 all-gather.3.cloned.1.call-start
  7.2 0.9 copy.39
  8.2 1.6 pad_maximum_fusion.2
  9.7 0.0 all-gather.3.cloned.1.call-update
  9.8 0.0 all-gather.5.cloned.1.call-start
  9.8 1.9 pad_maximum_fusion.1
  11.7 0.0 all-gather.5.cloned.1.call-update
  11.7 0.0 reduce-scatter.3.cloned.1.call-start
  11.7 3.1 collective-permute-start.1
  14.8 0.1 collective-permute-start
  14.9 0.1 pad.18.clone
  15.0 0.1 pad.15.clone
  15.1 0.3 multiply_sine_fusion
  15.4 0.9 maximum_maximum_fusion.2
  16.3 0.1 tile.31
  16.4 1.4 copy.33.sb_ref
  17.8 0.1 tile.14
  17.9 1.3 copy.32.sa_ref
  19.2 1.3 tile.12
  20.5 1.3 copy.31.c_ref
  21.8 0.6 pad_maximum_fusion.4.vec_ref
  22.4 3.1 constant_dynamic-update-slice_fusion.3
  25.5 1.5 constant_dynamic-update-slice_fusion.1
  27.0 34.6 %collective-permute-done.1 = bf16[1024,1024]{1,0:T(8,128)(2,1)} collective-permute-done((bf16[1024,1024]{1,0:T(8,128)(2,1)}, bf16[1024,1024]{1,0:T(8,128)(2,1)}, u32[]{:S(2)}, u32[]{:S(2)}) %collective-permute-start.1) | collective-permute-done | bytes 2097184 | tf_op jit(solution)/shard_map/ppermute | solution.py:349
  61.6 3.2 constant_dynamic-update-slice_fusion.2.g_ref
  64.8 40.9 %collective-permute-done = bf16[1024,1024]{1,0:T(8,128)(2,1)} collective-permute-done((bf16[1024,1024]{1,0:T(8,128)(2,1)}, bf16[1024,1024]{1,0:T(8,128)(2,1)}, u32[]{:S(2)}, u32[]{:S(2)}) %collective-permute-start) | collective-permute-done | bytes 2097184 | tf_op jit(solution)/shard_map/ppermute | solution.py:349
  105.7 3.1 constant_dynamic-update-slice_fusion.x_ref
  108.8 6.1 %shard_map.246.do_ref = bf16[2048,512]{1,0:T(8,128)(2,1)} custom-call(s32[1]{0:T(128)} %bitcast.shift, bf16[2048,1024]{1,0:T(8,128)(2,1)} %constant_dynamic-update-slice_fusion.2.g_ref, bf16[1024,2048]{1,0:T(8,128)(2,1)} %all-gather.3.cloned.1.call-done.w_ref.wd_ref), custom_call_target="tpu_custom_call" | custom-call | tf_op jit(solution)/shard_map/pallas_call | solution.py:111
  114.8 15.5 %shard_map.245 = (bf16[2048,1024]{1,0:T(8,128)(2,1)}, bf16[2048,1024]{1,0:T(8,128)(2,1)}, f32[2048,2]{1,0:T(8,128)}, bf16[2048,512]{1,0:T(8,128)(2,1)}, bf16[204...) custom-call(s32[1]{0:T(128)} %bitcast.shift, bf16[2048,1024]{1,0:T(8,128)(2,1)} %constant_dynamic-update-slice_fusion.x_ref, ...), custom_call_target="tpu_custom_call" | custom-call | tf_op jit(solution)/shard_map/pallas_call | solution.py:91
  130.3 87.6 %shard_map.247 = (bf16[2048,512]{1,0:T(8,128)(2,1)}, bf16[2048,512]{1,0:T(8,128)(2,1)}, bf16[2048,512]{1,0:T(8,128)(2,1)}, bf16[2048,512]{1,0:T(8,128)(2,1)}) custom-call(bf16[2048,512]{1,0:T(8,128)(2,1)} %get-tuple-element.36.q_ref, bf16[2048,512]{1,0:T(8,128)(2,1)} %get-tuple-element.37.k_ref, bf16[2048,512]{1,0:T(8,128)(2,1)} %get-tuple-element.38.v_ref, ...), custom_call_target="tpu_custom_call" | custom-call | tf_op jit(solution)/shard_map/pallas_call | solution.py:188
  217.9 24.1 %shard_map.249 = (f32[2048,1024]{1,0:T(8,128)}, bf16[1024,2048]{1,0:T(8,128)(2,1)}, f32[2,1024]{1,0:T(2,128)}, f32[3,512]{1,0:T(4,128)}) custom-call(s32[1]{0:T(128)} %bitcast.shift, bf16[2048,512]{1,0:T(8,128)(2,1)} %get-tuple-element.43.dq_ref, bf16[2048,512]{1,0:T(8,128)(2,1)} %get-tuple-element.44.dk_ref, bf16[2048,512]{1,0:T(8,128)(2,1)} %get-tuple-element.45.dv_ref, ...), custom_call_target="tpu_custom_call" | custom-call | tf_op jit(solution)/shard_map/pallas_call | solution.py:240
  242.1 0.0 reduce-scatter.3.cloned.1.call-update
  242.1 0.0 reduce-scatter.5.cloned.1.call-start
  242.1 0.0 all-gather.5.cloned.1.call-done.we_ref.ws_ref
  242.2 49.3 %shard_map.248 = (bf16[2048,2048]{1,0:T(8,128)(2,1)}, bf16[2048,1024]{1,0:T(8,128)(2,1)}, bf16[1024,2048]{1,0:T(8,128)(2,1)}) custom-call(s32[1]{0:T(128)} %bitcast.shift, bf16[2048,1024]{1,0:T(8,128)(2,1)} %get-tuple-element.35.n2_ref, bf16[2048,1024]{1,0:T(8,128)(2,1)} %constant_dynamic-update-slice_fusion.2.g_ref, ...), custom_call_target="tpu_custom_call" | custom-call | tf_op jit(solution)/shard_map/pallas_call | solution.py:281
  291.5 37.5 %shard_map.250 = (bf16[2048,1024]{1,0:T(8,128)(2,1)}, bf16[1024,2048]{1,0:T(8,128)(2,1)}, f32[2,1024]{1,0:T(2,128)}, f32[1,2048]{1,0:T(1,128)}) custom-call(bf16[2048,1024]{1,0:T(8,128)(2,1)} %get-tuple-element.35.n2_ref, bf16[2048,1024]{1,0:T(8,128)(2,1)} %constant_dynamic-update-slice_fusion.2.g_ref, bf16[2048,2048]{1,0:T(8,128)(2,1)} %get-tuple-element.42.gp_ref, ...), custom_call_target="tpu_custom_call" | custom-call | tf_op jit(solution)/shard_map/pallas_call | solution.py:324
  329.0 7.8 %pad_maximum_fusion = bf16[1024,4096]{1,0:T(8,128)(2,1)} fusion(bf16[1024,2048]{1,0:T(8,128)(2,1)} %get-tuple-element.55, bf16[1024,2048]{1,0:T(8,128)(2,1)} %get-tuple-element.54), kind=kLoop, calls=%fused_computation | loop fusion | flops 16777216 | bytes 16777216 | tf_op jit(solution)/shard_map/concatenate | solution.py:382
  336.8 0.0 reduce-scatter.5.cloned.1.call-update
  336.8 0.0 copy-start.7
  336.9 0.0 copy-start.6
  336.9 3.2 slice.78
  340.1 1.6 collective-permute-start.3
  341.8 1.5 slice.75
  343.3 0.4 collective-permute-start.2
  343.7 0.5 slice_reduce_fusion.1
  344.2 0.0 reduce-scatter.3.cloned.1.call-done
  344.2 1.0 slice.97
  345.2 0.0 copy-start.14
  345.2 0.8 copy.45
  346.0 1.0 convert_element_type.62
  347.0 0.7 slice_bitcast_fusion.1
  347.7 0.1 dynamic_update_slice.3
  347.9 41.0 %collective-permute-done.3 = bf16[1024,1024]{1,0:T(8,128)(2,1)} collective-permute-done((bf16[1024,1024]{1,0:T(8,128)(2,1)}, bf16[1024,1024]{1,0:T(8,128)(2,1)}, u32[]{:S(2)}, u32[]{:S(2)}) %collective-permute-start.3) | collective-permute-done | bytes 2097184 | tf_op jit(solution)/shard_map/ppermute | solution.py:349
  388.9 3.3 fusion.9
  392.3 39.9 %collective-permute-done.2 = bf16[1024,1024]{1,0:T(8,128)(2,1)} collective-permute-done((bf16[1024,1024]{1,0:T(8,128)(2,1)}, bf16[1024,1024]{1,0:T(8,128)(2,1)}, u32[]{:S(2)}, u32[]{:S(2)}) %collective-permute-start.2) | collective-permute-done | bytes 2097184 | tf_op jit(solution)/shard_map/ppermute | solution.py:349
  432.2 6.5 %convert_reduce_fusion = (f32[1024]{0:T(1024)S(1)}, f32[1024,1024]{1,0:T(8,128)}, bf16[1024,1024]{1,0:T(8,128)(2,1)}) fusion(bf16[1024,1024]{1,0:T(8,128)(2,1)S(1)} %copy-done.3, f32[1024]{0:T(1024)S(1)} %broadcast_multiply_fusion, f32[1024]{0:T(1024)S(1)} %get-tuple-element.87, bf16[1024,1024]{1,0:T(8,128)(2,1)S(1)} %copy-done, ...), kind=kLoop, calls=%fused_computation.1 | loop fusion | flops 20970496 | bytes 18903040 | tf_op jit(solution)/shard_map/reduce_sum | solution.py:391
  438.7 40.7 %psum.7 = f32[12288]{0:T(1024)S(1)} all-reduce(f32[12288]{0:T(1024)S(1)} %pad_maximum_fusion.3), channel_id=1, replica_groups=mesh['fsdp'=16,'tp'=2] {'fsdp','tp'}, use_global_device_ids=true, to_apply=%region_3.0 | all-reduce | flops 12288 | bytes 98304 | tf_op jit(solution)/shard_map/psum | solution.py:392
  479.5 0.6 fusion.11
  480.1 0.7 dynamic-slice.1
  480.8 0.6 reshape.111
  481.4 1.1 convert_element_type.63
  482.5 0.8 slice_bitcast_fusion
  483.4 1.8 slice.101
  485.1 0.6 copy.52
  (49 shorter events, 0.2 us)
Async XLA Ops:
  7.2 101.6 %all-gather.3.cloned.1.call-start = ((), (), s32[]{:S(2)}) async-start(), calls=%async_computation.2 | async-start | bytes 4456448 | tf_op jit(solution)/shard_map/all_gather | solution.py:367
  9.8 232.4 %all-gather.5.cloned.1.call-start = ((), (), s32[]{:S(2)}) async-start(), calls=%async_computation.3 | async-start | bytes 8912896 | tf_op jit(solution)/shard_map/all_gather | solution.py:369
  11.7 332.5 %reduce-scatter.3.cloned.1.call-start = ((), (), s32[]{:S(2)}) async-start(), calls=%async_computation.4 | async-start | bytes 4456448 | tf_op jit(solution)/shard_map/reduce_scatter | solution.py:377
  11.7 49.9 %collective-permute-start.1 = (bf16[1024,1024]{1,0:T(8,128)(2,1)}, bf16[1024,1024]{1,0:T(8,128)(2,1)}, u32[]{:S(2)}, u32[]{:S(2)}) collective-permute-start(bf16[1024,1024]{1,0:T(8,128)(2,1)} %param.15), channel_id=1, source_target_pairs={{0,1},{1,0},{2,3},{3,2},{4,5},{5,4},{6,7},{7,6},{8,9},{9,8},{10,11... | collective-permute-start | bytes 6291464 | tf_op jit(solution)/shard_map/ppermute | solution.py:349
  14.8 90.9 %collective-permute-start = (bf16[1024,1024]{1,0:T(8,128)(2,1)}, bf16[1024,1024]{1,0:T(8,128)(2,1)}, u32[]{:S(2)}, u32[]{:S(2)}) collective-permute-start(bf16[1024,1024]{1,0:T(8,128)(2,1)} %param.14), channel_id=1, source_target_pairs={{0,1},{1,0},{2,3},{3,2},{4,5},{5,4},{6,7},{7,6},{8,9},{9,8},{10,11... | collective-permute-start | bytes 6291464 | tf_op jit(solution)/shard_map/ppermute | solution.py:349
  17.8 4.0 copy-start.10
  17.8 4.0 copy-start.11
  17.8 4.0 copy-start.12
  17.8 4.0 copy-start.13
  19.2 6.3 %copy-start = (bf16[1024,1024]{1,0:T(8,128)(2,1)S(1)}, bf16[1024,1024]{1,0:T(8,128)(2,1)}, u32[]{:S(2)}) copy-start(bf16[1024,1024]{1,0:T(8,128)(2,1)} %param.14) | copy-start | bytes 6291460
  242.1 239.3 %reduce-scatter.5.cloned.1.call-start = ((), (), s32[]{:S(2)}) async-start(), calls=%async_computation.5 | async-start | bytes 8912896 | tf_op jit(solution)/shard_map/reduce_scatter | solution.py:382
  336.8 4.9 %copy-start.4 = (bf16[2048,1024]{1,0:T(8,128)(2,1)S(1)}, bf16[2048,1024]{1,0:T(8,128)(2,1)}, u32[]{:S(2)}) copy-start(bf16[2048,1024]{1,0:T(8,128)(2,1)} %get-tuple-element.40) | copy-start | bytes 12582916
  336.8 6.8 %copy-start.7 = (f32[2,1024]{1,0:T(2,128)S(1)}, f32[2,1024]{1,0:T(2,128)}, u32[]{:S(2)}) copy-start(f32[2,1024]{1,0:T(2,128)} %get-tuple-element.49) | copy-start | bytes 24580
  336.9 6.8 %copy-start.6 = (f32[3,512]{1,0:T(4,128)S(1)}, f32[3,512]{1,0:T(4,128)}, u32[]{:S(2)}) copy-start(f32[3,512]{1,0:T(4,128)} %get-tuple-element.51) | copy-start | bytes 18436
  336.9 6.8 %copy-start.1 = (f32[2048,2]{1,0:T(8,128)S(1)}, f32[2048,2]{1,0:T(8,128)}, u32[]{:S(2)}) copy-start(f32[2048,2]{1,0:T(8,128)} %get-tuple-element.41.st_ref) | copy-start | bytes 49156
  340.1 7.5 %copy-start.8 = (f32[2,1024]{1,0:T(2,128)S(1)}, f32[2,1024]{1,0:T(2,128)}, u32[]{:S(2)}) copy-start(f32[2,1024]{1,0:T(2,128)} %get-tuple-element.50) | copy-start | bytes 24580
  340.1 7.5 %copy-start.9 = (f32[1,2048]{1,0:T(1,128)S(1)}, f32[1,2048]{1,0:T(1,128)}, u32[]{:S(2)}) copy-start(f32[1,2048]{1,0:T(1,128)} %get-tuple-element.52) | copy-start | bytes 24580
  340.1 48.8 %collective-permute-start.3 = (bf16[1024,1024]{1,0:T(8,128)(2,1)}, bf16[1024,1024]{1,0:T(8,128)(2,1)}, u32[]{:S(2)}, u32[]{:S(2)}) collective-permute-start(bf16[1024,1024]{1,0:T(8,128)(2,1)} %slice.78), channel_id=1, source_target_pairs={{0,1},{1,0},{2,3},{3,2},{4,5},{5,4},{6,7},{7,6},{8,9},{9,8},{10,11... | collective-permute-start | bytes 6291464 | tf_op jit(solution)/shard_map/ppermute | solution.py:349
  343.3 88.9 %collective-permute-start.2 = (bf16[1024,1024]{1,0:T(8,128)(2,1)}, bf16[1024,1024]{1,0:T(8,128)(2,1)}, u32[]{:S(2)}, u32[]{:S(2)}) collective-permute-start(bf16[1024,1024]{1,0:T(8,128)(2,1)} %slice.75), channel_id=1, source_target_pairs={{0,1},{1,0},{2,3},{3,2},{4,5},{5,4},{6,7},{7,6},{8,9},{9,8},{10,11... | collective-permute-start | bytes 6291464 | tf_op jit(solution)/shard_map/ppermute | solution.py:349
  345.2 87.0 %copy-start.14 = (f32[1024]{0:T(1024)S(1)}, f32[1024]{0:T(1024)}, u32[]{:S(2)}) copy-start(f32[1024]{0:T(1024)} %param.27) | copy-start | bytes 12292
  345.2 87.0 %copy-start.15 = (f32[1024]{0:T(1024)S(1)}, f32[1024]{0:T(1024)}, u32[]{:S(2)}) copy-start(f32[1024]{0:T(1024)} %param.23) | copy-start | bytes 12292
  347.9 84.3 %copy-start.2 = (bf16[2048,1024]{1,0:T(8,128)(2,1)S(1)}, bf16[2048,1024]{1,0:T(8,128)(2,1)}, u32[]{:S(2)}) copy-start(bf16[2048,1024]{1,0:T(8,128)(2,1)} %get-tuple-element.48) | copy-start | bytes 12582916
  347.9 84.3 %copy-start.3 = (bf16[1024,1024]{1,0:T(8,128)(2,1)S(1)}, bf16[1024,1024]{1,0:T(8,128)(2,1)}, u32[]{:S(2)}) copy-start(bf16[1024,1024]{1,0:T(8,128)(2,1)} %param.15) | copy-start | bytes 6291460
  480.1 5.6 %copy-start.5 = (f32[1024]{0:T(1024)}, f32[1024]{0:T(1024)S(1)}, u32[]{:S(2)}) copy-start(f32[1024]{0:T(1024)S(1)} %get-tuple-element.129) | copy-start | bytes 12292
Sparse Core Ops, SparseCore 0:
  10.7 53.0 all-gather.2
  66.6 72.8 all-gather.4
  242.2 74.1 reduce-scatter.2
  337.0 104.8 reduce-scatter.4

commit v2 on v1

v2 whole, which is shorter than its diff:
```python
import functools

import jax
import jax.numpy as jnp
from jax import lax
from jax.experimental import pallas as pl
from jax.experimental.pallas import tpu as pltpu
from jax.sharding import PartitionSpec as P

f32, bf16 = jnp.float32, jnp.bfloat16
HS = 64
ROT = 16
LEN = 2048
EPS = 1e-05
NEG = -1e30
VMEM_LIMIT = 60 << 20
PIECES = 2
ERFC = (
    0.22567586308569043,
    0.22566953354787173,
    0.20784372127485384,
    0.1685348386069925,
    0.14145750936579315,
    -0.005660950942278366,
    0.16914715407444447,
    -0.18293900460081808,
    0.050271460956987875,
)


def dot(a, b, ca=1, cb=0):
    return lax.dot_general(a, b, (((ca,), (cb,)), ((), ())), preferred_element_type=f32)


def gelu_parts(x):
    t = pl.reciprocal(1.0 + (0.4 * 0.5**0.5) * jnp.abs(x))
    poly = jnp.full_like(t, ERFC[-1])
    for c in ERFC[-2::-1]:
        poly = poly * t + c
    e = jnp.exp(-0.5 * (x * x))
    tail = (0.5 * t) * poly * e
    cdf = jnp.where(x < 0, tail, 1.0 - tail)
    return x * cdf, cdf + x * (e * 0.3989422804014327)


def call(kernel, grid, in_specs, out_specs, out_shape, scratch, flops, scalars=1, collective=None):
    size = lambda a: a.dtype.itemsize * a.size
    return lambda *args: pl.pallas_call(
        kernel,
        grid_spec=pltpu.PrefetchScalarGridSpec(num_scalar_prefetch=scalars, grid=grid, in_specs=in_specs, out_specs=out_specs, scratch_shapes=scratch),
        out_shape=out_shape,
        compiler_params=pltpu.CompilerParams(vmem_limit_bytes=VMEM_LIMIT, collective_id=collective, has_side_effects=collective is not None),
        cost_estimate=pl.CostEstimate(flops=int(flops), transcendentals=0, bytes_accessed=sum(map(size, args)) + sum(map(size, out_shape))),
    )(*args)


def held(rows, cols, col_block=0):
    return pl.BlockSpec((rows, cols), lambda *i: (0, col_block), pipeline_mode=pl.Buffered(1))


def shape(rows, cols, dtype):
    return jax.ShapeDtypeStruct((rows, cols), dtype)


def both(rows, cols, count):
    return [
        pl.BlockSpec((rows, cols), lambda i, *s: (jnp.minimum(i, count - 1), 0)),
        pl.BlockSpec((rows, cols), lambda i, *s: (jnp.maximum(i - count, 0), 0)),
    ]


def own_order(rows, cols):
    return pl.BlockSpec((rows, cols), lambda i, *s: (i, 0))


def seq_order(rows, cols, n):
    return pl.BlockSpec((rows, cols), lambda i, shift, *s: ((i + shift[0] // rows) % n, 0))


def pick(refs, count):
    return jnp.where(pl.program_id(0) < count, refs[0][...], refs[1][...])


def put(refs, count, value):
    for ref, here in zip(refs, (pl.program_id(0) < count, pl.program_id(0) >= count)):

        @pl.when(here)
        def _():
            ref[...] = value


def at_first():
    return pl.when(pl.program_id(0) == 0)


def at_last():
    return pl.when(pl.program_id(0) == pl.num_programs(0) - 1)


def block_order(j):
    f = lax.axis_index("fsdp")
    z, x, core = lax.div(f, 4), lax.rem(lax.div(f, 2), 2), lax.rem(f, 2)
    other_core, other_x, k = 1 - j // 8, 1 - j // 4 % 2, j % 4
    x = 1 - x if other_x else x
    core = 1 - core if other_core else core
    return lax.rem(z + k, 4) * 4 + x * 2 + core


def put_blocks(fsdp, refs, acc):
    size, wide = acc.shape[0] // fsdp, acc.shape[1] // PIECES
    for j in range(fsdp):
        rows = pl.ds(pl.multiple_of(block_order(j) * size, size), size) if fsdp == 16 else slice(j * size, (j + 1) * size)
        at = j % (fsdp // 2) * size
        for p in range(PIECES):
            refs[j // (fsdp // 2)][p, at : at + size, :] = acc[rows, p * wide : (p + 1) * wide].astype(bf16)


def pieces(d, cols):
    dims = (PIECES, d // 2, cols // PIECES)
    return pl.BlockSpec(dims, lambda *i: (0, 0, 0), pipeline_mode=pl.Buffered(1)), jax.ShapeDtypeStruct(dims, bf16)


def neighbours():
    f, t = lax.axis_index("fsdp"), lax.axis_index("tp")
    core, x = lax.rem(f, 2), lax.rem(lax.div(f, 2), 2)
    around = [(lax.rem(f + 4 * k, 16), t) for k in range(1, 4)]
    return {"core": (f + 1 - 2 * core, t), "x": (f + 2 - 4 * x, t), "y": (f, 1 - t), "z": around}


def greet(to):
    barrier = pltpu.get_barrier_semaphore()
    peers = [to["core"], to["x"], to["y"], *to["z"]]
    for peer in peers:
        pl.semaphore_signal(barrier, inc=1, device_id=peer, device_id_type=pl.DeviceIdType.MESH)
    pl.semaphore_wait(barrier, len(peers))


def remote(src, dst, sems, at, peer):
    return pltpu.make_async_remote_copy(
        src_ref=src, dst_ref=dst, send_sem=sems[0].at[at], recv_sem=sems[1].at[at], device_id=peer, device_id_type=pl.DeviceIdType.MESH
    )


def sem_pair(count):
    return [pltpu.SemaphoreType.DMA((count,)), pltpu.SemaphoreType.DMA((count,))]


class Reduce:
    def __init__(self, send, keep, out, scratch, to):
        self.send, self.keep, self.out, self.to = send, keep, out, to
        self.got, self.send2, self.got2, self.send3, self.got3, *sems = scratch
        self.sems = [sems[0:2], sems[2:4], sems[4:6]]

    @staticmethod
    def scratch(d, cols):
        rows, wide = d // 16, cols // PIECES
        buffer = lambda n: pltpu.VMEM((PIECES, n * rows, wide), bf16)
        return [buffer(8), buffer(4), buffer(4), buffer(3), buffer(3)] + sem_pair(PIECES) + sem_pair(PIECES) + sem_pair(3 * PIECES)

    def copy1(self, p):
        return remote(self.send.at[p], self.got.at[p], self.sems[0], p, self.to["core"])

    def copy2(self, p):
        return remote(self.send2.at[p], self.got2.at[p], self.sems[1], p, self.to["x"])

    def copies3(self, p):
        rows = self.out.shape[0]
        cut = lambda ref, k: ref.at[p, k * rows : (k + 1) * rows]
        return [remote(cut(self.send3, k), cut(self.got3, k), self.sems[2], 3 * p + k, self.to["z"][k]) for k in range(3)]

    def begin(self, p):
        self.copy1(p).start()

    def across_x(self, p):
        self.copy1(p).wait()
        rows = slice(0, self.send2.shape[1])
        self.send2[p] = (self.keep[p, rows].astype(f32) + self.got[p, rows].astype(f32)).astype(bf16)
        self.copy2(p).start()

    def along_z(self, p):
        self.copy2(p).wait()
        rows, wide = self.out.shape[0], self.send2.shape[2]
        half = 4 * rows
        for k in (1, 2, 3, 0):
            here = slice(half + k * rows, half + (k + 1) * rows)
            total = self.keep[p, here].astype(f32) + self.got[p, here].astype(f32) + self.got2[p, k * rows : (k + 1) * rows].astype(f32)
            if k:
                self.send3[p, (k - 1) * rows : k * rows] = total.astype(bf16)
            else:
                self.out[:, p * wide : (p + 1) * wide] = total
        for copy in self.copies3(p):
            copy.start()

    def end(self, p):
        rows, wide = self.out.shape[0], self.send2.shape[2]
        for copy in self.copies3(p):
            copy.wait()
        got = [self.got3[p, k * rows : (k + 1) * rows].astype(f32) for k in range(3)]
        self.out[:, p * wide : (p + 1) * wide] += got[0] + got[1] + got[2]


def at_step(i):
    return pl.when(pl.program_id(0) == i)


def turn(y, cos, sin_up, sin_down):
    width = y.shape[1]
    half = ROT // 2
    return y * cos + pltpu.roll(y, width - half, 1) * sin_up + pltpu.roll(y, half, 1) * sin_down


def qkv_kernel(shift, x_ref, y_ref, vec_ref, w_ref, b_ref, c_ref, sa_ref, sb_ref, n1_ref, n2_ref, st_ref, q_ref, k_ref, v_ref, *, count):
    x = pick((x_ref, y_ref), count).astype(f32)
    mean = jnp.mean(x, axis=1, keepdims=True)
    centred = x - mean
    rstd = lax.rsqrt(jnp.mean(centred * centred, axis=1, keepdims=True) + EPS)
    normal = centred * rstd
    st_ref[:, 0:1] = mean
    st_ref[:, 1:2] = rstd
    n1 = (normal * vec_ref[0:1, :] + vec_ref[1:2, :]).astype(bf16)
    n1_ref[...] = n1
    n2_ref[...] = (normal * vec_ref[2:3, :] + vec_ref[3:4, :]).astype(bf16)
    width = q_ref.shape[1]
    tables = [jnp.concatenate([r[...]] * (width // 128), axis=1) for r in (c_ref, sa_ref, sb_ref)]
    for part, ref in enumerate((q_ref, k_ref, v_ref)):
        y = dot(n1, w_ref[:, part * width : (part + 1) * width]) + b_ref[part : part + 1, :]
        if part < 2:
            y = turn(y, *tables)
        if part == 0:
            y = y * HS**-0.5
        ref[...] = y.astype(bf16)


def qkv_call(shift, x, vec, w1, bias, tables, width, rows=256):
    d = x[0].shape[1]
    count = x[0].shape[0] // rows
    n = count + x[1].shape[0] // rows
    g = n * rows
    table = pl.BlockSpec((rows, 128), lambda i, shift: (((i + shift[0] // rows) % n) % (LEN // rows), 0))
    return call(
        functools.partial(qkv_kernel, count=count),
        (n,),
        both(rows, d, count) + [held(4, d), held(d, 3 * width), held(3, width), table, table, table],
        [own_order(rows, d), own_order(rows, d), own_order(rows, 2)] + [seq_order(rows, width, n)] * 3,
        [shape(g, d, bf16), shape(g, d, bf16), shape(g, 2, f32)] + [shape(g, width, bf16)] * 3,
        [],
        6 * g * d * width,
    )(shift, *x, vec, w1, bias, *tables)


def context_grad_kernel(shift, g_ref, w_ref, do_ref):
    do_ref[...] = dot(g_ref[...], w_ref[...]).astype(bf16)


def context_grad_call(shift, grads, w1, width, rows=512):
    g, d = grads.shape
    return call(
        context_grad_kernel,
        (g // rows,),
        [own_order(rows, d), held(d, width, 3)],
        [own_order(rows, width)],
        [shape(g, width, bf16)],
        [],
        2 * g * d * width,
    )(shift, grads, w1)[0]


def attention_kernel(start, *refs, block, opens, closes):
    q_ref, k_ref, v_ref, do_ref, c_ref, sa_ref, sb_ref = refs[:7]
    refs = list(refs[7:])
    before = [] if opens else [refs.pop(0), refs.pop(0)]
    o_ref, dq_ref, dk_ref, dv_ref, dk_sum, dv_sum = refs
    step = pl.program_id(2)
    here = start[0] // block + step
    heads = q_ref.shape[1] // HS

    @pl.when(step == 0)
    def _():
        dk_sum[...] = jnp.zeros_like(dk_sum) if opens else before[0][...]
        dv_sum[...] = jnp.zeros_like(dv_sum) if opens else before[1][...]

    def turn_back(y, rows):
        return turn(y, c_ref[rows, :], -sa_ref[rows, :], -sb_ref[rows, :])

    def run(i):
        outs, dqs = [], []
        for h in range(heads):
            lanes = slice(h * HS, (h + 1) * HS)
            q, do = q_ref[:, lanes], do_ref[:, lanes]
            parts = [slice(j * block, (j + 1) * block) for j in range(i + 1)]
            scores = [dot(k_ref[rows, lanes], q, 1, 1) for rows in parts]
            key_pos = lax.broadcasted_iota(jnp.int32, (block, block), 0)
            query_pos = lax.broadcasted_iota(jnp.int32, (block, block), 1)
            scores[i] = jnp.where(key_pos <= query_pos, scores[i], NEG)
            top = functools.reduce(jnp.maximum, [jnp.max(s, axis=0, keepdims=True) for s in scores])
            weights = [jnp.exp(s - top) for s in scores]
            total = functools.reduce(jnp.add, [jnp.sum(w, axis=0, keepdims=True) for w in weights])
            scale = 1.0 / total
            weights = [w * scale for w in weights]
            low = [w.astype(bf16) for w in weights]
            mixed = functools.reduce(jnp.add, [dot(v_ref[rows, lanes], low[j], 0, 0) for j, rows in enumerate(parts)])
            do_t = do.astype(f32).T
            delta = jnp.sum(mixed * do_t, axis=0, keepdims=True)
            do_t = do_t.astype(bf16)
            q_t = q.astype(f32).T.astype(bf16)
            dq = 0.0
            for j, rows in enumerate(parts):
                prob_grad = dot(v_ref[rows, lanes], do, 1, 1)
                score_grad = (weights[j] * (prob_grad - delta)).astype(bf16)
                dv_sum[lanes, rows] += dot(do_t, low[j], 1, 1)
                dk_sum[lanes, rows] += dot(q_t, score_grad, 1, 1)
                dq = dq + dot(k_ref[rows, lanes], score_grad, 0, 0)
            outs.append(mixed.T)
            dqs.append(dq.T)
        o_ref[...] = jnp.concatenate(outs, axis=1).astype(bf16)
        rows = slice(i * block, (i + 1) * block)
        dq_ref[...] = turn_back(jnp.concatenate(dqs, axis=1) * HS**-0.5, rows).astype(bf16)

    for i in range(LEN // block):
        pl.when(here == i)(functools.partial(run, i))

    @pl.when(step == pl.num_programs(2) - 1)
    def _():
        if not closes:
            dk_ref[...] = dk_sum[...]
            dv_ref[...] = dv_sum[...]
            return
        for i in range(LEN // block):
            rows = slice(i * block, (i + 1) * block)
            dk_ref[rows, :] = turn_back(dk_sum[:, rows].T, rows).astype(bf16)
            dv_ref[rows, :] = dv_sum[:, rows].T.astype(bf16)


def attention_call(start, q, k, v, do, tables, before=None, closes=True, block=512):
    g, width = q.shape
    rows = do.shape[0]
    seqs, pairs = g // LEN, width // 128
    count = rows // seqs // block
    query = pl.BlockSpec((block, 128), lambda s, h, i, start: (s * count + start[0] // block + i, h))
    one = pl.BlockSpec((block, 128), lambda s, h, i, start: (s * count + i, h))
    whole = pl.BlockSpec((LEN, 128), lambda s, h, i, start: (s, h))
    sums = pl.BlockSpec((128, LEN), lambda s, h, i, start: (h, s))
    table = pl.BlockSpec((LEN, 128), lambda s, h, i, start: (0, 0))
    before = before or ()
    return call(
        functools.partial(attention_kernel, block=block, opens=not before, closes=closes),
        (seqs, pairs, count),
        [query, whole, whole, one, table, table, table] + [sums] * len(before),
        [one, one] + [whole if closes else sums] * 2,
        [shape(rows, width, bf16)] * 2 + [shape(g, width, bf16) if closes else shape(width, g, f32)] * 2,
        [pltpu.VMEM((128, LEN), f32), pltpu.VMEM((128, LEN), f32)],
        24 * rows * LEN * width,
    )(start, q, k, v, do, *tables, *before)


def normal_of(refs, st_ref, count):
    return (pick(refs, count).astype(f32) - st_ref[:, 0:1]) * st_ref[:, 1:2]


def project_back_kernel(shift, qo_ref, qt_ref, dk_ref, dv_ref, co_ref, ct_ref, n1_ref, x_ref, y_ref, st_ref, go_ref, gt_ref, vec_ref, w_ref, s_ref, send_ref, keep_ref, cols_ref, bias_ref, acc, *, count, fsdp):
    @at_first()
    def _():
        acc[...] = jnp.zeros_like(acc)
        cols_ref[...] = jnp.zeros_like(cols_ref)
        bias_ref[...] = jnp.zeros_like(bias_ref)

    n1 = n1_ref[...]
    width = dk_ref.shape[1]
    s = 0.0
    for part, joined in enumerate((pick((qo_ref, qt_ref), count), dk_ref[...], dv_ref[...])):
        lanes = slice(part * width, (part + 1) * width)
        bias_ref[part : part + 1, :] += jnp.sum(joined.astype(f32), axis=0, keepdims=True)
        s = s + dot(joined, w_ref[:, lanes], 1, 1)
        acc[:, lanes] += dot(n1, joined, 0, 0)
    acc[:, 3 * width :] += dot(pick((go_ref, gt_ref), count), pick((co_ref, ct_ref), count), 0, 0)
    normal = normal_of((x_ref, y_ref), st_ref, count)
    cols_ref[0:1, :] += jnp.sum(s * normal, axis=0, keepdims=True)
    cols_ref[1:2, :] += jnp.sum(s, axis=0, keepdims=True)
    s_ref[...] = s * vec_ref[0:1, :]

    @at_last()
    def _():
        put_blocks(fsdp, (send_ref, keep_ref), acc)


def project_back_call(shift, fsdp, dq, dk, dv, ctx, n1, x, st, grads, vec, w1, rows=256):
    g, d = n1.shape
    width = dk.shape[1]
    n, count = g // rows, x[0].shape[0] // rows
    return call(
        functools.partial(project_back_kernel, count=count, fsdp=fsdp),
        (n,),
        both(rows, width, count)
        + [seq_order(rows, width, n)] * 2
        + both(rows, width, count)
        + [own_order(rows, d)]
        + both(rows, d, count)
        + [own_order(rows, 2)]
        + both(rows, d, count)
        + [held(4, d), held(d, 3 * width)],
        [own_order(rows, d), *[pieces(d, 4 * width)[0]] * 2, held(2, d), held(3, width)],
        [shape(g, d, f32), *[pieces(d, 4 * width)[1]] * 2, shape(2, d, f32), shape(3, width, f32)],
        [pltpu.VMEM((d, 4 * width), f32)],
        14 * g * d * width,
    )(shift, *dq, dk, dv, *ctx, n1, *x, st, *grads, vec, w1)


def feed_forward_kernel(n2_ref, go_ref, gt_ref, co_ref, ct_ref, we_ref, ws_ref, wd_ref, be_ref, *refs, count, fsdp, fast):
    if fast:
        x_ref, bias_ref, d_send, d_keep, gp_ref, out_ref, send_ref, keep_ref, dw1_ref, acc, to_owner, from_other, *scratch = refs
        to = neighbours()
        reduce = Reduce(d_send, d_keep, dw1_ref, scratch[2:], to)
        row_copy = lambda b: remote(to_owner.at[b], from_other.at[b], scratch[:2], b, to["y"])
    else:
        gp_ref, out_ref, others_ref, send_ref, keep_ref, acc = refs
    step = pl.program_id(0)

    @at_first()
    def _():
        acc[...] = jnp.zeros_like(acc)
        if fast:
            greet(to)
            for p in range(PIECES):
                reduce.begin(p)

    if fast:
        for at, what in ((1, "x"), (3, 0), (5, 1), (7, "end")):

            @at_step(at)
            def _():
                for p in range(PIECES) if what in ("x", "end") else [what]:
                    {"x": reduce.across_x, "end": reduce.end}.get(what, reduce.along_z)(p)

        for b in range(count):

            @at_step(b + 1)
            def _():
                row_copy(b).start()

    own = step >= count
    n2, g = n2_ref[...], jnp.where(own, go_ref[...], gt_ref[...])
    branch = dot(jnp.where(own, co_ref[...], ct_ref[...]), wd_ref[...], 1, 1)
    act, slope = gelu_parts(dot(n2, we_ref[...]) + be_ref[...])
    act = act.astype(bf16)
    gp_ref[...] = slope.astype(bf16)
    branch = branch + dot(act, ws_ref[...], 1, 1)
    acc[...] += dot(g, act, 0, 0)
    if fast:

        @pl.when(jnp.logical_not(own))
        def _():
            to_owner[step] = branch.astype(bf16)

        for b in range(count):

            @at_step(b + count)
            def _():
                row_copy(b).wait()
                out_ref[...] = (x_ref[...].astype(f32) + (branch + from_other[b].astype(f32)) + bias_ref[...]).astype(bf16)

    else:
        put((others_ref, out_ref), count, branch.astype(bf16))

    @at_last()
    def _():
        put_blocks(fsdp, (send_ref, keep_ref), acc)


def feed_forward_call(fsdp, n2, grads, ctx, w2, w1, be, more=None, rows=256):
    g, d = n2.shape
    hidden, width = w2.shape[1] // 2, ctx[0].shape[1]
    own = grads[0].shape[0]
    n = g // rows
    count = own // rows if more else (g - own) // rows
    first = lambda c: pl.BlockSpec((rows, c), lambda i, *s: (jnp.minimum(i, count - 1), 0))
    second = lambda c: pl.BlockSpec((rows, c), lambda i, *s: (jnp.maximum(i - count, 0), 0))
    turned = lambda c: pl.BlockSpec((rows, c), lambda i, *s: ((i + own // rows) % n, 0))
    ins = [turned(d), second(d), first(d), second(width), first(width), held(d, hidden, 0), held(d, hidden, 1), held(d, width, 3), held(1, hidden)]
    half = pieces(d, hidden)
    acc = pltpu.VMEM((d, hidden), f32)
    flops = g * d * (6 * hidden + 2 * width)
    kernel = functools.partial(feed_forward_kernel, count=count, fsdp=fsdp, fast=bool(more))
    args = (n2, *grads, *ctx, w2, w2, w1, be)
    if not more:
        outs = [turned(hidden), second(d), first(d), half[0], half[0]]
        shapes = [shape(g, hidden, bf16), shape(own, d, bf16), shape(g - own, d, bf16), half[1], half[1]]
        return call(kernel, (n,), ins, outs, shapes, [acc], flops, 0)(*args)
    part = d // 16
    ins += [second(d), held(1, d), pl.BlockSpec(memory_space=pl.ANY), pieces(d, 4 * width)[0]]
    outs = [turned(hidden), second(d), half[0], half[0], held(part, 4 * width)]
    shapes = [shape(g, hidden, bf16), shape(own, d, bf16), half[1], half[1], shape(part, 4 * width, f32)]
    rows_buffer = pltpu.VMEM((count, rows, d), bf16)
    scratch = [acc, rows_buffer, rows_buffer] + sem_pair(count) + Reduce.scratch(d, 4 * width)
    return call(kernel, (n,), ins, outs, shapes, scratch, flops, 0, collective=0)(*args, *more)


def feed_back_kernel(n2_ref, go_ref, gt_ref, gp_ref, s1_ref, x_ref, y_ref, st_ref, vec_ref, we_ref, ws_ref, *refs, count, last, fsdp):
    s_refs = refs[: 1 + last]
    send_ref, keep_ref, cols_ref, bias_ref, acc = refs[1 + last :]

    @at_first()
    def _():
        acc[...] = jnp.zeros_like(acc)
        cols_ref[...] = jnp.zeros_like(cols_ref)
        bias_ref[...] = jnp.zeros_like(bias_ref)

    n2, g = n2_ref[...], pick((go_ref, gt_ref), count)
    pre_grad = (dot(g, ws_ref[...]) * gp_ref[...].astype(f32)).astype(bf16)
    bias_ref[...] += jnp.sum(pre_grad.astype(f32), axis=0, keepdims=True)
    s = dot(pre_grad, we_ref[...], 1, 1)
    acc[...] += dot(n2, pre_grad, 0, 0)
    normal = normal_of((x_ref, y_ref), st_ref, count)
    cols_ref[0:1, :] += jnp.sum(s * normal, axis=0, keepdims=True)
    cols_ref[1:2, :] += jnp.sum(s, axis=0, keepdims=True)
    s = s1_ref[...] + s * vec_ref[2:3, :]
    if last:
        put(s_refs, count, s.astype(bf16))
    else:
        s_refs[0][...] = s

    @at_last()
    def _():
        put_blocks(fsdp, (send_ref, keep_ref), acc)


def feed_back_call(fsdp, n2, grads, gp, s1, x, st, vec, w2, half, last, rows=256):
    g, d = n2.shape
    hidden = gp.shape[1] // 2
    own = x[0].shape[0]
    n, count = g // rows, own // rows
    return call(
        functools.partial(feed_back_kernel, count=count, last=last, fsdp=fsdp),
        (n,),
        [own_order(rows, d)]
        + both(rows, d, count)
        + [pl.BlockSpec((rows, hidden), lambda i, *s: (i, half)), own_order(rows, d)]
        + both(rows, d, count)
        + [own_order(rows, 2), held(4, d), held(d, hidden, half), held(d, hidden, 2 + half)],
        (both(rows, d, count) if last else [own_order(rows, d)]) + [pieces(d, hidden)[0]] * 2 + [held(2, d), held(1, hidden)],
        ([shape(own, d, bf16), shape(g - own, d, bf16)] if last else [shape(g, d, f32)])
        + [pieces(d, hidden)[1]] * 2
        + [shape(2, d, f32), shape(1, hidden, f32)],
        [pltpu.VMEM((d, hidden), f32)],
        6 * g * d * hidden,
        0,
    )(n2, *grads, gp, s1, *x, st, vec, w2, w2)


def rotary_tables():
    half = ROT // 2
    position = jnp.arange(LEN).astype(f32)
    inverse = 10000.0 ** (-(jnp.arange(half).astype(f32) * 2.0) / ROT)
    angle = position[:, None] * inverse[None, :]
    cos, sin = jnp.cos(angle), jnp.sin(angle)
    rest = jnp.zeros((LEN, HS - ROT), f32)
    none = jnp.zeros((LEN, half), f32)
    period = lambda *a: jnp.tile(jnp.concatenate(a, axis=1), (1, 128 // HS))
    return period(cos, cos, rest + 1.0), period(-sin, none, rest), period(none, sin, rest)


CORE, X = 1, 2


def flip(a, bit):
    return lax.ppermute(a, "fsdp", [(i, i ^ bit) for i in range(16)])


def along_z(a, k):
    return lax.ppermute(a, "fsdp", [(i, (i + 4 * k) % 16) for i in range(16)])


def reduce_rows(send, keep):
    half = send.shape[1] // 2
    quarter = half // 4
    got = flip(send, CORE)
    add = lambda a, b, rows: (a[:, rows].astype(f32) + b[:, rows].astype(f32)).astype(bf16)
    got2 = flip(add(keep, got, slice(0, half)), X)
    total = lambda k: sum(a[:, half + k * quarter : half + (k + 1) * quarter].astype(f32) for a in (keep, got)) + got2[:, k * quarter : (k + 1) * quarter].astype(f32)
    return join(sum([along_z(total(k).astype(bf16), k).astype(f32) for k in (1, 2, 3)], total(0)))


def join(a):
    return jnp.concatenate(list(a), axis=1)


def sum_all(a, over_all):
    for bit in (1, 2, 4, 8):
        a = a + flip(a, bit)
    head = a[:over_all]
    return jnp.concatenate([head + lax.ppermute(head, "tp", [(0, 1), (1, 0)]), a[over_all:]])


def make_body(fsdp, tp):
    fast = (fsdp, tp) == (16, 2)

    def body(inputs, cotangent, first_gain, first_shift, second_gain, second_shift, project_weight, project_bias, dense_weight, dense_bias, expand_weight, expand_bias, shrink_weight, shrink_bias):
        rows, d = inputs.shape
        width = dense_weight.shape[0]
        hidden = shrink_weight.shape[0]
        part = project_weight.shape[0]
        me = lax.axis_index("tp")
        swap = lambda a: lax.ppermute(a, "tp", [(0, 1), (1, 0)])
        split = lambda a: (a[:rows], a[rows:])
        zero = jnp.zeros((1,), jnp.int32)
        vec = jnp.stack([first_gain, first_shift, second_gain, second_shift])
        shard1 = jnp.concatenate([project_weight.reshape(part, 3 * width), dense_weight.T], axis=1)
        shard2 = jnp.concatenate([expand_weight, shrink_weight.T], axis=1)
        if fast:
            shift = (me * rows).astype(jnp.int32)[None]
            x = (inputs, swap(inputs))
            later, _ = lax.optimization_barrier((cotangent, x[1]))
            grads = (cotangent, swap(later))
        else:
            shift = zero
            x = split(lax.all_gather(inputs, "tp", axis=0, tiled=True))
            grads = split(lax.all_gather(cotangent, "tp", axis=0, tiled=True))
        w1 = lax.all_gather(shard1, "fsdp", axis=0, tiled=True)
        w2 = lax.all_gather(shard2, "fsdp", axis=0, tiled=True)
        tables = rotary_tables()
        n1, n2, st, q, k, v = qkv_call(shift, x, vec, w1, project_bias, tables, width)
        if fast:
            do = context_grad_call(zero, cotangent, w1, width)
            *own, dk, dv = attention_call(shift, q, k, v, do, tables, closes=False)
            late, *_ = lax.optimization_barrier((grads[1], own))
            grads = (cotangent, late)
            do = context_grad_call(zero, late, w1, width)
            *others, dk, dv = attention_call(rows - shift, q, k, v, do, tables, (dk, dv))
            ctx, dq = zip(own, others)
        else:
            do = context_grad_call(zero, jnp.concatenate(grads), w1, width)
            ctx, dq, dk, dv = attention_call(zero, q, k, v, do, tables)
            ctx, dq = split(ctx), split(dq)
        s, *dw1, cols1, bias1 = project_back_call(shift, fsdp, dq, dk, dv, ctx, n1, x, st, grads, vec, w1)
        out_bias = dense_bias + shrink_bias
        if fast:
            gp, output, *dws, dw1 = feed_forward_call(fsdp, n2, grads, ctx, w2, w1, expand_bias[None], (inputs, out_bias[None], *dw1))
        else:
            gp, *branch = feed_forward_call(fsdp, n2, grads, ctx, w2, w1, expand_bias[None])
            branch, dws = branch[:2], branch[2:]
        s, *dwe, cols2, bias2 = feed_back_call(fsdp, n2, grads, gp, s, x, st, vec, w2, 0, False)
        *s, send, keep, cols3, bias3 = feed_back_call(fsdp, n2, grads, gp, s, x, st, vec, w2, 1, True)
        own_rows, own_grads = inputs.astype(f32), cotangent.astype(f32)
        cols = jnp.concatenate([cols1, cols2 + cols3, jnp.sum(own_grads, axis=0, keepdims=True)]).reshape(-1)
        local = jnp.concatenate([bias1.reshape(-1), bias2.reshape(-1), bias3.reshape(-1)])
        if fast:
            s = s[0].astype(f32) + swap(s[1]).astype(f32)
            own_st = st[:rows]
            scatter = lambda pair: reduce_rows(*pair)
            small = sum_all(jnp.concatenate([cols, local]), cols.shape[0])
            cols, local = small[: cols.shape[0]], small[cols.shape[0] :]
        else:
            over = lambda a, axis: lax.psum_scatter(jnp.concatenate(a), axis, scatter_dimension=0, tiled=True).astype(f32)
            s = over(s, "tp")
            output = (own_rows + over(branch, "tp") + out_bias).astype(bf16)
            own_st = lax.dynamic_slice_in_dim(st, me * rows, rows, 0)
            scatter = lambda pair: over([join(a) for a in pair], "fsdp")
            dw1 = scatter(dw1)
            cols = lax.psum(cols, ("fsdp", "tp"))
            local = lax.psum(local, "fsdp")
        cols = cols.reshape(5, d)
        dws, dwe, dwf = scatter(dws), scatter(dwe), scatter((send, keep))
        normal = (own_rows - own_st[:, 0:1]) * own_st[:, 1:2]
        term = own_st[:, 1:2] * (s - jnp.mean(s, axis=1, keepdims=True) - normal * jnp.mean(s * normal, axis=1, keepdims=True))
        return (
            output,
            own_grads + term,
            cols[0],
            cols[1],
            cols[2],
            cols[3],
            dw1[:, : 3 * width].reshape(part, 3, width),
            local[: 3 * width].reshape(3, width),
            dw1[:, 3 * width :].T,
            cols[4],
            jnp.concatenate([dwe, dwf], axis=1),
            local[3 * width :],
            dws.T,
            cols[4],
        )

    return body


def solution(mesh):
    rows, rep = P(("fsdp", "tp"), None), P()
    return jax.shard_map(
        make_body(mesh.shape["fsdp"], mesh.shape["tp"]),
        mesh=mesh,
        in_specs=(rows, rows, rep, rep, rep, rep, P("fsdp", None, "tp"), P(None, "tp"), P("tp", "fsdp"), rep, P("fsdp", "tp"), P("tp"), P("tp", "fsdp"), rep),
        out_specs=(rows, rows, rep, rep, rep, rep, P("fsdp", None, "tp"), P(None, "tp"), P("tp", "fsdp"), rep, P("fsdp", "tp"), P("tp"), P("tp", "fsdp"), rep),
        check_vma=False,
    )
```

time: 497 us -> 469 us (0.944)
  waiting for transfers between devices: 157 us -> 102 us
  Pallas kernels: 220 us -> 270 us
  blocking collectives: 40.7 us -> 0 us
  starting transfers between devices: 5.33 us -> 27.1 us
  local copies, waits for them, and re-layouts: 30.4 us -> 17.8 us
    ppermute x4 -> x23, waiting for transfers between devices: 156 us -> 101 us  [the longest x10 41.8 us: flip(): return lax.ppermute(a, 'fsdp', [(i, i ^ bit) for i in range(16)])]
    pallas_call x6 -> x9, Pallas kernels: 220 us -> 270 us  [call(): pl.pallas_call(kernel, grid_spec=pltpu.PrefetchScalarGridSpec(num_scalar_...]
    psum x1 -> x0, blocking collectives: 40.7 us -> none  [body(): small = lax.psum(small, ('fsdp', 'tp'))]
    ppermute x4 -> x23, starting transfers between devices: 5.17 us -> 27 us  [the longest x9 14.7 us: along_z(): return lax.ppermute(a, 'fsdp', [(i, (i + 4 * k) % 16) for i in range(16)])]
    convert_element_type x2 -> x6, other arithmetic: 2.12 us -> 9.85 us  [the longest x3 5.01 us: reduce_rows(): (a[:, rows].astype(f32) + b[:, rows].astype(f32)).astype(bf16)]
    concatenate x4, other arithmetic: 8.73 us -> 1.98 us  [the longest x1 1.13 us: rotary_tables(): period = lambda *a: jnp.tile(jnp.concatenate(a, axis=1), (1, 128 // HS))]
    slice x4 -> x1, local copies, waits for them, and re-layouts: 6.51 us -> 0.01 us  [sum_all(): head = a[:over_all]]
    concatenate x4 -> x2, local copies, waits for them, and re-layouts: 6.43 us -> 0.15 us  [rotary_tables(): period = lambda *a: jnp.tile(jnp.concatenate(a, axis=1), (1, 128 // HS))]
  transfers between devices with their start and end apart: 8 -> 25, of which waited for: 4 -> 14; matrix products, arithmetic and copies ran while one was open for 10% -> 9% of each run, Pallas kernels for 45% -> 40%
where the time goes in v2:
time: 469 us; the launch traced here: 462 us
  Pallas kernels  270 us (58%)
  waiting for transfers between devices  102 us (22%)
  other arithmetic  29.8 us (6%)
  starting transfers between devices  27.1 us (6%)
  local copies, waits for them, and re-layouts  17.8 us (4%)
  between operations  14.7 us (3%)
    pallas_call x9, Pallas kernels, call(): pl.pallas_call(kernel, grid_spec=pltpu.PrefetchScalarGridSpec(num_scalar_...  270 us
    ppermute x10, waiting for transfers between devices, flip(): return lax.ppermute(a, 'fsdp', [(i, i ^ bit) for i in range(16)])  41.8 us
    ppermute x3, waiting for transfers between devices, body(): swap = lambda a: lax.ppermute(a, 'tp', [(0, 1), (1, 0)])  40.6 us
    ppermute x9, waiting for transfers between devices, along_z(): return lax.ppermute(a, 'fsdp', [(i, (i + 4 * k) % 16) for i in range(16)])  18.5 us
    ppermute x9, starting transfers between devices, along_z(): return lax.ppermute(a, 'fsdp', [(i, (i + 4 * k) % 16) for i in range(16)])  14.7 us
  transfers between devices with their start and end apart: 25, of which 14 were waited for; matrix products, arithmetic and copies ran while one was open for 9% of the time, Pallas kernels for 40%

profile of v2, /device:TPU:0, one launch (start us, length us, event | category | flops | bytes accessed | tf_op | source)
XLA Modules:
  0.0 461.9 jit_solution(14680079555831963661)
XLA Ops:
  7.2 0.9 copy.42
  8.2 1.6 pad_maximum_fusion.2
  9.8 1.9 pad_maximum_fusion
  11.7 3.1 collective-permute-start
  15.3 1.1 maximum_maximum_fusion.2
  16.5 1.3 copy.31.c_ref.refs_4_
  17.9 1.3 tile.14
  19.2 1.3 copy.32.sa_ref.refs_5_
  20.5 1.2 tile.31
  21.7 1.3 copy.33.sb_ref.refs_6_
  24.3 36.4 %collective-permute-done.y_ref = bf16[1024,1024]{1,0:T(8,128)(2,1)} collective-permute-done((bf16[1024,1024]{1,0:T(8,128)(2,1)}, bf16[1024,1024]{1,0:T(8,128)(2,1)}, u32[]{:S(2)}, u32[]{:S(2)}) %collective-permute-start) | collective-permute-done | bytes 2097184 | tf_op jit(solution)/shard_map/ppermute | solution.py:602
  60.7 1.7 collective-permute-start.1
  62.5 1.4 all-gather.3.cloned.1.call-done.w_ref.wd_ref
  63.8 3.8 shard_map.246.refs_3_
  67.6 15.7 %shard_map.245 = (bf16[2048,1024]{1,0:T(8,128)(2,1)}, bf16[2048,1024]{1,0:T(8,128)(2,1)}, f32[2048,2]{1,0:T(8,128)}, bf16[2048,512]{1,0:T(8,128)(2,1)}, bf16[204...) custom-call(s32[1]{0:T(128)} %bitcast.shift.start, bf16[1024,1024]{1,0:T(8,128)(2,1)} %x_ref.7, ...), custom_call_target="tpu_custom_call" | custom-call | flops 6442450944 | bytes 26253316 | tf_op jit(solution)/shard_map/pallas_call | solution.py:48
  83.3 32.5 %shard_map.247 = (bf16[1024,512]{1,0:T(8,128)(2,1)}, bf16[1024,512]{1,0:T(8,128)(2,1)}, f32[512,2048]{1,0:T(8,128)}, f32[512,2048]{1,0:T(8,128)}) custom-call(s32[1]{0:T(128)} %bitcast.shift.start, bf16[2048,512]{1,0:T(8,128)(2,1)} %get-tuple-element.53.refs_0_, bf16[2048,512]{1,0:T(8,128)(2,1)} %get-tuple-element.54.refs_1_, ...), custom_call_target="tpu_custom_call" | custom-call | flops 25769803776 | bytes 20971524 | tf_op jit(solution)/shard_map/pallas_call | solution.py:48
  115.9 3.8 shard_map.248.refs_3_
  119.6 78.1 %shard_map.249 = (bf16[1024,512]{1,0:T(8,128)(2,1)}, bf16[1024,512]{1,0:T(8,128)(2,1)}, bf16[2048,512]{1,0:T(8,128)(2,1)}, bf16[2048,512]{1,0:T(8,128)(2,1)}) custom-call(s32[1]{0:T(128)S(6)} %sub.24.start, bf16[2048,512]{1,0:T(8,128)(2,1)} %get-tuple-element.53.refs_0_, bf16[2048,512]{1,0:T(8,128)(2,1)} %get-tuple-element.54.refs_1_, ...), custom_call_target="tpu_custom_call" | custom-call | flops 25769803776 | bytes 25165828 | tf_op jit(solution)/shard_map/pallas_call | solution.py:48
  197.7 25.5 %shard_map.250 = (f32[2048,1024]{1,0:T(8,128)}, bf16[2,512,1024]{2,1,0:T(8,128)(2,1)}, bf16[2,512,1024]{2,1,0:T(8,128)(2,1)}, f32[2,1024]{1,0:T(2,128)}, f32[3,512]{1,0:T(4,128)}) custom-call(s32[1]{0:T(128)} %bitcast.shift.start, bf16[1024,512]{1,0:T(8,128)(2,1)} %get-tuple-element.57.qo_ref, bf16[1024,512]{1,0:T(8,128)(2,1)} %get-tuple-element.62.qt_ref, ...), custom_call_target="tpu_custom_call" | custom-call | flops 15032385536 | bytes 37795844 | tf_op jit(solution)/shard_map/pallas_call | solution.py:48
  223.2 64.3 %shard_map.251 = (bf16[2048,2048]{1,0:T(8,128)(2,1)}, bf16[1024,1024]{1,0:T(8,128)(2,1)}, bf16[2,512,1024]{2,1,0:T(8,128)(2,1)}, bf16[2,512,1024]{2,1,0:T(8,128)(2,1)}, f32[64,2048]{1,0:T(8,128)}) custom-call(bf16[2048,1024]{1,0:T(8,128)(2,1)} %get-tuple-element.51.n2_ref, bf16[1024,1024]{1,0:T(8,128)(2,1)} %go_ref.7, ...), custom_call_target="tpu_custom_call" | custom-call | flops 27917287424 | bytes 52965376 | tf_op jit(solution)/shard_map/pallas_call | solution.py:48
  287.5 23.2 %shard_map.252 = (f32[2048,1024]{1,0:T(8,128)}, bf16[2,512,512]{2,1,0:T(8,128)(2,1)}, bf16[2,512,512]{2,1,0:T(8,128)(2,1)}, f32[2,1024]{1,0:T(2,128)}, f32[1,1024]{1,0:T(1,128)}) custom-call(bf16[2048,1024]{1,0:T(8,128)(2,1)} %get-tuple-element.51.n2_ref, bf16[1024,1024]{1,0:T(8,128)(2,1)} %go_ref.7, bf16[1024,1024]{1,0:T(8,128)(2,1)} %collective-permute-done.1.g_ref.gt_ref, ...), custom_call_target="tpu_custom_call" | custom-call | flops 12884901888 | bytes 56668160 | tf_op jit(solution)/shard_map/pallas_call | solution.py:48
  310.9 23.5 %shard_map.253 = (bf16[1024,1024]{1,0:T(8,128)(2,1)}, bf16[1024,1024]{1,0:T(8,128)(2,1)}, bf16[2,512,512]{2,1,0:T(8,128)(2,1)}, bf16[2,512,512]{2,1,0:T(8,128)(2...) custom-call(bf16[2048,1024]{1,0:T(8,128)(2,1)} %get-tuple-element.51.n2_ref, bf16[1024,1024]{1,0:T(8,128)(2,1)} %go_ref.7, ...), custom_call_target="tpu_custom_call" | custom-call | flops 12884901888 | bytes 52473856 | tf_op jit(solution)/shard_map/pallas_call | solution.py:48
  334.9 0.7 collective-permute-start.2
  335.7 1.1 add_convert_fusion.2
  337.4 1.0 copy-done.7
  338.4 2.0 add_convert_fusion.1
  340.4 1.3 collective-permute-start.14
  341.7 1.7 slice_reduce_fusion.1
  343.5 1.2 slice.192
  344.7 0.8 copy.44
  345.5 1.6 slice_bitcast_fusion.6
  347.1 4.8 %collective-permute-done.9 = bf16[2,256,512]{2,1,0:T(8,128)(2,1)} collective-permute-done((bf16[2,256,512]{2,1,0:T(8,128)(2,1)}, bf16[2,256,512]{2,1,0:T(8,128)(2,1)}, u32[]{:S(2)}, u32[]{:S(2)}) %collective-permute-start.9) | collective-permute-done | bytes 524320 | tf_op jit(solution)/shard_map/ppermute | solution.py:565
  351.8 1.5 add_convert_fusion.11
  353.3 1.0 collective-permute-start.10
  354.4 1.6 collective-permute-start.11
  356.0 6.0 %collective-permute-done.14 = bf16[2,256,512]{2,1,0:T(8,128)(2,1)} collective-permute-done((bf16[2,256,512]{2,1,0:T(8,128)(2,1)}, bf16[2,256,512]{2,1,0:T(8,128)(2,1)}, u32[]{:S(2)}, u32[]{:S(2)}) %collective-permute-start.14) | collective-permute-done | bytes 524320 | tf_op jit(solution)/shard_map/ppermute | solution.py:565
  361.9 2.0 collective-permute-start.12
  363.9 1.4 add_convert_fusion.8
  365.4 1.3 collective-permute-start.16
  366.7 1.2 collective-permute-done.12
  367.9 4.3 collective-permute-start.17
  372.2 1.1 convert_add_fusion.4
  373.6 3.4 collective-permute-done.16
  377.0 1.8 convert_add_fusion.3
  378.7 4.1 collective-permute-done.2
  382.9 3.1 fusion
  386.0 4.8 %convert_reduce_fusion = (f32[1024]{0:T(1024)S(1)}, f32[1024,1024]{1,0:T(8,128)}) fusion(bf16[1024,1024]{1,0:T(8,128)(2,1)S(1)} %copy-done.3, f32[1024]{0:T(1024)S(1)} %broadcast_multiply_fusion, f32[1024]{0:T(1024)S(1)} %get-tuple-element.119, bf16[1024,1024]{1,0:T(8,128)(2,1)S(1)} %copy-done, f32[1024]{0:T(1024)S(1)} %broadcast_multiply_fusion.1, ...), kind=kLoop, calls=%fused_computation | loop fusion | flops 13630464 | bytes 12603392 | tf_op jit(solution)/shard_map/reduce_sum | solution.py:643
  391.0 2.0 add_convert_fusion
  392.9 0.6 collective-permute-start.19
  393.6 1.5 collective-permute-start.4
  395.1 24.2 %collective-permute-done.4 = f32[8704]{0:T(1024)S(1)} collective-permute-done((f32[8704]{0:T(1024)S(1)}, f32[8704]{0:T(1024)S(1)}, u32[]{:S(2)}, u32[]{:S(2)}) %collective-permute-start.4) | collective-permute-done | bytes 34848 | tf_op jit(solution)/shard_map/ppermute | solution.py:565
  419.9 3.4 collective-permute-done.5
  423.3 1.1 collective-permute-start.6
  424.4 0.8 pad_maximum_fusion.1
  425.2 3.3 collective-permute-done.6
  430.1 2.0 add_convert_fusion.5
  432.1 1.0 collective-permute-start.20
  433.2 2.0 collective-permute-start.21
  435.1 1.3 collective-permute-start.22
  437.1 6.1 %collective-permute-done.20 = bf16[2,64,1024]{2,1,0:T(8,128)(2,1)S(1)} collective-permute-done((bf16[2,64,1024]{2,1,0:T(8,128)(2,1)S(1)}, bf16[2,64,1024]{2,1,0:T(8,128)(2,1)S(1)}, u32[]{:S(2)}, u32[]{:S(2)}) %collective-permute-start.20) | collective-permute-done | bytes 262176 | tf_op jit(solution)/shard_map/ppermute | solution.py:569
  443.2 7.5 %collective-permute-done.21 = bf16[2,64,1024]{2,1,0:T(8,128)(2,1)S(1)} collective-permute-done((bf16[2,64,1024]{2,1,0:T(8,128)(2,1)S(1)}, bf16[2,64,1024]{2,1,0:T(8,128)(2,1)S(1)}, u32[]{:S(2)}, u32[]{:S(2)}) %collective-permute-start.21) | collective-permute-done | bytes 262176 | tf_op jit(solution)/shard_map/ppermute | solution.py:569
  450.8 1.4 convert_add_fusion.2
  452.2 0.8 maximum_bitcast_fusion
  453.6 1.3 copy.48
  (102 shorter events, 7.3 us)
Async XLA Ops:
  7.2 56.7 %all-gather.3.cloned.1.call-start = ((), (), s32[]{:S(2)}) async-start(), calls=%async_computation | async-start | bytes 4456448 | tf_op jit(solution)/shard_map/all_gather | solution.py:617
  9.8 213.5 %all-gather.5.cloned.1.call-start = ((), (), s32[]{:S(2)}) async-start(), calls=%async_computation.1 | async-start | bytes 8912896 | tf_op jit(solution)/shard_map/all_gather | solution.py:618
  11.7 49.0 %collective-permute-start = (bf16[1024,1024]{1,0:T(8,128)(2,1)}, bf16[1024,1024]{1,0:T(8,128)(2,1)}, u32[]{:S(2)}, u32[]{:S(2)}) collective-permute-start(bf16[1024,1024]{1,0:T(8,128)(2,1)} %x_ref.7), channel_id=1, source_target_pairs={{0,1},{1,0},{2,3},{3,2},{4,5},{5,4},{6,7},{7,6},{8,9},{9,8},{10,11... | collective-permute-start | bytes 6291464 | tf_op jit(solution)/shard_map/ppermute | solution.py:602
  17.9 5.2 %copy-start.17 = (f32[1024]{0:T(1024)S(1)}, f32[1024]{0:T(1024)}, u32[]{:S(2)}) copy-start(f32[1024]{0:T(1024)} %param.23) | copy-start | bytes 12292
  17.9 5.2 %copy-start.18 = (f32[1024]{0:T(1024)S(1)}, f32[1024]{0:T(1024)}, u32[]{:S(2)}) copy-start(f32[1024]{0:T(1024)} %param.27) | copy-start | bytes 12292
  17.9 5.8 %copy-start.19 = (f32[1024]{0:T(1024)S(1)}, f32[1024]{0:T(1024)}, u32[]{:S(2)}) copy-start(f32[1024]{0:T(1024)} %param.19) | copy-start | bytes 12292
  17.9 5.8 %copy-start.20 = (f32[1024]{0:T(1024)S(1)}, f32[1024]{0:T(1024)}, u32[]{:S(2)}) copy-start(f32[1024]{0:T(1024)} %param.18) | copy-start | bytes 12292
  17.9 5.8 %copy-start.21 = (f32[1024]{0:T(1024)S(1)}, f32[1024]{0:T(1024)}, u32[]{:S(2)}) copy-start(f32[1024]{0:T(1024)} %param.17) | copy-start | bytes 12292
  17.9 5.8 %copy-start.22 = (f32[1024]{0:T(1024)S(1)}, f32[1024]{0:T(1024)}, u32[]{:S(2)}) copy-start(f32[1024]{0:T(1024)} %param.16) | copy-start | bytes 12292
  17.9 42.8 %copy-start.2 = (bf16[1024,1024]{1,0:T(8,128)(2,1)S(1)}, bf16[1024,1024]{1,0:T(8,128)(2,1)}, u32[]{:S(2)}) copy-start(bf16[1024,1024]{1,0:T(8,128)(2,1)} %go_ref.7) | copy-start | bytes 6291460
  60.7 55.1 %collective-permute-start.1 = (bf16[1024,1024]{1,0:T(8,128)(2,1)S(1)}, bf16[1024,1024]{1,0:T(8,128)(2,1)}, u32[]{:S(2)}, u32[]{:S(2)}) collective-permute-start(bf16[1024,1024]{1,0:T(8,128)(2,1)S(1)} %copy-done.2), channel_id=1, source_target_pairs={{0,1},{1,0},{2,3},{3,2},{4,5},{5,4},{6,7},{7,6},{8,9},{9,8},{10,11... | collective-permute-start | bytes 6291464 | tf_op jit(solution)/shard_map/ppermute | solution.py:602
  310.8 24.9 %collective-permute-start.8 = (bf16[2,512,512]{2,1,0:T(8,128)(2,1)}, bf16[2,512,512]{2,1,0:T(8,128)(2,1)S(1)}, u32[]{:S(2)}, u32[]{:S(2)}) collective-permute-start(bf16[2,512,512]{2,1,0:T(8,128)(2,1)} %get-tuple-element.83), channel_id=1, source_target_pairs={{0,2},{2,0},{4,6},{6,4},{8,10},{10,8},{12,14},{14,12},{16,18},{18,... | collective-permute-start | bytes 3145736 | tf_op jit(solution)/shard_map/ppermute | solution.py:565
  310.8 24.8 %copy-start.6 = (bf16[2,512,512]{2,1,0:T(8,128)(2,1)S(1)}, bf16[2,512,512]{2,1,0:T(8,128)(2,1)}, u32[]{:S(2)}) copy-start(bf16[2,512,512]{2,1,0:T(8,128)(2,1)} %get-tuple-element.82) | copy-start | bytes 3145732
  334.3 9.1 %copy-start.15 = (f32[3,512]{1,0:T(4,128)S(1)}, f32[3,512]{1,0:T(4,128)}, u32[]{:S(2)}) copy-start(f32[3,512]{1,0:T(4,128)} %get-tuple-element.78) | copy-start | bytes 18436
  334.3 11.1 %copy-start.13 = (f32[2,1024]{1,0:T(2,128)S(1)}, f32[2,1024]{1,0:T(2,128)}, u32[]{:S(2)}) copy-start(f32[2,1024]{1,0:T(2,128)} %get-tuple-element.76) | copy-start | bytes 24580
  334.4 11.1 %copy-start.14 = (f32[2,1024]{1,0:T(2,128)S(1)}, f32[2,1024]{1,0:T(2,128)}, u32[]{:S(2)}) copy-start(f32[2,1024]{1,0:T(2,128)} %get-tuple-element.77) | copy-start | bytes 24580
  334.4 29.6 %copy-start.5 = (bf16[2,512,512]{2,1,0:T(8,128)(2,1)S(1)}, bf16[2,512,512]{2,1,0:T(8,128)(2,1)}, u32[]{:S(2)}) copy-start(bf16[2,512,512]{2,1,0:T(8,128)(2,1)} %get-tuple-element.84) | copy-start | bytes 3145732
  334.4 3.0 collective-permute-start.13
  334.9 47.9 %collective-permute-start.2 = (bf16[1024,1024]{1,0:T(8,128)(2,1)}, bf16[1024,1024]{1,0:T(8,128)(2,1)}, u32[]{:S(2)}, u32[]{:S(2)}) collective-permute-start(bf16[1024,1024]{1,0:T(8,128)(2,1)} %get-tuple-element.74), channel_id=1, source_target_pairs={{0,1},{1,0},{2,3},{3,2},{4,5},{5,4},{6,7},{7,6},{8,9},{9,8},{10,11... | collective-permute-start | bytes 6291464 | tf_op jit(solution)/shard_map/ppermute | solution.py:602
  335.6 1.8 copy-start.8
  336.7 15.1 %collective-permute-start.9 = (bf16[2,256,512]{2,1,0:T(8,128)(2,1)}, bf16[2,256,512]{2,1,0:T(8,128)(2,1)}, u32[]{:S(2)}, u32[]{:S(2)}) collective-permute-start(bf16[2,256,512]{2,1,0:T(8,128)(2,1)} %add_convert_fusion.2), channel_id=1, source_target_pairs={{0,4},{2,6},{4,0},{6,2},{8,12},{10,14},{12,8},{14,10},{16,20},{18,... | collective-permute-start | bytes 1572872 | tf_op jit(solution)/shard_map/ppermute | solution.py:565
  337.4 1.0 copy-start.7
  340.4 42.5 %copy-start = (bf16[1024,1024]{1,0:T(8,128)(2,1)S(1)}, bf16[1024,1024]{1,0:T(8,128)(2,1)}, u32[]{:S(2)}) copy-start(bf16[1024,1024]{1,0:T(8,128)(2,1)} %x_ref.7) | copy-start | bytes 6291460
  340.4 21.5 %collective-permute-start.14 = (bf16[2,256,512]{2,1,0:T(8,128)(2,1)}, bf16[2,256,512]{2,1,0:T(8,128)(2,1)}, u32[]{:S(2)}, u32[]{:S(2)}) collective-permute-start(bf16[2,256,512]{2,1,0:T(8,128)(2,1)} %add_convert_fusion.1), channel_id=1, source_target_pairs={{0,4},{2,6},{4,0},{6,2},{8,12},{10,14},{12,8},{14,10},{16,20},{18,... | collective-permute-start | bytes 1572872 | tf_op jit(solution)/shard_map/ppermute | solution.py:565
  343.4 39.4 %copy-start.1 = (bf16[1024,1024]{1,0:T(8,128)(2,1)S(1)}, bf16[1024,1024]{1,0:T(8,128)(2,1)}, u32[]{:S(2)}) copy-start(bf16[1024,1024]{1,0:T(8,128)(2,1)} %get-tuple-element.73) | copy-start | bytes 6291460
  343.5 47.5 %collective-permute-start.18 = (bf16[2,512,1024]{2,1,0:T(8,128)(2,1)}, bf16[2,512,1024]{2,1,0:T(8,128)(2,1)}, u32[]{:S(2)}, u32[]{:S(2)}) collective-permute-start(bf16[2,512,1024]{2,1,0:T(8,128)(2,1)} %get-tuple-element.87), channel_id=1, source_target_pairs={{0,2},{2,0},{4,6},{6,4},{8,10},{10,8},{12,14},{14,12},{16,18},{18,... | collective-permute-start | bytes 6291464 | tf_op jit(solution)/shard_map/ppermute | solution.py:565
  353.3 12.0 %collective-permute-start.10 = (bf16[2,64,512]{2,1,0:T(8,128)(2,1)S(1)}, bf16[2,64,512]{2,1,0:T(8,128)(2,1)S(1)}, u32[]{:S(2)}, u32[]{:S(2)}) collective-permute-start(bf16[2,64,512]{2,1,0:T(8,128)(2,1)S(1)} %get-tuple-element.123), channel_id=1, source_target_pairs={{0,8},{2,10},{4,12},{6,14},{8,16},{10,18},{12,20},{14,22},{16,24},... | collective-permute-start | bytes 393224 | tf_op jit(solution)/shard_map/ppermute | solution.py:569
  354.4 11.0 %collective-permute-start.11 = (bf16[2,64,512]{2,1,0:T(8,128)(2,1)S(1)}, bf16[2,64,512]{2,1,0:T(8,128)(2,1)S(1)}, u32[]{:S(2)}, u32[]{:S(2)}) collective-permute-start(bf16[2,64,512]{2,1,0:T(8,128)(2,1)S(1)} %get-tuple-element.125), channel_id=1, source_target_pairs={{0,16},{2,18},{4,20},{6,22},{8,24},{10,26},{12,28},{14,30},{16,0},... | collective-permute-start | bytes 393224 | tf_op jit(solution)/shard_map/ppermute | solution.py:569
  361.9 5.9 %collective-permute-start.12 = (bf16[2,64,512]{2,1,0:T(8,128)(2,1)S(1)}, bf16[2,64,512]{2,1,0:T(8,128)(2,1)S(1)}, u32[]{:S(2)}, u32[]{:S(2)}) collective-permute-start(bf16[2,64,512]{2,1,0:T(8,128)(2,1)S(1)} %get-tuple-element.124), channel_id=1, source_target_pairs={{0,24},{2,26},{4,28},{6,30},{8,0},{10,2},{12,4},{14,6},{16,8},{18,... | collective-permute-start | bytes 393224 | tf_op jit(solution)/shard_map/ppermute | solution.py:569
  365.3 8.3 %collective-permute-start.15 = (bf16[2,64,512]{2,1,0:T(8,128)(2,1)S(1)}, bf16[2,64,512]{2,1,0:T(8,128)(2,1)S(1)}, u32[]{:S(2)}, u32[]{:S(2)}) collective-permute-start(bf16[2,64,512]{2,1,0:T(8,128)(2,1)S(1)} %get-tuple-element.126), channel_id=1, source_target_pairs={{0,8},{2,10},{4,12},{6,14},{8,16},{10,18},{12,20},{14,22},{16,24},... | collective-permute-start | bytes 393224 | tf_op jit(solution)/shard_map/ppermute | solution.py:569
  365.4 11.6 %collective-permute-start.16 = (bf16[2,64,512]{2,1,0:T(8,128)(2,1)S(1)}, bf16[2,64,512]{2,1,0:T(8,128)(2,1)S(1)}, u32[]{:S(2)}, u32[]{:S(2)}) collective-permute-start(bf16[2,64,512]{2,1,0:T(8,128)(2,1)S(1)} %get-tuple-element.128), channel_id=1, source_target_pairs={{0,16},{2,18},{4,20},{6,22},{8,24},{10,26},{12,28},{14,30},{16,0},... | collective-permute-start | bytes 393224 | tf_op jit(solution)/shard_map/ppermute | solution.py:569
  367.9 18.1 %copy-start.3 = (bf16[1024,1024]{1,0:T(8,128)(2,1)S(1)}, bf16[1024,1024]{1,0:T(8,128)(2,1)}, u32[]{:S(2)}) copy-start(bf16[1024,1024]{1,0:T(8,128)(2,1)} %go_ref.7) | copy-start | bytes 6291460
  367.9 9.1 %collective-permute-start.17 = (bf16[2,64,512]{2,1,0:T(8,128)(2,1)S(1)}, bf16[2,64,512]{2,1,0:T(8,128)(2,1)S(1)}, u32[]{:S(2)}, u32[]{:S(2)}) collective-permute-start(bf16[2,64,512]{2,1,0:T(8,128)(2,1)S(1)} %get-tuple-element.127), channel_id=1, source_target_pairs={{0,24},{2,26},{4,28},{6,30},{8,0},{10,2},{12,4},{14,6},{16,8},{18,... | collective-permute-start | bytes 393224 | tf_op jit(solution)/shard_map/ppermute | solution.py:569
  386.0 4.8 %copy-start.16 = (f32[2,1024]{1,0:T(2,128)S(1)}, f32[2,1024]{1,0:T(2,128)}, u32[]{:S(2)}) copy-start(f32[2,1024]{1,0:T(2,128)} %get-tuple-element.75) | copy-start | bytes 24580
  386.0 4.8 %copy-start.10 = (f32[1,1024]{1,0:T(1,128)S(1)}, f32[1,1024]{1,0:T(1,128)}, u32[]{:S(2)}) copy-start(f32[1,1024]{1,0:T(1,128)} %get-tuple-element.79) | copy-start | bytes 12292
  386.0 4.8 %copy-start.11 = (f32[1,1024]{1,0:T(1,128)S(1)}, f32[1,1024]{1,0:T(1,128)}, u32[]{:S(2)}) copy-start(f32[1,1024]{1,0:T(1,128)} %get-tuple-element.80) | copy-start | bytes 12292
  390.8 29.1 %copy-start.9 = (f32[2,64,512]{2,1,0:T(8,128)S(1)}, f32[2,64,512]{2,1,0:T(8,128)}, u32[]{:S(2)}) copy-start(f32[2,64,512]{2,1,0:T(8,128)} %convert_add_fusion.3) | copy-start | bytes 786436
  390.9 2.7 collective-permute-start.3
  392.9 37.2 %collective-permute-start.19 = (bf16[2,256,1024]{2,1,0:T(8,128)(2,1)S(1)}, bf16[2,256,1024]{2,1,0:T(8,128)(2,1)}, u32[]{:S(2)}, u32[]{:S(2)}) collective-permute-start(bf16[2,256,1024]{2,1,0:T(8,128)(2,1)S(1)} %add_convert_fusion), channel_id=1, source_target_pairs={{0,4},{2,6},{4,0},{6,2},{8,12},{10,14},{12,8},{14,10},{16,20},{18,... | collective-permute-start | bytes 3145736 | tf_op jit(solution)/shard_map/ppermute | solution.py:565
  393.6 25.8 %collective-permute-start.4 = (f32[8704]{0:T(1024)S(1)}, f32[8704]{0:T(1024)S(1)}, u32[]{:S(2)}, u32[]{:S(2)}) collective-permute-start(f32[8704]{0:T(1024)S(1)} %fusion.2), channel_id=1, source_target_pairs={{0,4},{2,6},{4,0},{6,2},{8,12},{10,14},{12,8},{14,10},{16,20},{18,... | collective-permute-start | bytes 104456 | tf_op jit(solution)/shard_map/ppermute | solution.py:565
  419.3 4.0 collective-permute-start.5
  423.3 5.3 %collective-permute-start.6 = (f32[8704]{0:T(1024)S(1)}, f32[8704]{0:T(1024)S(1)}, u32[]{:S(2)}, u32[]{:S(2)}) collective-permute-start(f32[8704]{0:T(1024)S(1)} %add.145), channel_id=1, source_target_pairs={{0,16},{2,18},{4,20},{6,22},{8,24},{10,26},{12,28},{14,30},{16,0},... | collective-permute-start | bytes 104456 | tf_op jit(solution)/shard_map/ppermute | solution.py:565
  424.4 29.2 %copy-start.4 = (bf16[1024,1024]{1,0:T(8,128)(2,1)S(1)}, bf16[1024,1024]{1,0:T(8,128)(2,1)}, u32[]{:S(2)}) copy-start(bf16[1024,1024]{1,0:T(8,128)(2,1)} %get-tuple-element.190) | copy-start | bytes 6291460
  429.2 7.3 %collective-permute-start.7 = (f32[5120]{0:T(1024)S(1)}, f32[5120]{0:T(1024)S(1)}, u32[]{:S(2)}, u32[]{:S(2)}) collective-permute-start(f32[5120]{0:T(1024)S(1)} %slice.240), channel_id=1, source_target_pairs={{0,1},{1,0},{2,3},{3,2},{4,5},{5,4},{6,7},{7,6},{8,9},{9,8},{10,11... | collective-permute-start | bytes 61448 | tf_op jit(solution)/shard_map/ppermute | solution.py:590
  432.1 11.1 %collective-permute-start.20 = (bf16[2,64,1024]{2,1,0:T(8,128)(2,1)S(1)}, bf16[2,64,1024]{2,1,0:T(8,128)(2,1)S(1)}, u32[]{:S(2)}, u32[]{:S(2)}) collective-permute-start(bf16[2,64,1024]{2,1,0:T(8,128)(2,1)S(1)} %get-tuple-element.120), channel_id=1, source_target_pairs={{0,8},{2,10},{4,12},{6,14},{8,16},{10,18},{12,20},{14,22},{16,24},... | collective-permute-start | bytes 786440 | tf_op jit(solution)/shard_map/ppermute | solution.py:569
  433.2 17.6 %collective-permute-start.21 = (bf16[2,64,1024]{2,1,0:T(8,128)(2,1)S(1)}, bf16[2,64,1024]{2,1,0:T(8,128)(2,1)S(1)}, u32[]{:S(2)}, u32[]{:S(2)}) collective-permute-start(bf16[2,64,1024]{2,1,0:T(8,128)(2,1)S(1)} %get-tuple-element.122), channel_id=1, source_target_pairs={{0,16},{2,18},{4,20},{6,22},{8,24},{10,26},{12,28},{14,30},{16,0},... | collective-permute-start | bytes 786440 | tf_op jit(solution)/shard_map/ppermute | solution.py:569
  435.1 15.6 %collective-permute-start.22 = (bf16[2,64,1024]{2,1,0:T(8,128)(2,1)S(1)}, bf16[2,64,1024]{2,1,0:T(8,128)(2,1)S(1)}, u32[]{:S(2)}, u32[]{:S(2)}) collective-permute-start(bf16[2,64,1024]{2,1,0:T(8,128)(2,1)S(1)} %get-tuple-element.121), channel_id=1, source_target_pairs={{0,24},{2,26},{4,28},{6,30},{8,0},{10,2},{12,4},{14,6},{16,8},{18,... | collective-permute-start | bytes 786440 | tf_op jit(solution)/shard_map/ppermute | solution.py:569
  437.1 17.8 %copy-start.12 = (f32[1024]{0:T(1024)}, f32[1024]{0:T(1024)S(1)}, u32[]{:S(2)}) copy-start(f32[1024]{0:T(1024)S(1)} %get-tuple-element.199) | copy-start | bytes 12292
Sparse Core Ops, SparseCore 0:
  10.7 53.0 all-gather.2
  66.0 72.8 all-gather.4

commit v3 on v2

v3 whole, which is shorter than its diff:
```python
import functools

import jax
import jax.numpy as jnp
from jax import lax
from jax.experimental import pallas as pl
from jax.experimental.pallas import tpu as pltpu
from jax.sharding import PartitionSpec as P

f32, bf16 = jnp.float32, jnp.bfloat16
HS = 64
ROT = 16
LEN = 2048
EPS = 1e-05
NEG = -1e30
VMEM_LIMIT = 60 << 20
PIECES = 2
ERFC = (
    0.22567586308569043,
    0.22566953354787173,
    0.20784372127485384,
    0.1685348386069925,
    0.14145750936579315,
    -0.005660950942278366,
    0.16914715407444447,
    -0.18293900460081808,
    0.050271460956987875,
)


def dot(a, b, ca=1, cb=0):
    return lax.dot_general(a, b, (((ca,), (cb,)), ((), ())), preferred_element_type=f32)


def gelu_parts(x):
    t = pl.reciprocal(1.0 + (0.4 * 0.5**0.5) * jnp.abs(x))
    poly = jnp.full_like(t, ERFC[-1])
    for c in ERFC[-2::-1]:
        poly = poly * t + c
    e = jnp.exp(-0.5 * (x * x))
    tail = (0.5 * t) * poly * e
    cdf = jnp.where(x < 0, tail, 1.0 - tail)
    return x * cdf, cdf + x * (e * 0.3989422804014327)


def call(kernel, grid, in_specs, out_specs, out_shape, scratch, flops, scalars=1, collective=None):
    size = lambda a: a.dtype.itemsize * a.size
    return lambda *args: pl.pallas_call(
        kernel,
        grid_spec=pltpu.PrefetchScalarGridSpec(num_scalar_prefetch=scalars, grid=grid, in_specs=in_specs, out_specs=out_specs, scratch_shapes=scratch),
        out_shape=out_shape,
        compiler_params=pltpu.CompilerParams(vmem_limit_bytes=VMEM_LIMIT, collective_id=collective, has_side_effects=collective is not None),
        cost_estimate=pl.CostEstimate(flops=int(flops), transcendentals=0, bytes_accessed=sum(map(size, args)) + sum(map(size, out_shape))),
    )(*args)


def held(rows, cols, col_block=0):
    return pl.BlockSpec((rows, cols), lambda *i: (0, col_block), pipeline_mode=pl.Buffered(1))


def weight_of(w2, p, half=None):
    _, rows, cols = w2.shape
    if half is not None:
        cols = cols // 2
    return pl.BlockSpec((None, rows, cols), lambda *i: (p, 0, half or 0), pipeline_mode=pl.Buffered(1))


def shape(rows, cols, dtype):
    return jax.ShapeDtypeStruct((rows, cols), dtype)


def both(rows, cols, count):
    return [
        pl.BlockSpec((rows, cols), lambda i, *s: (jnp.minimum(i, count - 1), 0)),
        pl.BlockSpec((rows, cols), lambda i, *s: (jnp.maximum(i - count, 0), 0)),
    ]


def own_order(rows, cols):
    return pl.BlockSpec((rows, cols), lambda i, *s: (i, 0))


def seq_order(rows, cols, n):
    return pl.BlockSpec((rows, cols), lambda i, shift, *s: ((i + shift[0] // rows) % n, 0))


def pick(refs, count):
    return jnp.where(pl.program_id(0) < count, refs[0][...], refs[1][...])


def put(refs, count, value):
    for ref, here in zip(refs, (pl.program_id(0) < count, pl.program_id(0) >= count)):

        @pl.when(here)
        def _():
            ref[...] = value


def at_first():
    return pl.when(pl.program_id(0) == 0)


def at_last():
    return pl.when(pl.program_id(0) == pl.num_programs(0) - 1)


def block_order(j):
    f = lax.axis_index("fsdp")
    z, x, core = lax.div(f, 4), lax.rem(lax.div(f, 2), 2), lax.rem(f, 2)
    other_core, other_x, k = 1 - j // 8, 1 - j // 4 % 2, j % 4
    x = 1 - x if other_x else x
    core = 1 - core if other_core else core
    return lax.rem(z + k, 4) * 4 + x * 2 + core


def put_blocks(fsdp, refs, acc):
    size, wide = acc.shape[0] // fsdp, acc.shape[1] // PIECES
    for j in range(fsdp):
        rows = pl.ds(pl.multiple_of(block_order(j) * size, size), size) if fsdp == 16 else slice(j * size, (j + 1) * size)
        at = j % (fsdp // 2) * size
        for p in range(PIECES):
            refs[j // (fsdp // 2)][p, at : at + size, :] = acc[rows, p * wide : (p + 1) * wide].astype(bf16)


def pieces(d, cols):
    dims = (PIECES, d // 2, cols // PIECES)
    return pl.BlockSpec(dims, lambda *i: (0, 0, 0), pipeline_mode=pl.Buffered(1)), jax.ShapeDtypeStruct(dims, bf16)


def neighbours():
    f, t = lax.axis_index("fsdp"), lax.axis_index("tp")
    core, x = lax.rem(f, 2), lax.rem(lax.div(f, 2), 2)
    around = [(lax.rem(f + 4 * k, 16), t) for k in range(1, 4)]
    z_pair = (f + 4 - 8 * lax.rem(lax.div(f, 4), 2), t)
    return {"core": (f + 1 - 2 * core, t), "x": (f + 2 - 4 * x, t), "y": (f, 1 - t), "z": around, "z_pair": z_pair}


def greet(to):
    barrier = pltpu.get_barrier_semaphore()
    peers = [to["core"], to["x"], to["y"], *to["z"]]
    for peer in peers:
        pl.semaphore_signal(barrier, inc=1, device_id=peer, device_id_type=pl.DeviceIdType.MESH)
    pl.semaphore_wait(barrier, len(peers))


def remote(src, dst, sems, at, peer):
    return pltpu.make_async_remote_copy(
        src_ref=src, dst_ref=dst, send_sem=sems[0].at[at], recv_sem=sems[1].at[at], device_id=peer, device_id_type=pl.DeviceIdType.MESH
    )


def sem_pair(count):
    return [pltpu.SemaphoreType.DMA((count,)), pltpu.SemaphoreType.DMA((count,))]


class Reduce:
    def __init__(self, send, keep, out, scratch, to):
        self.send, self.keep, self.out, self.to = send, keep, out, to
        self.got, self.send2, self.got2, self.send3, self.got3, *sems = scratch
        self.sems = [sems[0:2], sems[2:4], sems[4:6]]
        self.count, rows, self.wide = self.got.shape
        self.rows = rows // 8

    @staticmethod
    def scratch(d, cols, count=PIECES):
        rows, wide = d // 16, cols // count
        buffer = lambda n: pltpu.VMEM((count, n * rows, wide), bf16)
        return [buffer(8), buffer(4), buffer(4), buffer(3), buffer(3)] + sem_pair(count) + sem_pair(count) + sem_pair(3 * count)

    def block(self, j):
        return slice(j * self.rows, (j + 1) * self.rows)

    def emit(self, p, total, add=False):
        if len(self.out.shape) == 2:
            self.out[:, self.cols(p)] = total + self.out[:, self.cols(p)] if add else total
            return
        width = self.out.shape[2]
        for r in range(self.wide // width):
            at, here = p * (self.wide // width) + r, total[:, r * width : (r + 1) * width]
            self.out[at] = here + self.out[at] if add else here

    def cols(self, p):
        return slice(p * self.wide, (p + 1) * self.wide)

    def copy1(self, p):
        return remote(self.send.at[p], self.got.at[p], self.sems[0], p, self.to["core"])

    def copy2(self, p):
        return remote(self.send2.at[p], self.got2.at[p], self.sems[1], p, self.to["x"])

    def copies3(self, p):
        cut = lambda ref, k: ref.at[p, self.block(k)]
        return [remote(cut(self.send3, k), cut(self.got3, k), self.sems[2], 3 * p + k, self.to["z"][k]) for k in range(3)]

    def across_core(self, p):
        self.copy1(p).start()

    def across_x(self, p):
        self.copy1(p).wait()
        for j in range(4):
            self.send2[p, self.block(j)] = (self.keep(p, j) + self.got[p, self.block(j)].astype(f32)).astype(bf16)
        self.copy2(p).start()

    def along_z(self, p):
        self.copy2(p).wait()
        for k in (1, 2, 3, 0):
            total = self.keep(p, 4 + k) + self.got[p, self.block(4 + k)].astype(f32) + self.got2[p, self.block(k)].astype(f32)
            if k:
                self.send3[p, self.block(k - 1)] = total.astype(bf16)
            else:
                self.emit(p, total)
        for copy in self.copies3(p):
            copy.start()

    def end(self, p):
        for copy in self.copies3(p):
            copy.wait()
        got = [self.got3[p, self.block(k)].astype(f32) for k in range(3)]
        self.emit(p, got[0] + got[1] + got[2], add=True)


def kept(ref, d):
    rows = d // 16
    return lambda p, j: ref[p, j * rows : (j + 1) * rows].astype(f32)


class SumAll:
    def __init__(self, parts, got, sems, to):
        self.parts, self.got, self.sems = parts, got, sems
        self.peers = [to["core"], to["x"], to["z"][1], to["z_pair"], to["y"]]

    def copy(self, i):
        return remote(self.parts.at[i], self.got.at[i], self.sems, i, self.peers[i])

    def start(self, i):
        self.copy(i).start()

    def turn(self, i):
        self.copy(i).wait()
        self.parts[i + 1] = self.parts[i] + self.got[i]
        self.copy(i + 1).start()

    def end(self, rows_over_tp):
        last = len(self.peers) - 1
        self.copy(last).wait()
        row = lax.broadcasted_iota(jnp.int32, self.parts.shape[1:], 0)
        return self.parts[last] + jnp.where(row < rows_over_tp, self.got[last], 0.0)


def at_step(i):
    return pl.when(pl.program_id(0) == i)


def turn(y, cos, sin_up, sin_down):
    width = y.shape[1]
    half = ROT // 2
    return y * cos + pltpu.roll(y, width - half, 1) * sin_up + pltpu.roll(y, half, 1) * sin_down


def norms(x, vec, n1_ref, n2_ref, st_ref):
    x = x.astype(f32)
    mean = jnp.mean(x, axis=1, keepdims=True)
    centred = x - mean
    rstd = lax.rsqrt(jnp.mean(centred * centred, axis=1, keepdims=True) + EPS)
    normal = centred * rstd
    st_ref[:, 0:1] = mean
    st_ref[:, 1:2] = rstd
    n1 = (normal * vec[0][...] + vec[1][...]).astype(bf16)
    n1_ref[...] = n1
    n2_ref[...] = (normal * vec[2][...] + vec[3][...]).astype(bf16)
    return n1


def project(part, n1, w, b_ref, tables):
    y = dot(n1, w) + b_ref[part : part + 1, :]
    if part < 2:
        y = turn(y, *[jnp.concatenate([t] * (y.shape[1] // 128), axis=1) for t in tables])
    if part == 0:
        y = y * HS**-0.5
    return y.astype(bf16)


def qkv_kernel(shift, x_ref, y_ref, v0_ref, v1_ref, v2_ref, v3_ref, w_ref, b_ref, c_ref, sa_ref, sb_ref, n1_ref, n2_ref, st_ref, q_ref, k_ref, v_ref, *, count):
    n1 = norms(pick((x_ref, y_ref), count), [v0_ref, v1_ref, v2_ref, v3_ref], n1_ref, n2_ref, st_ref)
    width = q_ref.shape[1]
    for part, ref in enumerate((q_ref, k_ref, v_ref)):
        ref[...] = project(part, n1, w_ref[:, part * width : (part + 1) * width], b_ref, [c_ref[...], sa_ref[...], sb_ref[...]])


def qkv_call(shift, x, vec, w1, bias, tables, width, rows=256):
    d = x[0].shape[1]
    count = x[0].shape[0] // rows
    n = count + x[1].shape[0] // rows
    g = n * rows
    table = pl.BlockSpec((rows, 128), lambda i, shift: (((i + shift[0] // rows) % n) % (LEN // rows), 0))
    return call(
        functools.partial(qkv_kernel, count=count),
        (n,),
        both(rows, d, count) + [held(1, d)] * 4 + [held(d, 3 * width), held(3, width), table, table, table],
        [own_order(rows, d), own_order(rows, d), own_order(rows, 2)] + [seq_order(rows, width, n)] * 3,
        [shape(g, d, bf16), shape(g, d, bf16), shape(g, 2, f32)] + [shape(g, width, bf16)] * 3,
        [],
        6 * g * d * width,
    )(shift, *x, *vec, w1, bias, *tables)


def context_grad_kernel(shift, g_ref, w_ref, do_ref):
    do_ref[...] = dot(g_ref[...], w_ref[...]).astype(bf16)


def context_grad_call(shift, grads, w1, width, rows=512):
    g, d = grads.shape
    return call(
        context_grad_kernel,
        (g // rows,),
        [own_order(rows, d), held(d, width, 3)],
        [own_order(rows, width)],
        [shape(g, width, bf16)],
        [],
        2 * g * d * width,
    )(shift, grads, w1)[0]


def attend(i, q_all, do_all, k_ref, v_ref, dk_sum, dv_sum, tables, block):
    outs, dqs = [], []
    parts = [slice(j * block, (j + 1) * block) for j in range(i + 1)]
    for h in range(q_all.shape[1] // HS):
        lanes = slice(h * HS, (h + 1) * HS)
        q, do = q_all[:, lanes], do_all[:, lanes]
        scores = [dot(k_ref[rows, lanes], q, 1, 1) for rows in parts]
        key_pos = lax.broadcasted_iota(jnp.int32, (block, block), 0)
        query_pos = lax.broadcasted_iota(jnp.int32, (block, block), 1)
        scores[i] = jnp.where(key_pos <= query_pos, scores[i], NEG)
        top = functools.reduce(jnp.maximum, [jnp.max(s, axis=0, keepdims=True) for s in scores])
        weights = [jnp.exp(s - top) for s in scores]
        total = functools.reduce(jnp.add, [jnp.sum(w, axis=0, keepdims=True) for w in weights])
        scale = 1.0 / total
        weights = [w * scale for w in weights]
        low = [w.astype(bf16) for w in weights]
        mixed = functools.reduce(jnp.add, [dot(v_ref[rows, lanes], low[j], 0, 0) for j, rows in enumerate(parts)])
        do_t = do.astype(f32).T
        delta = jnp.sum(mixed * do_t, axis=0, keepdims=True)
        do_t = do_t.astype(bf16)
        q_t = q.astype(f32).T.astype(bf16)
        dq = 0.0
        for j, rows in enumerate(parts):
            prob_grad = dot(v_ref[rows, lanes], do, 1, 1)
            score_grad = (weights[j] * (prob_grad - delta)).astype(bf16)
            dv_sum[lanes, rows] += dot(do_t, low[j], 1, 1)
            dk_sum[lanes, rows] += dot(q_t, score_grad, 1, 1)
            dq = dq + dot(k_ref[rows, lanes], score_grad, 0, 0)
        outs.append(mixed.T)
        dqs.append(dq.T)
    dq = turn_back(jnp.concatenate(dqs, axis=1) * HS**-0.5, tables, parts[i])
    return jnp.concatenate(outs, axis=1).astype(bf16), dq.astype(bf16)


def turn_back(y, tables, rows):
    cos, sin_up, sin_down = (t[rows, :] for t in tables)
    return turn(y, cos, -sin_up, -sin_down)


def put_sums(dk_ref, dv_ref, dk_sum, dv_sum, tables, block):
    for i in range(LEN // block):
        rows = slice(i * block, (i + 1) * block)
        dk_ref[rows, :] = turn_back(dk_sum[:, rows].T, tables, rows).astype(bf16)
        dv_ref[rows, :] = dv_sum[:, rows].T.astype(bf16)


def attention_kernel(q_ref, k_ref, v_ref, do_ref, c_ref, sa_ref, sb_ref, o_ref, dq_ref, dk_ref, dv_ref, dk_sum, dv_sum, *, block):
    step = pl.program_id(2)
    tables = (c_ref, sa_ref, sb_ref)

    @pl.when(step == 0)
    def _():
        dk_sum[...] = jnp.zeros_like(dk_sum)
        dv_sum[...] = jnp.zeros_like(dv_sum)

    for i in range(LEN // block):

        @pl.when(step == i)
        def _():
            o_ref[...], dq_ref[...] = attend(i, q_ref[...], do_ref[...], k_ref, v_ref, dk_sum, dv_sum, tables, block)

    @pl.when(step == pl.num_programs(2) - 1)
    def _():
        put_sums(dk_ref, dv_ref, dk_sum, dv_sum, tables, block)


def attention_call(q, k, v, do, tables, block=512):
    g, width = q.shape
    seqs, pairs, count = g // LEN, width // 128, LEN // block
    one = pl.BlockSpec((block, 128), lambda s, h, i: (s * count + i, h))
    whole = pl.BlockSpec((LEN, 128), lambda s, h, i: (s, h))
    return call(
        functools.partial(attention_kernel, block=block),
        (seqs, pairs, count),
        [one, whole, whole, one] + [held(LEN, 128)] * 3,
        [one, one, whole, whole],
        [shape(g, width, bf16)] * 4,
        [pltpu.VMEM((128, LEN), f32), pltpu.VMEM((128, LEN), f32)],
        24 * g * LEN * width,
        0,
    )(q, k, v, do, *tables)


ROWS, BLOCK = 256, 512


INVERSE = [10000.0 ** (-2.0 * j / ROT) for j in range(ROT // 2)]


def put_tables(cos_ref, up_ref, down_ref):
    half = ROT // 2
    lane = lax.rem(lax.broadcasted_iota(jnp.int32, (ROWS, 128), 1), HS)
    inverse = functools.reduce(lambda a, j: jnp.where(lax.rem(lane, half) == j, INVERSE[j], a), range(half), jnp.zeros((ROWS, 128), f32))
    for i in range(LEN // ROWS):
        rows = slice(i * ROWS, (i + 1) * ROWS)
        position = (lax.broadcasted_iota(jnp.int32, (ROWS, 128), 0) + i * ROWS).astype(f32)
        angle = position * inverse
        cos, sin = jnp.cos(angle), jnp.sin(angle)
        cos_ref[rows, :] = jnp.where(lane < ROT, cos, 1.0)
        up_ref[rows, :] = jnp.where(lane < half, -sin, 0.0)
        down_ref[rows, :] = jnp.where(jnp.logical_and(lane >= half, lane < ROT), sin, 0.0)


class Gather:
    def __init__(self, all_ref, piece, sems, to):
        self.all, self.piece, self.to = all_ref, piece, to
        self.sems = [sems[2 * i : 2 * i + 2] for i in range(3)]
        f = lax.axis_index("fsdp")
        self.z, self.x, self.core = lax.div(f, 4), lax.rem(lax.div(f, 2), 2), lax.rem(f, 2)

    @staticmethod
    def scratch(count):
        return sem_pair(3 * count) + sem_pair(count) + sem_pair(count)

    def copies_z(self, p):
        mine = self.all.at[p, self.z, self.x, self.core]
        return [remote(self.piece(p), mine, self.sems[0], 3 * p + k, self.to["z"][k]) for k in range(3)]

    def copy_x(self, p):
        mine = self.all.at[p, :, self.x, self.core]
        return remote(mine, mine, self.sems[1], p, self.to["x"])

    def copy_core(self, p):
        mine = self.all.at[p, :, :, self.core]
        return remote(mine, mine, self.sems[2], p, self.to["core"])

    def along_z(self, p):
        for copy in self.copies_z(p):
            copy.start()

    def across_x(self, p):
        for copy in self.copies_z(p):
            copy.wait()
        self.copy_x(p).start()

    def across_core(self, p):
        self.copy_x(p).wait()
        self.copy_core(p).start()

    def end(self, p):
        self.copy_core(p).wait()


def choose(own, out_ref, own_ref, others):
    @pl.when(own)
    def _():
        out_ref[...] = own_ref[...]

    @pl.when(jnp.logical_not(own))
    def _():
        out_ref[...] = others()


def head_kernel(
    x_ref, x_hbm, g_ref, g_hbm, project_ref, dense_ref, expand_ref, shrink_ref, v0_ref, v1_ref, v2_ref, v3_ref, b_ref,
    n1_ref, n2_ref, st_ref, o_ref, dq_ref, dk_ref, dv_ref, w_ref, x_other, g_other, w2_ref,
    w, x_got, g_got, q_all, k_all, v_all, do_all, dk_sum, dv_sum, c_ref, sa_ref, sb_ref, local_sem, *sems, own, pairs,
):
    step = pl.program_id(0)
    count = own // ROWS
    blocks = own // BLOCK
    n = 2 * count
    t = lax.axis_index("tp")
    to = neighbours()
    tables = (c_ref, sa_ref, sb_ref)
    width = w.shape[-1]
    d = w.shape[1] * w.shape[2] * w.shape[3] * w.shape[4]
    lanes = lambda p: slice(p * width, (p + 1) * width)
    weight = lambda p: w[p].reshape(d, width)
    x_sems, g_sems, sems = sems[0:2], sems[2:4], sems[4:]
    rows_of = lambda ref, i, size: ref.at[pl.ds(i * size, size)]
    x_copy = lambda i: remote(rows_of(x_hbm, i, ROWS), x_got.at[i], x_sems, i, to["y"])
    g_copy = lambda i: remote(rows_of(g_hbm, i, BLOCK), g_got.at[i], g_sems, i, to["y"])
    gather1 = Gather(w, lambda p: dense_ref if p == 3 else project_ref.at[p], sems[:6], to)
    gather2 = Gather(w2_ref, lambda p: (expand_ref, shrink_ref)[p], sems[6:], to)
    own_copy = lambda p: pltpu.make_async_copy(gather2.piece(p), w2_ref.at[p, gather2.z, gather2.x, gather2.core], local_sem.at[p])

    @at_step(0)
    def _():
        greet(to)
        for i in range(count):
            x_copy(i).start()
        for p in range(4):
            gather1.along_z(p)
            w[p, gather1.z, gather1.x, gather1.core] = gather1.piece(p)[...]
        dk_sum[...] = jnp.zeros_like(dk_sum)
        dv_sum[...] = jnp.zeros_like(dv_sum)
        put_tables(*tables)
        for p in range(4):
            gather1.across_x(p)
        for p in range(4):
            gather1.across_core(p)
        for p in range(2):
            own_copy(p).start()
            gather2.along_z(p)
        for p in range(4):
            gather1.end(p)

    def pass_on(p):
        own_copy(p).wait()
        gather2.across_x(p)

    for first, second, what, p in ((5, 1, pass_on, 0), (8, 3, pass_on, 1), (9, 5, gather2.across_core, 0), (13, 8, gather2.across_core, 1)):
        pl.when(step == n + jnp.where(t == 0, first, second))(functools.partial(what, p))

    @at_step(n + 2 * blocks * pairs - 1)
    def _():
        for p in range(2):
            gather2.end(p)

    for i in range(count):

        @at_step(count + i)
        def _():
            x_copy(i).wait()
            if i >= count - blocks:
                g_copy(i - count + blocks).start()

    @pl.when(step < n)
    def _():
        choose(step < count, x_other, x_ref, lambda: x_got[step - count])
        n1 = norms(x_other[...], [v0_ref, v1_ref, v2_ref, v3_ref], n1_ref, n2_ref, st_ref)
        at = pl.ds(pl.multiple_of(lax.rem(step * ROWS + t * own, 2 * own), ROWS), ROWS)
        here = [r[at, :] for r in tables]
        for part, ref in enumerate((q_all, k_all, v_all)):
            y = project(part, n1, weight(part), b_ref, here)
            for p in range(pairs):
                ref[p, at, :] = y[:, p * 128 : (p + 1) * 128]

    later = step - n
    turn_of, pair = lax.div(later, pairs), lax.rem(later, pairs)
    block = lax.rem(turn_of + t * blocks, 2 * blocks)

    @pl.when(jnp.logical_and(later >= 0, pair == 0))
    def _():
        for i in range(blocks):

            @pl.when(turn_of == blocks + i)
            def _():
                g_copy(i).wait()

        choose(turn_of < blocks, g_other, g_ref, lambda: g_got[turn_of - blocks])
        y = dot(g_other[...], weight(3)).astype(bf16)
        for p in range(pairs):
            do_all[p] = y[:, p * 128 : (p + 1) * 128]

    for i in range(2 * blocks):

        @pl.when(jnp.logical_and(later >= 0, block == i))
        def _():
            q = q_all[pair, i * BLOCK : (i + 1) * BLOCK, :]
            o_ref[...], dq_ref[...] = attend(i, q, do_all[pair], k_all.at[pair], v_all.at[pair], dk_sum.at[pair], dv_sum.at[pair], tables, BLOCK)

    @pl.when(turn_of == 2 * blocks - 1)
    def _():
        put_sums(dk_ref, dv_ref, dk_sum.at[pair], dv_sum.at[pair], tables, BLOCK)

    @at_step(n)
    def _():
        for p in range(4):
            w_ref[:, lanes(p)] = weight(p)


def head_call(x, grads, project, dense, expand, shrink, vec, bias):
    own, d = x.shape
    (part, width), hidden = dense.shape, shrink.shape[1]
    pairs, g = width // 128, 2 * own
    n, blocks = g // ROWS, own // BLOCK
    count = n // 2
    last = lambda i, top: jnp.clip(i, 0, top - 1)
    rows = lambda c: pl.BlockSpec((ROWS, c), lambda i: (last(i, n), 0))
    other_rows = pl.BlockSpec((ROWS, d), lambda i: (last(i - count, count), 0))
    own_rows = pl.BlockSpec((ROWS, d), lambda i: (last(i, count), 0))
    at = lambda i: last(lax.div(jnp.maximum(i - n, 0), pairs), 2 * blocks)
    pair = lambda i: lax.rem(jnp.maximum(i - n, 0), pairs)
    out = pl.BlockSpec((BLOCK, 128), lambda i: (at(i), pair(i)))
    sums = pl.BlockSpec((LEN, 128), lambda i: (0, jnp.where(at(i) == 2 * blocks - 1, pair(i), 0)))
    any_spec = pl.BlockSpec(memory_space=pl.ANY)
    head_rows = lambda: pltpu.VMEM((pairs, LEN, 128), bf16)
    head_sums = lambda: pltpu.VMEM((pairs, 128, LEN), f32)
    return call(
        functools.partial(head_kernel, own=own, pairs=pairs),
        (n + 2 * blocks * pairs,),
        [own_rows, any_spec, pl.BlockSpec((BLOCK, d), lambda i: (last(at(i), blocks), 0)), any_spec]
        + [pl.BlockSpec(project.shape, lambda i: (0, 0, 0), pipeline_mode=pl.Buffered(1))]
        + [held(*a.shape) for a in (dense, expand, shrink, *vec, bias)],
        [rows(d), rows(d), rows(2), out, out, sums, sums, held(d, 4 * width), other_rows]
        + [pl.BlockSpec((BLOCK, d), lambda i: (last(at(i) - blocks, blocks), 0)), any_spec],
        [shape(g, d, bf16), shape(g, d, bf16), shape(g, 2, f32)]
        + [shape(g, width, bf16)] * 4
        + [shape(d, 4 * width, bf16), shape(own, d, bf16), shape(own, d, bf16), jax.ShapeDtypeStruct((2, 4, 2, 2, part, hidden), bf16)],
        [
            pltpu.VMEM((4, 4, 2, 2, part, width), bf16),
            pltpu.VMEM((count, ROWS, d), bf16),
            pltpu.VMEM((blocks, BLOCK, d), bf16),
            head_rows(),
            head_rows(),
            head_rows(),
            pltpu.VMEM((pairs, BLOCK, 128), bf16),
            head_sums(),
            head_sums(),
        ]
        + [pltpu.VMEM((LEN, 128), f32)] * 3
        + [pltpu.SemaphoreType.DMA((2,))]
        + sem_pair(count)
        + sem_pair(blocks)
        + Gather.scratch(4)
        + Gather.scratch(2),
        6 * g * d * width + 24 * g * LEN * width,
        0,
        collective=2,
    )(x, x, grads, grads, project, dense, expand, shrink, *vec, bias)


def normal_of(refs, st_ref, count):
    return (pick(refs, count).astype(f32) - st_ref[:, 0:1]) * st_ref[:, 1:2]


def project_back_kernel(shift, dq_ref, dk_ref, dv_ref, ctx_ref, n1_ref, x_ref, y_ref, st_ref, go_ref, gt_ref, gain_ref, w_ref, s_ref, send_ref, keep_ref, cols_ref, bias_ref, acc, *, count, fsdp):
    @at_first()
    def _():
        acc[...] = jnp.zeros_like(acc)
        cols_ref[...] = jnp.zeros_like(cols_ref)
        bias_ref[...] = jnp.zeros_like(bias_ref)

    n1 = n1_ref[...]
    width = dk_ref.shape[1]
    s = 0.0
    for part, joined in enumerate((dq_ref[...], dk_ref[...], dv_ref[...])):
        lanes = slice(part * width, (part + 1) * width)
        bias_ref[part : part + 1, :] += jnp.sum(joined.astype(f32), axis=0, keepdims=True)
        s = s + dot(joined, w_ref[:, lanes], 1, 1)
        acc[:, lanes] += dot(n1, joined, 0, 0)
    acc[:, 3 * width :] += dot(pick((go_ref, gt_ref), count), ctx_ref[...], 0, 0)
    normal = normal_of((x_ref, y_ref), st_ref, count)
    cols_ref[0:1, :] += jnp.sum(s * normal, axis=0, keepdims=True)
    cols_ref[1:2, :] += jnp.sum(s, axis=0, keepdims=True)
    s_ref[...] = s * gain_ref[...]

    @at_last()
    def _():
        put_blocks(fsdp, (send_ref, keep_ref), acc)


def project_back_call(shift, fsdp, dq, dk, dv, ctx, n1, x, st, grads, vec, w1, rows=256):
    g, d = n1.shape
    width = dk.shape[1]
    n, count = g // rows, x[0].shape[0] // rows
    return call(
        functools.partial(project_back_kernel, count=count, fsdp=fsdp),
        (n,),
        [own_order(rows, width), *[seq_order(rows, width, n)] * 2, own_order(rows, width), own_order(rows, d)]
        + both(rows, d, count)
        + [own_order(rows, 2)]
        + both(rows, d, count)
        + [held(1, d), held(d, 3 * width)],
        [own_order(rows, d), *[pieces(d, 4 * width)[0]] * 2, held(2, d), held(3, width)],
        [shape(g, d, f32), *[pieces(d, 4 * width)[1]] * 2, shape(2, d, f32), shape(3, width, f32)],
        [pltpu.VMEM((d, 4 * width), f32)],
        14 * g * d * width,
    )(shift, dq, dk, dv, ctx, n1, *x, st, *grads, vec[0], w1)


def feed_forward_kernel(n2_ref, go_ref, gt_ref, ctx_ref, we_ref, ws_ref, wd_ref, be_ref, *refs, count, fsdp, fast):
    if fast:
        x_ref, bias_ref, d_send, d_keep, gp_ref, out_ref, send_ref, keep_ref, dw1_ref, acc, to_owner, from_other, *scratch = refs
        to = neighbours()
        reduce = Reduce(d_send, kept(d_keep, acc.shape[0]), dw1_ref, scratch[2:], to)
        row_copy = lambda b: remote(to_owner.at[b], from_other.at[b], scratch[:2], b, to["y"])
    else:
        gp_ref, out_ref, others_ref, send_ref, keep_ref, acc = refs
    step = pl.program_id(0)

    @at_first()
    def _():
        acc[...] = jnp.zeros_like(acc)
        if fast:
            greet(to)
            for p in range(PIECES):
                reduce.across_core(p)

    if fast:
        for at, what in ((1, "x"), (3, 0), (5, 1), (7, "end")):

            @at_step(at)
            def _():
                for p in range(PIECES) if what in ("x", "end") else [what]:
                    {"x": reduce.across_x, "end": reduce.end}.get(what, reduce.along_z)(p)

        for b in range(count):

            @at_step(b + 1)
            def _():
                row_copy(b).start()

    own = step >= count
    n2, g = n2_ref[...], jnp.where(own, go_ref[...], gt_ref[...])
    branch = dot(ctx_ref[...], wd_ref[...], 1, 1)
    act, slope = gelu_parts(dot(n2, we_ref[...]) + be_ref[...])
    act = act.astype(bf16)
    gp_ref[...] = slope.astype(bf16)
    branch = branch + dot(act, ws_ref[...], 1, 1)
    acc[...] += dot(g, act, 0, 0)
    if fast:

        @pl.when(jnp.logical_not(own))
        def _():
            to_owner[step] = branch.astype(bf16)

        for b in range(count):

            @at_step(b + count)
            def _():
                row_copy(b).wait()
                out_ref[...] = (x_ref[...].astype(f32) + (branch + from_other[b].astype(f32)) + bias_ref[...]).astype(bf16)

    else:
        put((others_ref, out_ref), count, branch.astype(bf16))

    @at_last()
    def _():
        put_blocks(fsdp, (send_ref, keep_ref), acc)


def feed_forward_call(fsdp, n2, grads, ctx, w2, w1, be, more=None, rows=256):
    g, d = n2.shape
    hidden, width = w2.shape[2], ctx.shape[1]
    own = grads[0].shape[0]
    n = g // rows
    count = own // rows if more else (g - own) // rows
    first = lambda c: pl.BlockSpec((rows, c), lambda i, *s: (jnp.minimum(i, count - 1), 0))
    second = lambda c: pl.BlockSpec((rows, c), lambda i, *s: (jnp.maximum(i - count, 0), 0))
    turned = lambda c: pl.BlockSpec((rows, c), lambda i, *s: ((i + own // rows) % n, 0))
    ins = [turned(d), second(d), first(d), turned(width), weight_of(w2, 0), weight_of(w2, 1), held(d, width, 3), held(1, hidden)]
    half = pieces(d, hidden)
    acc = pltpu.VMEM((d, hidden), f32)
    flops = g * d * (6 * hidden + 2 * width)
    kernel = functools.partial(feed_forward_kernel, count=count, fsdp=fsdp, fast=bool(more))
    args = (n2, *grads, ctx, w2, w2, w1, be)
    if not more:
        outs = [turned(hidden), second(d), first(d), half[0], half[0]]
        shapes = [shape(g, hidden, bf16), shape(own, d, bf16), shape(g - own, d, bf16), half[1], half[1]]
        return call(kernel, (n,), ins, outs, shapes, [acc], flops, 0)(*args)
    part = d // 16
    ins += [second(d), held(1, d), pl.BlockSpec(memory_space=pl.ANY), pieces(d, 4 * width)[0]]
    parts = (4, part, width)
    outs = [turned(hidden), second(d), half[0], half[0], pl.BlockSpec(parts, lambda i: (0, 0, 0), pipeline_mode=pl.Buffered(1))]
    shapes = [shape(g, hidden, bf16), shape(own, d, bf16), half[1], half[1], jax.ShapeDtypeStruct(parts, f32)]
    rows_buffer = pltpu.VMEM((count, rows, d), bf16)
    scratch = [acc, rows_buffer, rows_buffer] + sem_pair(count) + Reduce.scratch(d, 4 * width)
    return call(kernel, (n,), ins, outs, shapes, scratch, flops, 0, collective=0)(*args, *more)


def feed_back_kernel(n2_ref, go_ref, gt_ref, gp_ref, s1_ref, x_ref, y_ref, st_ref, gain_ref, we_ref, ws_ref, *refs, count, last, fsdp):
    s_refs = refs[: 1 + last]
    send_ref, keep_ref, cols_ref, bias_ref, acc = refs[1 + last :]

    @at_first()
    def _():
        acc[...] = jnp.zeros_like(acc)
        cols_ref[...] = jnp.zeros_like(cols_ref)
        bias_ref[...] = jnp.zeros_like(bias_ref)

    n2, g = n2_ref[...], pick((go_ref, gt_ref), count)
    pre_grad = (dot(g, ws_ref[...]) * gp_ref[...].astype(f32)).astype(bf16)
    bias_ref[...] += jnp.sum(pre_grad.astype(f32), axis=0, keepdims=True)
    s = dot(pre_grad, we_ref[...], 1, 1)
    acc[...] += dot(n2, pre_grad, 0, 0)
    normal = normal_of((x_ref, y_ref), st_ref, count)
    cols_ref[0:1, :] += jnp.sum(s * normal, axis=0, keepdims=True)
    cols_ref[1:2, :] += jnp.sum(s, axis=0, keepdims=True)
    s = s1_ref[...] + s * gain_ref[...]
    if last:
        put(s_refs, count, s.astype(bf16))
    else:
        s_refs[0][...] = s

    @at_last()
    def _():
        put_blocks(fsdp, (send_ref, keep_ref), acc)


def feed_back_call(fsdp, n2, grads, gp, s1, x, st, vec, w2, half, last, rows=256):
    g, d = n2.shape
    hidden = gp.shape[1] // 2
    own = x[0].shape[0]
    n, count = g // rows, own // rows
    return call(
        functools.partial(feed_back_kernel, count=count, last=last, fsdp=fsdp),
        (n,),
        [own_order(rows, d)]
        + both(rows, d, count)
        + [pl.BlockSpec((rows, hidden), lambda i, *s: (i, half)), own_order(rows, d)]
        + both(rows, d, count)
        + [own_order(rows, 2), held(1, d), weight_of(w2, 0, half), weight_of(w2, 1, half)],
        (both(rows, d, count) if last else [own_order(rows, d)]) + [pieces(d, hidden)[0]] * 2 + [held(2, d), held(1, hidden)],
        ([shape(own, d, bf16), shape(g - own, d, bf16)] if last else [shape(g, d, f32)])
        + [pieces(d, hidden)[1]] * 2
        + [shape(2, d, f32), shape(1, hidden, f32)],
        [pltpu.VMEM((d, hidden), f32)],
        6 * g * d * hidden,
        0,
    )(n2, *grads, gp, s1, *x, st, vec[2], w2, w2)


TAIL = 7
LAST_PIECES = 4


def feed_back_last_kernel(
    n2_ref, go_ref, gt_ref, gp_ref, s1_ref, x_ref, y_ref, st_ref, gain_ref, we_ref, ws_ref, d_send, d_keep, cols_ref, bias_ref,
    grad_ref, dws_ref, dwe_ref, sum_ref,
    acc, to_owner, from_other, own_s, e_send, parts, parts_got, *scratch, count,
):
    n = 2 * count
    d = acc.shape[0]
    step = pl.program_id(0)
    to = neighbours()
    row_sems, sum_sems, scratch = scratch[0:2], scratch[2:4], scratch[4:]
    size = len(scratch) // 2
    shrink = Reduce(d_send, kept(d_keep, d), dws_ref, scratch[:size], to)

    def from_acc(p, j):
        rows = d // 16
        return acc[pl.ds(pl.multiple_of(block_order(j) * rows, rows), rows), expand.cols(p)]

    expand = Reduce(e_send, lambda p, j: from_acc(p, 8 + j), dwe_ref, scratch[size:], to)
    small = SumAll(parts, parts_got, sum_sems, to)
    row_copy = lambda b: remote(to_owner.at[b], from_other.at[b], row_sems, b, to["y"])
    normal = (jnp.where(step < count, y_ref[...], x_ref[...]).astype(f32) - st_ref[:, 0:1]) * st_ref[:, 1:2]

    @at_step(0)
    def _():
        acc[...] = jnp.zeros_like(acc)
        parts[0] = jnp.zeros_like(sum_ref)
        parts[0, 0:2, :] = cols_ref[...]
        wide = bias_ref.shape[1]
        for r in range(3):
            at = r * wide % d
            parts[0, 5 + r * wide // d : 6 + r * wide // d, at : at + wide] = bias_ref[r : r + 1, :]
        greet(to)
        for p in range(PIECES):
            shrink.across_core(p)

    @at_step(1)
    def _():
        for p in range(PIECES):
            shrink.across_x(p)

    for p, at in enumerate((4, 6)):
        pl.when(step == at)(functools.partial(shrink.along_z, p))
    for b in range(count):

        @at_step(b + 1)
        def _():
            row_copy(b).start()

    @pl.when(step < n)
    def _():
        own = step >= count
        n2, g = n2_ref[...], jnp.where(own, go_ref[...], gt_ref[...])
        pre_grad = (dot(g, ws_ref[...]) * gp_ref[...].astype(f32)).astype(bf16)
        bias = jnp.sum(pre_grad.astype(f32), axis=0, keepdims=True)
        for r in range(pre_grad.shape[1] // d):
            parts[0, 7 + r : 8 + r, :] += bias[:, r * d : (r + 1) * d]
        s = dot(pre_grad, we_ref[...], 1, 1)
        acc[...] += dot(n2, pre_grad, 0, 0)
        parts[0, 2:3, :] += jnp.sum(s * normal, axis=0, keepdims=True)
        parts[0, 3:4, :] += jnp.sum(s, axis=0, keepdims=True)
        s = s1_ref[...] + s * gain_ref[...]

        @pl.when(own)
        def _():
            own_s[step - count] = s
            parts[0, 4:5, :] += jnp.sum(g.astype(f32), axis=0, keepdims=True)

        @pl.when(jnp.logical_not(own))
        def _():
            to_owner[step] = s.astype(bf16)

    @at_step(n)
    def _():
        small.start(0)
        for p in range(LAST_PIECES):
            for j in range(8):
                e_send[p, expand.block(j)] = from_acc(p, j).astype(bf16)
        for p in range(LAST_PIECES):
            expand.across_core(p)

    @at_step(n + 1)
    def _():
        small.turn(0)
        for p in range(LAST_PIECES):
            expand.across_x(p)

    for p in range(LAST_PIECES):

        @at_step(n + 2 + p)
        def _():
            if p < 3:
                small.turn(p + 1)
            else:
                sum_ref[...] = small.end(5)
            expand.along_z(p)

    @at_step(n + 2)
    def _():
        for p in range(PIECES):
            shrink.end(p)

    for b in range(count):

        @at_step(n + b)
        def _():
            row_copy(b).wait()
            s = own_s[b] + from_other[b].astype(f32)
            centred = s - jnp.mean(s, axis=1, keepdims=True) - normal * jnp.mean(s * normal, axis=1, keepdims=True)
            grad_ref[...] = go_ref[...].astype(f32) + st_ref[:, 1:2] * centred

    @at_step(n + TAIL - 1)
    def _():
        for p in range(LAST_PIECES):
            expand.end(p)


def feed_back_last_call(n2, grads, gp, s1, x, st, vec, w2, dws, cols, bias, rows=256):
    g, d = n2.shape
    hidden = gp.shape[1]
    own = x[0].shape[0]
    n, count = g // rows, own // rows
    part = d // 16
    first = lambda c: pl.BlockSpec((rows, c), lambda i: (jnp.minimum(i, count - 1), 0))
    second = lambda c: pl.BlockSpec((rows, c), lambda i: (jnp.where(i < n, jnp.maximum(i - count, 0), jnp.minimum(i - n, count - 1)), 0))
    turned = lambda c: pl.BlockSpec((rows, c), lambda i: (jnp.where(i < n, lax.rem(i + count, n), jnp.minimum(i - n, count - 1)), 0))
    turned_once = lambda c: pl.BlockSpec((rows, c), lambda i: (lax.rem(jnp.minimum(i, n - 1) + count, n), 0))
    ins = [turned_once(d), second(d), first(d), turned_once(hidden), turned_once(d), second(d), first(d), turned(2), held(1, d)]
    ins += [weight_of(w2, 0), weight_of(w2, 1), pl.BlockSpec(memory_space=pl.ANY), pieces(d, hidden)[0], held(2, d), held(*bias.shape)]
    small = jax.ShapeDtypeStruct((16, d), f32)
    outs = [pl.BlockSpec((rows, d), lambda i: (jnp.clip(i - n, 0, count - 1), 0)), held(part, hidden), held(part, hidden), held(*small.shape)]
    shapes = [shape(own, d, f32), shape(part, hidden, f32), shape(part, hidden, f32), shape(*small.shape, f32)]
    rows_buffer = lambda dtype: pltpu.VMEM((count, rows, d), dtype)
    sums = pltpu.VMEM((5, *small.shape), f32)
    scratch = [pltpu.VMEM((d, hidden), f32), rows_buffer(bf16), rows_buffer(bf16), rows_buffer(f32)]
    scratch += [pltpu.VMEM((LAST_PIECES, d // 2, hidden // LAST_PIECES), bf16), sums, sums]
    scratch += sem_pair(count) + sem_pair(5) + Reduce.scratch(d, hidden) + Reduce.scratch(d, hidden, LAST_PIECES)
    return call(functools.partial(feed_back_last_kernel, count=count), (n + TAIL,), ins, outs, shapes, scratch, 6 * g * d * hidden, 0, collective=1)(
        n2, *grads, gp, s1, *x, st, vec[2], w2, w2, *dws, cols, bias
    )


def rotary_tables():
    half = ROT // 2
    position = jnp.arange(LEN).astype(f32)
    inverse = 10000.0 ** (-(jnp.arange(half).astype(f32) * 2.0) / ROT)
    angle = position[:, None] * inverse[None, :]
    cos, sin = jnp.cos(angle), jnp.sin(angle)
    rest = jnp.zeros((LEN, HS - ROT), f32)
    none = jnp.zeros((LEN, half), f32)
    period = lambda *a: jnp.tile(jnp.concatenate(a, axis=1), (1, 128 // HS))
    return period(cos, cos, rest + 1.0), period(-sin, none, rest), period(none, sin, rest)


def join(a):
    return jnp.concatenate(list(a), axis=1)


def make_body(fsdp, tp):
    fast = (fsdp, tp) == (16, 2)

    def body(inputs, cotangent, first_gain, first_shift, second_gain, second_shift, project_weight, project_bias, dense_weight, dense_bias, expand_weight, expand_bias, shrink_weight, shrink_bias):
        rows, d = inputs.shape
        width = dense_weight.shape[0]
        hidden = shrink_weight.shape[0]
        part = project_weight.shape[0]
        me = lax.axis_index("tp")
        split = lambda a: (a[:rows], a[rows:])
        zero = jnp.zeros((1,), jnp.int32)
        vec = [a[None] for a in (first_gain, first_shift, second_gain, second_shift)]
        if fast:
            shift = (me * rows).astype(jnp.int32)[None]
            n1, n2, st, ctx, dq, dk, dv, w1, x, grads, w2 = head_call(
                inputs, cotangent, project_weight.transpose(1, 0, 2), dense_weight.T, expand_weight, shrink_weight.T, vec, project_bias
            )
            w2 = w2.reshape(2, d, hidden)
            x, grads = (inputs, x), (cotangent, grads)
        else:
            shift = zero
            gather = lambda a: lax.all_gather(a, "fsdp", axis=0, tiled=True)
            w1 = gather(jnp.concatenate([project_weight.reshape(part, 3 * width), dense_weight.T], axis=1))
            w2 = jnp.stack([gather(expand_weight), gather(shrink_weight.T)])
            tables = rotary_tables()
            x = split(lax.all_gather(inputs, "tp", axis=0, tiled=True))
            grads = split(lax.all_gather(cotangent, "tp", axis=0, tiled=True))
            n1, n2, st, q, k, v = qkv_call(shift, x, vec, w1, project_bias, tables, width)
            do = context_grad_call(zero, jnp.concatenate(grads), w1, width)
            ctx, dq, dk, dv = attention_call(q, k, v, do, tables)
        s, *dw1, cols1, bias1 = project_back_call(shift, fsdp, dq, dk, dv, ctx, n1, x, st, grads, vec, w1)
        out_bias = dense_bias + shrink_bias
        if fast:
            gp, output, *dws, dw1 = feed_forward_call(fsdp, n2, grads, ctx, w2, w1, expand_bias[None], (inputs, out_bias[None], *dw1))
        else:
            gp, *branch = feed_forward_call(fsdp, n2, grads, ctx, w2, w1, expand_bias[None])
            branch, dws = branch[:2], branch[2:]
        if fast:
            input_grad, dws, dwe, small = feed_back_last_call(n2, grads, gp, s, x, st, vec, w2, dws, cols1, bias1)
            cols, local = small[:5], jnp.concatenate([small[5:7].reshape(-1)[: 3 * width], small[7:9].reshape(-1)])
        else:
            s, *dwe, cols2, bias2 = feed_back_call(fsdp, n2, grads, gp, s, x, st, vec, w2, 0, False)
            *s, send, keep, cols3, bias3 = feed_back_call(fsdp, n2, grads, gp, s, x, st, vec, w2, 1, True)
            over = lambda a, axis: lax.psum_scatter(jnp.concatenate(a), axis, scatter_dimension=0, tiled=True).astype(f32)
            scatter = lambda pair: over([join(a) for a in pair], "fsdp")
            s = over(s, "tp")
            own_rows = inputs.astype(f32)
            output = (own_rows + over(branch, "tp") + out_bias).astype(bf16)
            own_st = lax.dynamic_slice_in_dim(st, me * rows, rows, 0)
            own_bias = jnp.sum(cotangent.astype(f32), axis=0, keepdims=True)
            cols = lax.psum(jnp.concatenate([cols1, cols2 + cols3, own_bias]), ("fsdp", "tp"))
            local = lax.psum(jnp.concatenate([bias1.reshape(-1), bias2.reshape(-1), bias3.reshape(-1)]), "fsdp")
            dw1 = scatter(dw1).reshape(part, 4, width).transpose(1, 0, 2)
            dws, dwe = scatter(dws), jnp.concatenate([scatter(dwe), scatter((send, keep))], axis=1)
            normal = (own_rows - own_st[:, 0:1]) * own_st[:, 1:2]
            term = own_st[:, 1:2] * (s - jnp.mean(s, axis=1, keepdims=True) - normal * jnp.mean(s * normal, axis=1, keepdims=True))
            input_grad = cotangent.astype(f32) + term
        return (
            output,
            input_grad,
            cols[0],
            cols[1],
            cols[2],
            cols[3],
            dw1[:3].transpose(1, 0, 2),
            local[: 3 * width].reshape(3, width),
            dw1[3].T,
            cols[4],
            dwe,
            local[3 * width :],
            dws.T,
            cols[4],
        )

    return body


def solution(mesh):
    rows, rep = P(("fsdp", "tp"), None), P()
    return jax.shard_map(
        make_body(mesh.shape["fsdp"], mesh.shape["tp"]),
        mesh=mesh,
        in_specs=(rows, rows, rep, rep, rep, rep, P("fsdp", None, "tp"), P(None, "tp"), P("tp", "fsdp"), rep, P("fsdp", "tp"), P("tp"), P("tp", "fsdp"), rep),
        out_specs=(rows, rows, rep, rep, rep, rep, P("fsdp", None, "tp"), P(None, "tp"), P("tp", "fsdp"), rep, P("fsdp", "tp"), P("tp"), P("tp", "fsdp"), rep),
        check_vma=False,
    )
```

time: 469 us -> 362 us (0.77); the launches traced: 462 us -> 361 us
  waiting for transfers between devices: 102 us -> 0 us
  Pallas kernels: 270 us -> 347 us
  other arithmetic: 29.8 us -> 1.3 us
  starting transfers between devices: 27.1 us -> 0 us
  between operations: 14.7 us -> 1 us
  local copies, waits for them, and re-layouts: 17.8 us -> 12.2 us
    ppermute x23 -> x0, waiting for transfers between devices: 101 us -> none  [the longest x10 41.8 us: flip(): return lax.ppermute(a, 'fsdp', [(i, i ^ bit) for i in range(16)])]
    pallas_call x9 -> x4, Pallas kernels: 270 us -> 347 us  [call(): pl.pallas_call(kernel, grid_spec=pltpu.PrefetchScalarGridSpec(num_scalar_...]
    ppermute x23 -> x0, starting transfers between devices: 27 us -> none  [the longest x9 14.7 us: along_z(): return lax.ppermute(a, 'fsdp', [(i, (i + 4 * k) % 16) for i in range(16)])]
    convert_element_type x7 -> x0, other arithmetic: 9.86 us -> none  [the longest x3 5.01 us: reduce_rows(): (a[:, rows].astype(f32) + b[:, rows].astype(f32)).astype(bf16)]
    reduce_sum x2 -> x0, other arithmetic: 7.86 us -> none  [the longest x1 4.76 us: body(): jnp.sum(own_grads, axis=0, keepdims=True)]
    another operation x9 -> x0, local copies, waits for them, and re-layouts: 6.62 us -> none  [the longest x6 6.55 us: rotary_tables(): period = lambda *a: jnp.tile(jnp.concatenate(a, axis=1), (1, 128 // HS))]
    unnamed x48 -> x19, local copies, waits for them, and re-layouts: 2.99 us -> 8.6 us
    concatenate x6 -> x0, other arithmetic: 5.42 us -> none  [the longest x1 1.88 us: body(): shard2 = jnp.concatenate([expand_weight, shrink_weight.T], axis=1)]
  transfers between devices with their start and end apart: 25 -> 0, of which waited for: 14 -> 0; matrix products, arithmetic and copies ran while one was open for 9% -> 0% of each run, Pallas kernels for 40% -> 0%
where the time goes in v3:
time: 362 us; the launch traced here: 361 us
  Pallas kernels  347 us (96%)
  local copies, waits for them, and re-layouts  12.2 us (3%)
    pallas_call x4, Pallas kernels, call(): pl.pallas_call(kernel, grid_spec=pltpu.PrefetchScalarGridSpec(num_scalar_...  347 us
    unnamed x19, local copies, waits for them, and re-layouts  8.6 us

profile of v3, /device:TPU:0, one launch (start us, length us, event | category | flops | bytes accessed | tf_op | source)
XLA Modules:
  0.0 361.2 jit_solution(14555250929146288368)
XLA Ops:
  0.6 1.3 add.3
  1.9 166.5 %shard_map.245 = (bf16[2048,1024]{1,0:T(8,128)(2,1)}, bf16[2048,1024]{1,0:T(8,128)(2,1)}, f32[2048,2]{1,0:T(8,128)}, bf16[2048,512]{1,0:T(8,128)(2,1)}, bf16[204...) custom-call(bf16[1024,1024]{1,0:T(8,128)(2,1)} %x_ref.5, ...), custom_call_target="tpu_custom_call" | custom-call | flops 57982058496 | bytes 42768384 | tf_op jit(solution)/shard_map/pallas_call | solution.py:48
  168.4 25.2 %shard_map.246 = (f32[2048,1024]{1,0:T(8,128)}, bf16[2,512,1024]{2,1,0:T(8,128)(2,1)}, bf16[2,512,1024]{2,1,0:T(8,128)(2,1)}, f32[2,1024]{1,0:T(2,128)}, f32[3,512]{1,0:T(4,128)}) custom-call(s32[1]{0:T(128)} %bitcast.10.shift, bf16[2048,512]{1,0:T(8,128)(2,1)} %get-tuple-element.44.dq_ref, bf16[2048,512]{1,0:T(8,128)(2,1)} %get-tuple-element.45.dk_ref, ...), custom_call_target="tpu_custom_call" | custom-call | flops 15032385536 | bytes 37783556 | tf_op jit(solution)/shard_map/pallas_call | solution.py:48
  193.7 74.2 %shard_map.247 = (bf16[2048,2048]{1,0:T(8,128)(2,1)}, bf16[1024,1024]{1,0:T(8,128)(2,1)}, bf16[2,512,1024]{2,1,0:T(8,128)(2,1)}, bf16[2,512,1024]{2,1,0:T(8,128)(2,1)}, f32[4,64,512]{2,1,0:T(8,128)}) custom-call(bf16[2048,1024]{1,0:T(8,128)(2,1)} %get-tuple-element.39.n2_ref, bf16[1024,1024]{1,0:T(8,128)(2,1)} %go_ref.5, ...), custom_call_target="tpu_custom_call" | custom-call | flops 27917287424 | bytes 52965376 | tf_op jit(solution)/shard_map/pallas_call | solution.py:48
  267.9 0.0 copy-start.2
  267.9 0.0 copy-start.1
  267.9 80.8 %shard_map.248 = (f32[1024,1024]{1,0:T(8,128)}, f32[64,2048]{1,0:T(8,128)}, f32[64,2048]{1,0:T(8,128)}, f32[16,1024]{1,0:T(8,128)}) custom-call(bf16[2048,1024]{1,0:T(8,128)(2,1)} %get-tuple-element.39.n2_ref, bf16[1024,1024]{1,0:T(8,128)(2,1)} %go_ref.5, bf16[1024,1024]{1,0:T(8,128)(2,1)} %get-tuple-element.40.gt_ref, ...), custom_call_target="tpu_custom_call" | custom-call | flops 25769803776 | bytes 55674880 | tf_op jit(solution)/shard_map/pallas_call | solution.py:48
  348.7 0.9 slice_bitcast_fusion.2
  349.6 1.6 fusion
  351.1 0.0 copy-start.5
  351.1 0.6 copy.30
  351.7 0.6 slice.46
  352.3 0.0 copy-done.2
  352.3 0.7 slice_bitcast_fusion.1
  353.0 0.8 slice_bitcast_fusion
  353.8 0.6 copy.36
  354.4 0.0 copy-done.1
  354.4 0.0 copy-start
  354.4 1.3 copy.37
  355.7 0.0 copy-done.5
  355.7 1.6 copy-done
  357.3 0.0 copy-start.4
  357.3 0.0 copy-start.3
  357.3 2.0 copy.38
  359.3 0.0 copy-done.4
  359.3 0.8 copy.39
  360.1 0.0 copy-done.3
  360.1 0.8 copy.40
Async XLA Ops:
  267.9 84.5 %copy-start.2 = (f32[4,64,512]{2,1,0:T(8,128)S(1)}, f32[4,64,512]{2,1,0:T(8,128)}, u32[]{:S(2)}) copy-start(f32[4,64,512]{2,1,0:T(8,128)} %get-tuple-element.61) | copy-start | bytes 1572868
  267.9 86.5 %copy-start.1 = (bf16[1024,1024]{1,0:T(8,128)(2,1)S(1)}, bf16[1024,1024]{1,0:T(8,128)(2,1)}, u32[]{:S(2)}) copy-start(bf16[1024,1024]{1,0:T(8,128)(2,1)} %get-tuple-element.113) | copy-start | bytes 6291460
  351.1 4.6 %copy-start.5 = (f32[1,1024]{1,0:T(1,128)}, f32[1,1024]{1,0:T(1,128)S(1)}, u32[]{:S(2)}) copy-start(f32[1,1024]{1,0:T(1,128)S(1)} %get-tuple-element.66) | copy-start | bytes 12292
  354.4 2.9 copy-start
  357.3 2.0 copy-start.4
  357.3 2.8 copy-start.3

commit v4 on v3

--- a/solution.py
+++ b/solution.py
@@ -323,35 +323,44 @@
 
 def attend(i, q_all, do_all, k_ref, v_ref, dk_sum, dv_sum, tables, block):
     outs, dqs = [], []
-    parts = [slice(j * block, (j + 1) * block) for j in range(i + 1)]
+    half = block // 2
+    parts = [(slice(j * block, (j + 1) * block), 0) for j in range(i)]
+    parts += [(slice(i * block, i * block + half), 0), (slice(i * block + half, (i + 1) * block), half)]
+
+    def widen(a, start, fill):
+        return a if start == 0 else jnp.concatenate([jnp.full((a.shape[0], start), fill, a.dtype), a], axis=1)
+
+    def gather(op, fill, arrays):
+        return functools.reduce(op, [widen(a, start, fill) for a, (_, start) in zip(arrays, parts)])
+
     for h in range(q_all.shape[1] // HS):
         lanes = slice(h * HS, (h + 1) * HS)
         q, do = q_all[:, lanes], do_all[:, lanes]
-        scores = [dot(k_ref[rows, lanes], q, 1, 1) for rows in parts]
-        key_pos = lax.broadcasted_iota(jnp.int32, (block, block), 0)
-        query_pos = lax.broadcasted_iota(jnp.int32, (block, block), 1)
-        scores[i] = jnp.where(key_pos <= query_pos, scores[i], NEG)
-        top = functools.reduce(jnp.maximum, [jnp.max(s, axis=0, keepdims=True) for s in scores])
-        weights = [jnp.exp(s - top) for s in scores]
-        total = functools.reduce(jnp.add, [jnp.sum(w, axis=0, keepdims=True) for w in weights])
-        scale = 1.0 / total
-        weights = [w * scale for w in weights]
+        scores = [dot(k_ref[rows, lanes], q[start:], 1, 1) for rows, start in parts]
+        for n in (i, i + 1):
+            rows, start = parts[n]
+            key_pos = lax.broadcasted_iota(jnp.int32, scores[n].shape, 0) + (rows.start - i * block)
+            query_pos = lax.broadcasted_iota(jnp.int32, scores[n].shape, 1) + start
+            scores[n] = jnp.where(key_pos <= query_pos, scores[n], NEG)
+        top = gather(jnp.maximum, NEG, [jnp.max(s, axis=0, keepdims=True) for s in scores])
+        weights = [jnp.exp(s - top[:, start:]) for s, (_, start) in zip(scores, parts)]
+        scale = 1.0 / gather(jnp.add, 0.0, [jnp.sum(w, axis=0, keepdims=True) for w in weights])
         low = [w.astype(bf16) for w in weights]
-        mixed = functools.reduce(jnp.add, [dot(v_ref[rows, lanes], low[j], 0, 0) for j, rows in enumerate(parts)])
-        do_t = do.astype(f32).T
+        mixed = gather(jnp.add, 0.0, [dot(v_ref[rows, lanes], w, 0, 0) for w, (rows, _) in zip(low, parts)]) * scale
+        do_t = do.astype(f32).T * scale
         delta = jnp.sum(mixed * do_t, axis=0, keepdims=True)
         do_t = do_t.astype(bf16)
         q_t = q.astype(f32).T.astype(bf16)
-        dq = 0.0
-        for j, rows in enumerate(parts):
-            prob_grad = dot(v_ref[rows, lanes], do, 1, 1)
-            score_grad = (weights[j] * (prob_grad - delta)).astype(bf16)
-            dv_sum[lanes, rows] += dot(do_t, low[j], 1, 1)
-            dk_sum[lanes, rows] += dot(q_t, score_grad, 1, 1)
-            dq = dq + dot(k_ref[rows, lanes], score_grad, 0, 0)
+        terms = []
+        for n, (rows, start) in enumerate(parts):
+            prob_grad = dot(v_ref[rows, lanes], do_t[:, start:])
+            score_grad = (weights[n] * (prob_grad - delta[:, start:])).astype(bf16)
+            dv_sum[lanes, rows] += dot(do_t[:, start:], low[n], 1, 1)
+            dk_sum[lanes, rows] += dot(q_t[:, start:], score_grad, 1, 1)
+            terms.append(dot(k_ref[rows, lanes], score_grad, 0, 0))
         outs.append(mixed.T)
-        dqs.append(dq.T)
-    dq = turn_back(jnp.concatenate(dqs, axis=1) * HS**-0.5, tables, parts[i])
+        dqs.append(gather(jnp.add, 0.0, terms).T)
+    dq = turn_back(jnp.concatenate(dqs, axis=1) * HS**-0.5, tables, slice(i * block, (i + 1) * block))
     return jnp.concatenate(outs, axis=1).astype(bf16), dq.astype(bf16)
 
 
@@ -511,25 +520,20 @@
         put_tables(*tables)
         for p in range(4):
             gather1.across_x(p)
-        for p in range(4):
-            gather1.across_core(p)
         for p in range(2):
             own_copy(p).start()
             gather2.along_z(p)
         for p in range(4):
+            gather1.across_core(p)
+        for p in range(4):
             gather1.end(p)
 
     def pass_on(p):
         own_copy(p).wait()
         gather2.across_x(p)
 
-    for first, second, what, p in ((5, 1, pass_on, 0), (8, 3, pass_on, 1), (9, 5, gather2.across_core, 0), (13, 8, gather2.across_core, 1)):
+    for first, second, what, p in ((5, 1, pass_on, 0), (8, 5, pass_on, 1), (11, 6, gather2.across_core, 0), (14, 12, gather2.across_core, 1)):
         pl.when(step == n + jnp.where(t == 0, first, second))(functools.partial(what, p))
-
-    @at_step(n + 2 * blocks * pairs - 1)
-    def _():
-        for p in range(2):
-            gather2.end(p)
 
     for i in range(count):
 
@@ -582,6 +586,11 @@
     def _():
         for p in range(4):
             w_ref[:, lanes(p)] = weight(p)
+
+    @at_last()
+    def _():
+        for p in range(2):
+            gather2.end(p)
 
 
 def head_call(x, grads, project, dense, expand, shrink, vec, bias):
@@ -686,7 +695,7 @@
 
 def feed_forward_kernel(n2_ref, go_ref, gt_ref, ctx_ref, we_ref, ws_ref, wd_ref, be_ref, *refs, count, fsdp, fast):
     if fast:
-        x_ref, bias_ref, d_send, d_keep, gp_ref, out_ref, send_ref, keep_ref, dw1_ref, acc, to_owner, from_other, *scratch = refs
+        x_ref, bias_ref, d_send, d_keep, gp_ref, out_ref, late_ref, late_own_ref, send_ref, keep_ref, dw1_ref, acc, to_owner, from_other, *scratch = refs
         to = neighbours()
         reduce = Reduce(d_send, kept(d_keep, acc.shape[0]), dw1_ref, scratch[2:], to)
         row_copy = lambda b: remote(to_owner.at[b], from_other.at[b], scratch[:2], b, to["y"])
@@ -710,7 +719,7 @@
                 for p in range(PIECES) if what in ("x", "end") else [what]:
                     {"x": reduce.across_x, "end": reduce.end}.get(what, reduce.along_z)(p)
 
-        for b in range(count):
+        for b in range(count - 1):
 
             @at_step(b + 1)
             def _():
@@ -726,11 +735,19 @@
     acc[...] += dot(g, act, 0, 0)
     if fast:
 
-        @pl.when(jnp.logical_not(own))
+        @pl.when(step < count - 1)
         def _():
             to_owner[step] = branch.astype(bf16)
 
-        for b in range(count):
+        @at_step(count - 1)
+        def _():
+            late_ref[...] = branch.astype(bf16)
+
+        @at_last()
+        def _():
+            late_own_ref[...] = x_ref[...].astype(f32) + (branch + bias_ref[...])
+
+        for b in range(count - 1):
 
             @at_step(b + count)
             def _():
@@ -767,10 +784,12 @@
     part = d // 16
     ins += [second(d), held(1, d), pl.BlockSpec(memory_space=pl.ANY), pieces(d, 4 * width)[0]]
     parts = (4, part, width)
-    outs = [turned(hidden), second(d), half[0], half[0], pl.BlockSpec(parts, lambda i: (0, 0, 0), pipeline_mode=pl.Buffered(1))]
-    shapes = [shape(g, hidden, bf16), shape(own, d, bf16), half[1], half[1], jax.ShapeDtypeStruct(parts, f32)]
-    rows_buffer = pltpu.VMEM((count, rows, d), bf16)
-    scratch = [acc, rows_buffer, rows_buffer] + sem_pair(count) + Reduce.scratch(d, 4 * width)
+    done = pl.BlockSpec((rows, d), lambda i: (jnp.clip(i - count, 0, count - 2), 0))
+    outs = [turned(hidden), done, held(rows, d), held(rows, d), half[0], half[0], pl.BlockSpec(parts, lambda i: (0, 0, 0), pipeline_mode=pl.Buffered(1))]
+    shapes = [shape(g, hidden, bf16), shape(own - rows, d, bf16), shape(rows, d, bf16), shape(rows, d, f32)]
+    shapes += [half[1], half[1], jax.ShapeDtypeStruct(parts, f32)]
+    rows_buffer = pltpu.VMEM((count - 1, rows, d), bf16)
+    scratch = [acc, rows_buffer, rows_buffer] + sem_pair(count - 1) + Reduce.scratch(d, 4 * width)
     return call(kernel, (n,), ins, outs, shapes, scratch, flops, 0, collective=0)(*args, *more)
 
 
@@ -831,15 +850,15 @@
 
 
 def feed_back_last_kernel(
-    n2_ref, go_ref, gt_ref, gp_ref, s1_ref, x_ref, y_ref, st_ref, gain_ref, we_ref, ws_ref, d_send, d_keep, cols_ref, bias_ref,
-    grad_ref, dws_ref, dwe_ref, sum_ref,
-    acc, to_owner, from_other, own_s, e_send, parts, parts_got, *scratch, count,
+    n2_ref, go_ref, gt_ref, gp_ref, s1_ref, x_ref, y_ref, st_ref, gain_ref, we_ref, ws_ref, d_send, d_keep, cols_ref, bias_ref, late_hbm, late_own_ref,
+    grad_ref, dws_ref, dwe_ref, sum_ref, out_ref,
+    late_got, acc, to_owner, from_other, own_s, e_send, parts, parts_got, *scratch, count,
 ):
     n = 2 * count
     d = acc.shape[0]
     step = pl.program_id(0)
     to = neighbours()
-    row_sems, sum_sems, scratch = scratch[0:2], scratch[2:4], scratch[4:]
+    row_sems, sum_sems, late_sems, scratch = scratch[0:2], scratch[2:4], scratch[4:6], scratch[6:]
     size = len(scratch) // 2
     shrink = Reduce(d_send, kept(d_keep, d), dws_ref, scratch[:size], to)
 
@@ -850,6 +869,7 @@
     expand = Reduce(e_send, lambda p, j: from_acc(p, 8 + j), dwe_ref, scratch[size:], to)
     small = SumAll(parts, parts_got, sum_sems, to)
     row_copy = lambda b: remote(to_owner.at[b], from_other.at[b], row_sems, b, to["y"])
+    late_copy = remote(late_hbm, late_got, late_sems, 0, to["y"])
     normal = (jnp.where(step < count, y_ref[...], x_ref[...]).astype(f32) - st_ref[:, 0:1]) * st_ref[:, 1:2]
 
     @at_step(0)
@@ -862,6 +882,7 @@
             at = r * wide % d
             parts[0, 5 + r * wide // d : 6 + r * wide // d, at : at + wide] = bias_ref[r : r + 1, :]
         greet(to)
+        late_copy.start()
         for p in range(PIECES):
             shrink.across_core(p)
 
@@ -940,13 +961,18 @@
             centred = s - jnp.mean(s, axis=1, keepdims=True) - normal * jnp.mean(s * normal, axis=1, keepdims=True)
             grad_ref[...] = go_ref[...].astype(f32) + st_ref[:, 1:2] * centred
 
+    @at_step(n)
+    def _():
+        late_copy.wait()
+        out_ref[...] = (late_own_ref[...] + late_got[...].astype(f32)).astype(bf16)
+
     @at_step(n + TAIL - 1)
     def _():
         for p in range(LAST_PIECES):
             expand.end(p)
 
 
-def feed_back_last_call(n2, grads, gp, s1, x, st, vec, w2, dws, cols, bias, rows=256):
+def feed_back_last_call(n2, grads, gp, s1, x, st, vec, w2, dws, cols, bias, late, rows=256):
     g, d = n2.shape
     hidden = gp.shape[1]
     own = x[0].shape[0]
@@ -958,16 +984,17 @@
     turned_once = lambda c: pl.BlockSpec((rows, c), lambda i: (lax.rem(jnp.minimum(i, n - 1) + count, n), 0))
     ins = [turned_once(d), second(d), first(d), turned_once(hidden), turned_once(d), second(d), first(d), turned(2), held(1, d)]
     ins += [weight_of(w2, 0), weight_of(w2, 1), pl.BlockSpec(memory_space=pl.ANY), pieces(d, hidden)[0], held(2, d), held(*bias.shape)]
+    ins += [pl.BlockSpec(memory_space=pl.ANY), held(rows, d)]
     small = jax.ShapeDtypeStruct((16, d), f32)
-    outs = [pl.BlockSpec((rows, d), lambda i: (jnp.clip(i - n, 0, count - 1), 0)), held(part, hidden), held(part, hidden), held(*small.shape)]
-    shapes = [shape(own, d, f32), shape(part, hidden, f32), shape(part, hidden, f32), shape(*small.shape, f32)]
+    outs = [pl.BlockSpec((rows, d), lambda i: (jnp.clip(i - n, 0, count - 1), 0)), held(part, hidden), held(part, hidden), held(*small.shape), held(rows, d)]
+    shapes = [shape(own, d, f32), shape(part, hidden, f32), shape(part, hidden, f32), shape(*small.shape, f32), shape(rows, d, bf16)]
     rows_buffer = lambda dtype: pltpu.VMEM((count, rows, d), dtype)
     sums = pltpu.VMEM((5, *small.shape), f32)
-    scratch = [pltpu.VMEM((d, hidden), f32), rows_buffer(bf16), rows_buffer(bf16), rows_buffer(f32)]
+    scratch = [pltpu.VMEM((rows, d), bf16), pltpu.VMEM((d, hidden), f32), rows_buffer(bf16), rows_buffer(bf16), rows_buffer(f32)]
     scratch += [pltpu.VMEM((LAST_PIECES, d // 2, hidden // LAST_PIECES), bf16), sums, sums]
-    scratch += sem_pair(count) + sem_pair(5) + Reduce.scratch(d, hidden) + Reduce.scratch(d, hidden, LAST_PIECES)
+    scratch += sem_pair(count) + sem_pair(5) + sem_pair(1) + Reduce.scratch(d, hidden) + Reduce.scratch(d, hidden, LAST_PIECES)
     return call(functools.partial(feed_back_last_kernel, count=count), (n + TAIL,), ins, outs, shapes, scratch, 6 * g * d * hidden, 0, collective=1)(
-        n2, *grads, gp, s1, *x, st, vec[2], w2, w2, *dws, cols, bias
+        n2, *grads, gp, s1, *x, st, vec[2], w2, w2, *dws, cols, bias, *late
     )
 
 
@@ -1020,12 +1047,13 @@
         s, *dw1, cols1, bias1 = project_back_call(shift, fsdp, dq, dk, dv, ctx, n1, x, st, grads, vec, w1)
         out_bias = dense_bias + shrink_bias
         if fast:
-            gp, output, *dws, dw1 = feed_forward_call(fsdp, n2, grads, ctx, w2, w1, expand_bias[None], (inputs, out_bias[None], *dw1))
+            gp, output, *late, send, keep, dw1 = feed_forward_call(fsdp, n2, grads, ctx, w2, w1, expand_bias[None], (inputs, out_bias[None], *dw1))
         else:
             gp, *branch = feed_forward_call(fsdp, n2, grads, ctx, w2, w1, expand_bias[None])
             branch, dws = branch[:2], branch[2:]
         if fast:
-            input_grad, dws, dwe, small = feed_back_last_call(n2, grads, gp, s, x, st, vec, w2, dws, cols1, bias1)
+            input_grad, dws, dwe, small, rest = feed_back_last_call(n2, grads, gp, s, x, st, vec, w2, (send, keep), cols1, bias1, late)
+            output = jnp.concatenate([output, rest])
             cols, local = small[:5], jnp.concatenate([small[5:7].reshape(-1)[: 3 * width], small[7:9].reshape(-1)])
         else:
             s, *dwe, cols2, bias2 = feed_back_call(fsdp, n2, grads, gp, s, x, st, vec, w2, 0, False)

time: 362 us -> 341 us (0.942)
  Pallas kernels: 347 us -> 326 us
    pallas_call x4, Pallas kernels: 347 us -> 326 us  [call(): pl.pallas_call(kernel, grid_spec=pltpu.PrefetchScalarGridSpec(num_scalar_...]
    unnamed x19 -> x18, local copies, waits for them, and re-layouts: 8.6 us -> 7.69 us
where the time goes in v4:
time: 341 us
  Pallas kernels  326 us (96%)
  local copies, waits for them, and re-layouts  10.4 us (3%)
  other arithmetic  3.89 us (1%)
    pallas_call x4, Pallas kernels, call(): pl.pallas_call(kernel, grid_spec=pltpu.PrefetchScalarGridSpec(num_scalar_...  326 us
    unnamed x18, local copies, waits for them, and re-layouts  7.69 us

profile of v4, /device:TPU:0, one launch (start us, length us, event | category | flops | bytes accessed | tf_op | source)
XLA Modules:
  0.0 340.8 jit_solution(12511140447131651459)
XLA Ops:
  0.6 1.3 add.3
  1.9 154.6 %shard_map.245 = (bf16[2048,1024]{1,0:T(8,128)(2,1)}, bf16[2048,1024]{1,0:T(8,128)(2,1)}, f32[2048,2]{1,0:T(8,128)}, bf16[2048,512]{1,0:T(8,128)(2,1)}, bf16[204...) custom-call(bf16[1024,1024]{1,0:T(8,128)(2,1)} %x_ref.5, ...), custom_call_target="tpu_custom_call" | custom-call | flops 57982058496 | bytes 42768384 | tf_op jit(solution)/shard_map/pallas_call | solution.py:48
  156.5 25.2 %shard_map.246 = (f32[2048,1024]{1,0:T(8,128)}, bf16[2,512,1024]{2,1,0:T(8,128)(2,1)}, bf16[2,512,1024]{2,1,0:T(8,128)(2,1)}, f32[2,1024]{1,0:T(2,128)}, f32[3,512]{1,0:T(4,128)}) custom-call(s32[1]{0:T(128)} %bitcast.10.shift, bf16[2048,512]{1,0:T(8,128)(2,1)} %get-tuple-element.47.dq_ref, bf16[2048,512]{1,0:T(8,128)(2,1)} %get-tuple-element.48.dk_ref, ...), custom_call_target="tpu_custom_call" | custom-call | flops 15032385536 | bytes 37783556 | tf_op jit(solution)/shard_map/pallas_call | solution.py:48
  181.7 62.6 %shard_map.247 = (bf16[2048,2048]{1,0:T(8,128)(2,1)}, bf16[768,1024]{1,0:T(8,128)(2,1)}, bf16[256,1024]{1,0:T(8,128)(2,1)}, f32[256,1024]{1,0:T(8,128)}, bf16[2,...) custom-call(bf16[2048,1024]{1,0:T(8,128)(2,1)} %get-tuple-element.42.n2_ref, ...), custom_call_target="tpu_custom_call" | custom-call | flops 27917287424 | bytes 54013952 | tf_op jit(solution)/shard_map/pallas_call | solution.py:48
  244.4 0.0 copy-start
  244.4 83.2 %shard_map.248 = (f32[1024,1024]{1,0:T(8,128)}, f32[64,2048]{1,0:T(8,128)}, f32[64,2048]{1,0:T(8,128)}, f32[16,1024]{1,0:T(8,128)}, bf16[256,1024]{1,0:T(8,128)(2,1)}) custom-call(bf16[2048,1024]{1,0:T(8,128)(2,1)} %get-tuple-element.42.n2_ref, bf16[1024,1024]{1,0:T(8,128)(2,1)} %go_ref.5, bf16[1024,1024]{1,0:T(8,128)(2,1)} %get-tuple-element.43.gt_ref, ...), custom_call_target="tpu_custom_call" | custom-call | flops 25769803776 | bytes 57772032 | tf_op jit(solution)/shard_map/pallas_call | solution.py:48
  327.6 0.0 copy-done
  327.6 0.0 copy-start.4
  327.6 0.0 copy-start.1
  327.6 2.6 pad_maximum_fusion
  330.2 0.0 copy-done.4
  330.2 0.6 fusion
  330.8 0.0 copy-start.5
  330.8 0.6 copy.30
  331.4 0.6 slice.46
  332.0 0.0 copy-done.1
  332.0 0.7 slice_bitcast_fusion.1
  332.7 0.8 slice_bitcast_fusion
  333.5 0.6 copy.35
  334.1 0.0 copy-start.3
  334.1 0.0 copy-start.2
  334.1 4.9 %copy.36 = f32[1024,1024]{1,0:T(8,128)} copy(f32[1024,1024]{1,0:T(8,128)} %get-tuple-element.120) | data formatting | bytes 8388608
  338.9 0.0 copy-done.5
  338.9 0.0 copy-done.3
  338.9 0.8 copy.37
  339.7 0.0 copy-done.2
  339.7 0.8 copy.38
  (1 shorter events, 0.0 us)
Async XLA Ops:
  244.4 83.2 %copy-start = (bf16[768,1024]{1,0:T(8,128)(2,1)S(1)}, bf16[768,1024]{1,0:T(8,128)(2,1)}, u32[]{:S(2)}) copy-start(bf16[768,1024]{1,0:T(8,128)(2,1)} %get-tuple-element.55) | copy-start | bytes 4718596
  327.6 2.6 copy-start.4
  327.6 4.5 %copy-start.1 = (f32[4,64,512]{2,1,0:T(8,128)S(1)}, f32[4,64,512]{2,1,0:T(8,128)}, u32[]{:S(2)}) copy-start(f32[4,64,512]{2,1,0:T(8,128)} %get-tuple-element.67) | copy-start | bytes 1572868
  330.8 8.1 %copy-start.5 = (f32[1,1024]{1,0:T(1,128)}, f32[1,1024]{1,0:T(1,128)S(1)}, u32[]{:S(2)}) copy-start(f32[1,1024]{1,0:T(1,128)S(1)} %get-tuple-element.72) | copy-start | bytes 12292
  334.1 4.9 %copy-start.3 = (f32[64,2048]{1,0:T(8,128)S(1)}, f32[64,2048]{1,0:T(8,128)}, u32[]{:S(2)}) copy-start(f32[64,2048]{1,0:T(8,128)} %get-tuple-element.129) | copy-start | bytes 1572868
  334.1 5.7 %copy-start.2 = (f32[64,2048]{1,0:T(8,128)S(1)}, f32[64,2048]{1,0:T(8,128)}, u32[]{:S(2)}) copy-start(f32[64,2048]{1,0:T(8,128)} %get-tuple-element.69) | copy-start | bytes 1572868
